TPU v7x, 8 devices: a whole 2x2x1 slice. The times are simulated.
8 devices in a mesh: dp: 1 (over z), cy: 2 (over y), cx: 4 (over x, core).
Axes of the slice: x: 2, y: 2, z: 1, core: 2. Of those that a mesh axis runs over, the one named last changes fastest.
Arguments:
- query_rows: bfloat16 [8192, 28, 128], P(('dp', 'cy', 'cx'))
- key_rows: bfloat16 [8192, 4, 128], P(('dp', 'cy', 'cx'))
- value_rows: bfloat16 [8192, 4, 128], P(('dp', 'cy', 'cx'))
- out_rows: bfloat16 [8192, 28, 128], P(('dp', 'cy', 'cx'))
- grad_out: bfloat16 [8192, 28, 128], P(('dp', 'cy', 'cx'))
- log_sum_exp: float32 [8192, 28], P(('dp', 'cy', 'cx'))
Outputs:
- output 1: bfloat16 [8192, 28, 128], P(('dp', 'cy', 'cx'))
- output 2: bfloat16 [8192, 4, 128], P(('dp', 'cy', 'cx'))
- output 3: bfloat16 [8192, 4, 128], P(('dp', 'cy', 'cx'))
All inputs are finite; a program needn't handle non-finite values.
Results may differ from a plain program's by a relative error of at most 0.00401.
Values are sent between devices in bfloat16 or wider.
A program may use at most 1 GiB of HBM per device.

v0:
```python
import math
import jax
import jax.numpy as jnp
from jax import lax
from jax.sharding import PartitionSpec as P


def block_grads(q_blk, do_blk, lse_blk, delta_blk, k_blk, v_blk, keep_mask, scaling):
    score_f32 = jnp.einsum('qkgd,skd->kqgs', q_blk, k_blk, preferred_element_type=jnp.float32) * scaling
    prob_f32 = jnp.exp(score_f32 - lse_blk[..., None])
    if keep_mask is not None:
        prob_f32 = jnp.where(keep_mask[None, :, None, :], prob_f32, 0.0)
    dprob_f32 = jnp.einsum('qkgd,skd->kqgs', do_blk, v_blk, preferred_element_type=jnp.float32)
    dscore_b16 = (prob_f32 * (dprob_f32 - delta_blk[..., None])).astype(jnp.bfloat16)
    prob_b16 = prob_f32.astype(jnp.bfloat16)
    dq_part = jnp.einsum('kqgs,skd->kqgd', dscore_b16, k_blk, preferred_element_type=jnp.float32)
    dk_part = jnp.einsum('kqgs,qkgd->ksd', dscore_b16, q_blk, preferred_element_type=jnp.float32)
    dv_part = jnp.einsum('kqgs,qkgd->ksd', prob_b16, do_blk, preferred_element_type=jnp.float32)
    return dq_part, dk_part, dv_part


def solution(mesh):
    n_cx = mesh.shape['cx']
    n_ctx = mesh.shape['cy'] * n_cx
    ctx_axes = ('cy', 'cx')
    shift_perm = [(dev_idx, (dev_idx + 1) % n_ctx) for dev_idx in range(n_ctx)]
    row_spec = P(('dp', 'cy', 'cx'), None, None)
    stat_spec = P(('dp', 'cy', 'cx'), None)

    def local_grads(query_rows, key_rows, value_rows, out_rows, grad_out, log_sum_exp):
        tok_dev, n_heads, head_dim = query_rows.shape
        kv_heads = key_rows.shape[1]
        group_size = n_heads // kv_heads
        half_tok = tok_dev // 2
        scaling = 1.0 / math.sqrt(head_dim)
        ctx_rank = lax.axis_index('cy') * n_cx + lax.axis_index('cx')
        q_grp = query_rows.reshape(tok_dev, kv_heads, group_size, head_dim)
        do_grp = grad_out.reshape(tok_dev, kv_heads, group_size, head_dim)
        lse_grp = log_sum_exp.reshape(tok_dev, kv_heads, group_size).transpose(1, 0, 2)
        delta_grp = jnp.einsum('thd,thd->th', grad_out, out_rows, preferred_element_type=jnp.float32).reshape(tok_dev, kv_heads, group_size).transpose(1, 0, 2)
        local_idx = jnp.arange(tok_dev)
        piece_id = jnp.where(local_idx < half_tok, ctx_rank, 2 * n_ctx - 1 - ctx_rank)
        own_pos = piece_id * half_tok + local_idx % half_tok
        diag_mask = own_pos[:, None] >= own_pos[None, :]
        dq_own, dk_own, dv_own = block_grads(q_grp, do_grp, lse_grp, delta_grp, key_rows, value_rows, diag_mask, scaling)

        def src_before(k_blk, v_blk):
            dq_part, dk_part, dv_part = block_grads(q_grp, do_grp, lse_grp, delta_grp, k_blk[:half_tok], v_blk[:half_tok], None, scaling)
            zero_pad = jnp.zeros_like(dk_part)
            return dq_part, jnp.concatenate([dk_part, zero_pad], axis=1), jnp.concatenate([dv_part, zero_pad], axis=1)

        def src_after(k_blk, v_blk):
            dq_part, dk_part, dv_part = block_grads(q_grp[half_tok:], do_grp[half_tok:], lse_grp[:, half_tok:], delta_grp[:, half_tok:], k_blk, v_blk, None, scaling)
            zero_pad = jnp.zeros_like(dq_part)
            return jnp.concatenate([zero_pad, dq_part], axis=1), dk_part, dv_part

        def step_body(step_idx, state):
            k_cur, v_cur, dk_cur, dv_cur, dq_cur = state
            k_cur = lax.ppermute(k_cur, ctx_axes, shift_perm)
            v_cur = lax.ppermute(v_cur, ctx_axes, shift_perm)
            dk_cur = lax.ppermute(dk_cur, ctx_axes, shift_perm)
            dv_cur = lax.ppermute(dv_cur, ctx_axes, shift_perm)
            src_rank = (ctx_rank - step_idx) % n_ctx
            dq_part, dk_part, dv_part = lax.cond(src_rank < ctx_rank, src_before, src_after, k_cur, v_cur)
            return (k_cur, v_cur, dk_cur + dk_part, dv_cur + dv_part, dq_cur + dq_part)

        k_end, v_end, dk_end, dv_end, dq_end = lax.fori_loop(1, n_ctx, step_body, (key_rows, value_rows, dk_own, dv_own, dq_own))
        dk_home = lax.ppermute(dk_end, ctx_axes, shift_perm)
        dv_home = lax.ppermute(dv_end, ctx_axes, shift_perm)
        grad_query = (dq_end * scaling).astype(jnp.bfloat16).transpose(1, 0, 2, 3).reshape(tok_dev, n_heads, head_dim)
        grad_key = (dk_home * scaling).astype(jnp.bfloat16).transpose(1, 0, 2)
        grad_value = dv_home.astype(jnp.bfloat16).transpose(1, 0, 2)
        return grad_query, grad_key, grad_value

    return jax.shard_map(local_grads, mesh=mesh, in_specs=(row_spec, row_spec, row_spec, row_spec, row_spec, stat_spec), out_specs=(row_spec, row_spec, row_spec), check_vma=False)
```

profile of v0, /device:TPU:0, one launch (start us, length us, event | category | flops | bytes accessed | tf_op | source)
XLA Modules:
  0.0 1832.5 jit_solution(9495449616915574354)
XLA Ops:
  12.8 41.5 %fusion.49 = f32[4,1024,7,1024]{3,1,2,0:T(8,128)} fusion(bf16[1024,4,7,128]{3,0,2,1:T(8,128)(2,1)} %bitcast.79, bf16[1024,4,128,1]{2,1,0,3:T(4,128)(2,1)S(1)} %bitcast.90), kind=kOutput, calls=%fused_computation.49 | convolution fusion | flops 7516192768 | bytes 125829120 | tf_op jit(solution)/shard_map/qkgd,skd->kqgs/dot_general | solution.py:9
  54.4 45.1 %fusion.42 = f32[4,1024,128]{2,1,0:T(8,128)} fusion(bf16[1024,4,7,128]{3,0,2,1:T(8,128)(2,1)} %bitcast.82, f32[4,1024,7,1024]{3,1,2,0:T(8,128)} %fusion.49, f32[4,1024,7]{1,2,0:T(8,128)S(1)} %bitcast.85, pred[1024,1024]{1,0:T(8,128)(4,1)S(1)} %broadcast_compare_fusion), kind=kOutput, calls=%fused_computation.42 | convolution fusion | flops 7633633280 | bytes 128040960 | tf_op jit(solution)/shard_map/kqgs,qkgd->ksd/dot_general | solution.py:18
  99.4 62.6 %multiply_convert_fusion.2 = bf16[4,1024,7,1024]{3,1,2,0:T(8,128)(2,1)} fusion(f32[4,1024,7,1024]{3,1,2,0:T(8,128)} %fusion.49, f32[4,1024,7]{1,2,0:T(8,128)S(1)} %bitcast.88, f32[4,1024,7]{1,2,0:T(8,128)S(1)} %bitcast.86, pred[1024,1024]{1,0:T(8,128)(4,1)S(1)} %broadcast_compare_fusion, bf16[1024,4,7,128]{3,0,2,1:T(8,128)(2,1)} %bitcast.83, ...), kind=kOutput, calls=%fused_computation.32 | convolution fusion | flops 7692353536 | bytes 185827328 | tf_op jit(solution)/shard_map/qkgd,skd->kqgs/dot_general | solution.py:13
  162.1 28.9 %convolution_bitcast_fusion.1 = f32[4,1024,128]{2,1,0:T(8,128)} fusion(bf16[4,1024,7,1024]{3,1,2,0:T(8,128)(2,1)} %multiply_convert_fusion.2, bf16[1024,4,7,128]{3,0,2,1:T(8,128)(2,1)} %bitcast.80), kind=kOutput, calls=%fused_computation.43 | convolution fusion | flops 7516192768 | bytes 68157440 | tf_op jit(solution)/shard_map/kqgs,qkgd->ksd/dot_general | solution.py:17
  190.9 28.2 %fusion.47 = f32[4,1024,7,128]{3,1,2,0:T(8,128)} fusion(bf16[4,1024,7,1024]{3,1,2,0:T(8,128)(2,1)} %multiply_convert_fusion.2, bf16[1024,4,128,1]{2,1,0,3:T(4,128)(2,1)S(1)} %bitcast.91), kind=kOutput, calls=%fused_computation.47 | convolution fusion | flops 7516192768 | bytes 74448896 | tf_op jit(solution)/shard_map/kqgs,skd->kqgd/dot_general | solution.py:16
  219.1 1567.3 %while.23 = (s32[]{:T(128)}, bf16[1024,4,128]{2,0,1:T(8,128)(2,1)}, bf16[1024,4,128]{2,0,1:T(8,128)(2,1)}, f32[4,1024,128]{2,1,0:T(8,128)}, f32[4,1024,128]{2,1,...) while((s32[]{:T(128)}, bf16[1024,4,128]{2,0,1:T(8,128)(2,1)}, ...), condition=%wide.region_3.4_spmd, body=%wide.region_0.3_spmd.sunk | while | flops 18912641024 | bytes 417153632 | solution.py:67
  247.2 56.1 %collective-permute-done.1 = bf16[1024,4,128]{2,0,1:T(8,128)(2,1)} collective-permute-done((bf16[1024,4,128]{2,0,1:T(8,128)(2,1)}, bf16[1024,4,128]{2,0,1:T(8,128)(2,1)}, u32[]{:S(2)}, u32[]{:S(2)}) %collective-permute-start.1) | collective-permute-done | bytes 1048608 | tf_op jit(solution)/shard_map/while/body/eval_jaxpr/ppermute | solution.py:60
  314.6 122.9 %conditional.2 = (f32[4,1024,7,128]{3,1,2,0:T(8,128)}, f32[4,1024,128]{2,1,0:T(8,128)}, f32[4,1024,128]{2,1,0:T(8,128)S(1)}) conditional(s32[]{:T(128)} %convert_element_type.65, (bf16[1024,4,7,128]{3,0,2,1:T(8,128)(2,1)}, bf16[1024,4,128]{2,0,1:T(8,128)(2,1)S(1)}, f32[4,1024,7]{1,2,0:T(8,128)S(1)}, bf16[1024,4,7,128]{3,0,2,1:T(8,128)(2,1)}, ...), branch_computations={%region_1.1_spmd, %region_2.2_spmd} | conditional | flops 18907922432 | bytes 322781248 | solution.py:64
  314.6 22.5 %fusion.7 = f32[4,512,7,1024]{3,1,2,0:T(8,128)} fusion(bf16[1024,4,7,128]{3,0,2,1:T(8,128)(2,1)} %get-tuple-element.276, bf16[1024,4,128]{2,0,1:T(8,128)(2,1)S(1)} %get-tuple-element.277), kind=kOutput, calls=%fused_computation.8 | convolution fusion | flops 3758096384 | bytes 63438848 | tf_op jit(solution)/shard_map/while/body/eval_jaxpr/cond/branch_0_fun/qkgd,skd->kqgs/dot_general | solution.py:9
  337.1 23.1 %fusion.12 = f32[4,1024,128]{2,1,0:T(8,128)S(1)} fusion(bf16[1024,4,7,128]{3,0,2,1:T(8,128)(2,1)} %get-tuple-element.279, f32[4,512,7,1024]{3,1,2,0:T(8,128)} %fusion.7, f32[4,512,7]{1,2,0:T(8,128)S(1)} %slice.13), kind=kOutput, calls=%fused_computation.11 | convolution fusion | flops 3802136576 | bytes 64544768 | tf_op jit(solution)/shard_map/while/body/eval_jaxpr/cond/branch_0_fun/kqgs,qkgd->ksd/dot_general | solution.py:18
  360.2 34.4 %multiply_convert_fusion = bf16[4,512,7,1024]{3,1,2,0:T(8,128)(2,1)} fusion(f32[4,512,7,1024]{3,1,2,0:T(8,128)} %fusion.7, f32[4,512,7]{1,2,0:T(8,128)S(1)} %slice.15, f32[4,512,7]{1,2,0:T(8,128)S(1)} %slice.13, bf16[1024,4,7,128]{3,0,2,1:T(8,128)(2,1)} %get-tuple-element.279, bf16[1024,4,128]{2,0,1:T(8,128)(2,1)} %get-tuple-element.280), kind=kOutput, calls=%fused_computation | convolution fusion | flops 3831496704 | bytes 92913664 | tf_op jit(solution)/shard_map/while/body/eval_jaxpr/cond/branch_0_fun/qkgd,skd->kqgs/dot_general | solution.py:13
  394.5 16.6 fusion.9
  411.2 16.4 fusion.18
  437.5 15.9 add.112
  463.5 59.7 %collective-permute-done.1 = bf16[1024,4,128]{2,0,1:T(8,128)(2,1)} collective-permute-done((bf16[1024,4,128]{2,0,1:T(8,128)(2,1)}, bf16[1024,4,128]{2,0,1:T(8,128)(2,1)}, u32[]{:S(2)}, u32[]{:S(2)}) %collective-permute-start.1) | collective-permute-done | bytes 1048608 | tf_op jit(solution)/shard_map/while/body/eval_jaxpr/ppermute | solution.py:60
  534.4 122.9 %conditional.2 = (f32[4,1024,7,128]{3,1,2,0:T(8,128)}, f32[4,1024,128]{2,1,0:T(8,128)}, f32[4,1024,128]{2,1,0:T(8,128)S(1)}) conditional(s32[]{:T(128)} %convert_element_type.65, (bf16[1024,4,7,128]{3,0,2,1:T(8,128)(2,1)}, bf16[1024,4,128]{2,0,1:T(8,128)(2,1)S(1)}, f32[4,1024,7]{1,2,0:T(8,128)S(1)}, bf16[1024,4,7,128]{3,0,2,1:T(8,128)(2,1)}, ...), branch_computations={%region_1.1_spmd, %region_2.2_spmd} | conditional | flops 18907922432 | bytes 322781248 | solution.py:64
  534.4 22.5 %fusion.7 = f32[4,512,7,1024]{3,1,2,0:T(8,128)} fusion(bf16[1024,4,7,128]{3,0,2,1:T(8,128)(2,1)} %get-tuple-element.276, bf16[1024,4,128]{2,0,1:T(8,128)(2,1)S(1)} %get-tuple-element.277), kind=kOutput, calls=%fused_computation.8 | convolution fusion | flops 3758096384 | bytes 63438848 | tf_op jit(solution)/shard_map/while/body/eval_jaxpr/cond/branch_0_fun/qkgd,skd->kqgs/dot_general | solution.py:9
  556.9 23.1 %fusion.12 = f32[4,1024,128]{2,1,0:T(8,128)S(1)} fusion(bf16[1024,4,7,128]{3,0,2,1:T(8,128)(2,1)} %get-tuple-element.279, f32[4,512,7,1024]{3,1,2,0:T(8,128)} %fusion.7, f32[4,512,7]{1,2,0:T(8,128)S(1)} %slice.13), kind=kOutput, calls=%fused_computation.11 | convolution fusion | flops 3802136576 | bytes 64544768 | tf_op jit(solution)/shard_map/while/body/eval_jaxpr/cond/branch_0_fun/kqgs,qkgd->ksd/dot_general | solution.py:18
  580.0 34.4 %multiply_convert_fusion = bf16[4,512,7,1024]{3,1,2,0:T(8,128)(2,1)} fusion(f32[4,512,7,1024]{3,1,2,0:T(8,128)} %fusion.7, f32[4,512,7]{1,2,0:T(8,128)S(1)} %slice.15, f32[4,512,7]{1,2,0:T(8,128)S(1)} %slice.13, bf16[1024,4,7,128]{3,0,2,1:T(8,128)(2,1)} %get-tuple-element.279, bf16[1024,4,128]{2,0,1:T(8,128)(2,1)} %get-tuple-element.280), kind=kOutput, calls=%fused_computation | convolution fusion | flops 3831496704 | bytes 92913664 | tf_op jit(solution)/shard_map/while/body/eval_jaxpr/cond/branch_0_fun/qkgd,skd->kqgs/dot_general | solution.py:13
  614.4 16.6 fusion.9
  631.0 16.4 fusion.18
  657.4 15.9 add.112
  683.0 60.0 %collective-permute-done.1 = bf16[1024,4,128]{2,0,1:T(8,128)(2,1)} collective-permute-done((bf16[1024,4,128]{2,0,1:T(8,128)(2,1)}, bf16[1024,4,128]{2,0,1:T(8,128)(2,1)}, u32[]{:S(2)}, u32[]{:S(2)}) %collective-permute-start.1) | collective-permute-done | bytes 1048608 | tf_op jit(solution)/shard_map/while/body/eval_jaxpr/ppermute | solution.py:60
  754.2 122.9 %conditional.2 = (f32[4,1024,7,128]{3,1,2,0:T(8,128)}, f32[4,1024,128]{2,1,0:T(8,128)}, f32[4,1024,128]{2,1,0:T(8,128)S(1)}) conditional(s32[]{:T(128)} %convert_element_type.65, (bf16[1024,4,7,128]{3,0,2,1:T(8,128)(2,1)}, bf16[1024,4,128]{2,0,1:T(8,128)(2,1)S(1)}, f32[4,1024,7]{1,2,0:T(8,128)S(1)}, bf16[1024,4,7,128]{3,0,2,1:T(8,128)(2,1)}, ...), branch_computations={%region_1.1_spmd, %region_2.2_spmd} | conditional | flops 18907922432 | bytes 322781248 | solution.py:64
  754.2 22.5 %fusion.7 = f32[4,512,7,1024]{3,1,2,0:T(8,128)} fusion(bf16[1024,4,7,128]{3,0,2,1:T(8,128)(2,1)} %get-tuple-element.276, bf16[1024,4,128]{2,0,1:T(8,128)(2,1)S(1)} %get-tuple-element.277), kind=kOutput, calls=%fused_computation.8 | convolution fusion | flops 3758096384 | bytes 63438848 | tf_op jit(solution)/shard_map/while/body/eval_jaxpr/cond/branch_0_fun/qkgd,skd->kqgs/dot_general | solution.py:9
  776.7 23.1 %fusion.12 = f32[4,1024,128]{2,1,0:T(8,128)S(1)} fusion(bf16[1024,4,7,128]{3,0,2,1:T(8,128)(2,1)} %get-tuple-element.279, f32[4,512,7,1024]{3,1,2,0:T(8,128)} %fusion.7, f32[4,512,7]{1,2,0:T(8,128)S(1)} %slice.13), kind=kOutput, calls=%fused_computation.11 | convolution fusion | flops 3802136576 | bytes 64544768 | tf_op jit(solution)/shard_map/while/body/eval_jaxpr/cond/branch_0_fun/kqgs,qkgd->ksd/dot_general | solution.py:18
  799.8 34.4 %multiply_convert_fusion = bf16[4,512,7,1024]{3,1,2,0:T(8,128)(2,1)} fusion(f32[4,512,7,1024]{3,1,2,0:T(8,128)} %fusion.7, f32[4,512,7]{1,2,0:T(8,128)S(1)} %slice.15, f32[4,512,7]{1,2,0:T(8,128)S(1)} %slice.13, bf16[1024,4,7,128]{3,0,2,1:T(8,128)(2,1)} %get-tuple-element.279, bf16[1024,4,128]{2,0,1:T(8,128)(2,1)} %get-tuple-element.280), kind=kOutput, calls=%fused_computation | convolution fusion | flops 3831496704 | bytes 92913664 | tf_op jit(solution)/shard_map/while/body/eval_jaxpr/cond/branch_0_fun/qkgd,skd->kqgs/dot_general | solution.py:13
  834.2 16.6 fusion.9
  850.8 16.4 fusion.18
  877.2 15.9 add.112
  902.8 60.0 %collective-permute-done.1 = bf16[1024,4,128]{2,0,1:T(8,128)(2,1)} collective-permute-done((bf16[1024,4,128]{2,0,1:T(8,128)(2,1)}, bf16[1024,4,128]{2,0,1:T(8,128)(2,1)}, u32[]{:S(2)}, u32[]{:S(2)}) %collective-permute-start.1) | collective-permute-done | bytes 1048608 | tf_op jit(solution)/shard_map/while/body/eval_jaxpr/ppermute | solution.py:60
  974.0 122.9 %conditional.2 = (f32[4,1024,7,128]{3,1,2,0:T(8,128)}, f32[4,1024,128]{2,1,0:T(8,128)}, f32[4,1024,128]{2,1,0:T(8,128)S(1)}) conditional(s32[]{:T(128)} %convert_element_type.65, (bf16[1024,4,7,128]{3,0,2,1:T(8,128)(2,1)}, bf16[1024,4,128]{2,0,1:T(8,128)(2,1)S(1)}, f32[4,1024,7]{1,2,0:T(8,128)S(1)}, bf16[1024,4,7,128]{3,0,2,1:T(8,128)(2,1)}, ...), branch_computations={%region_1.1_spmd, %region_2.2_spmd} | conditional | flops 18907922432 | bytes 322781248 | solution.py:64
  974.0 22.5 %fusion.7 = f32[4,512,7,1024]{3,1,2,0:T(8,128)} fusion(bf16[1024,4,7,128]{3,0,2,1:T(8,128)(2,1)} %get-tuple-element.276, bf16[1024,4,128]{2,0,1:T(8,128)(2,1)S(1)} %get-tuple-element.277), kind=kOutput, calls=%fused_computation.8 | convolution fusion | flops 3758096384 | bytes 63438848 | tf_op jit(solution)/shard_map/while/body/eval_jaxpr/cond/branch_0_fun/qkgd,skd->kqgs/dot_general | solution.py:9
  996.5 23.1 %fusion.12 = f32[4,1024,128]{2,1,0:T(8,128)S(1)} fusion(bf16[1024,4,7,128]{3,0,2,1:T(8,128)(2,1)} %get-tuple-element.279, f32[4,512,7,1024]{3,1,2,0:T(8,128)} %fusion.7, f32[4,512,7]{1,2,0:T(8,128)S(1)} %slice.13), kind=kOutput, calls=%fused_computation.11 | convolution fusion | flops 3802136576 | bytes 64544768 | tf_op jit(solution)/shard_map/while/body/eval_jaxpr/cond/branch_0_fun/kqgs,qkgd->ksd/dot_general | solution.py:18
  1019.6 34.4 %multiply_convert_fusion = bf16[4,512,7,1024]{3,1,2,0:T(8,128)(2,1)} fusion(f32[4,512,7,1024]{3,1,2,0:T(8,128)} %fusion.7, f32[4,512,7]{1,2,0:T(8,128)S(1)} %slice.15, f32[4,512,7]{1,2,0:T(8,128)S(1)} %slice.13, bf16[1024,4,7,128]{3,0,2,1:T(8,128)(2,1)} %get-tuple-element.279, bf16[1024,4,128]{2,0,1:T(8,128)(2,1)} %get-tuple-element.280), kind=kOutput, calls=%fused_computation | convolution fusion | flops 3831496704 | bytes 92913664 | tf_op jit(solution)/shard_map/while/body/eval_jaxpr/cond/branch_0_fun/qkgd,skd->kqgs/dot_general | solution.py:13
  1054.0 16.6 fusion.9
  1070.6 16.4 fusion.18
  1097.0 15.9 add.112
  1122.6 60.0 %collective-permute-done.1 = bf16[1024,4,128]{2,0,1:T(8,128)(2,1)} collective-permute-done((bf16[1024,4,128]{2,0,1:T(8,128)(2,1)}, bf16[1024,4,128]{2,0,1:T(8,128)(2,1)}, u32[]{:S(2)}, u32[]{:S(2)}) %collective-permute-start.1) | collective-permute-done | bytes 1048608 | tf_op jit(solution)/shard_map/while/body/eval_jaxpr/ppermute | solution.py:60
  1193.8 122.9 %conditional.2 = (f32[4,1024,7,128]{3,1,2,0:T(8,128)}, f32[4,1024,128]{2,1,0:T(8,128)}, f32[4,1024,128]{2,1,0:T(8,128)S(1)}) conditional(s32[]{:T(128)} %convert_element_type.65, (bf16[1024,4,7,128]{3,0,2,1:T(8,128)(2,1)}, bf16[1024,4,128]{2,0,1:T(8,128)(2,1)S(1)}, f32[4,1024,7]{1,2,0:T(8,128)S(1)}, bf16[1024,4,7,128]{3,0,2,1:T(8,128)(2,1)}, ...), branch_computations={%region_1.1_spmd, %region_2.2_spmd} | conditional | flops 18907922432 | bytes 322781248 | solution.py:64
  1193.9 22.5 %fusion.7 = f32[4,512,7,1024]{3,1,2,0:T(8,128)} fusion(bf16[1024,4,7,128]{3,0,2,1:T(8,128)(2,1)} %get-tuple-element.276, bf16[1024,4,128]{2,0,1:T(8,128)(2,1)S(1)} %get-tuple-element.277), kind=kOutput, calls=%fused_computation.8 | convolution fusion | flops 3758096384 | bytes 63438848 | tf_op jit(solution)/shard_map/while/body/eval_jaxpr/cond/branch_0_fun/qkgd,skd->kqgs/dot_general | solution.py:9
  1216.3 23.1 %fusion.12 = f32[4,1024,128]{2,1,0:T(8,128)S(1)} fusion(bf16[1024,4,7,128]{3,0,2,1:T(8,128)(2,1)} %get-tuple-element.279, f32[4,512,7,1024]{3,1,2,0:T(8,128)} %fusion.7, f32[4,512,7]{1,2,0:T(8,128)S(1)} %slice.13), kind=kOutput, calls=%fused_computation.11 | convolution fusion | flops 3802136576 | bytes 64544768 | tf_op jit(solution)/shard_map/while/body/eval_jaxpr/cond/branch_0_fun/kqgs,qkgd->ksd/dot_general | solution.py:18
  1239.4 34.4 %multiply_convert_fusion = bf16[4,512,7,1024]{3,1,2,0:T(8,128)(2,1)} fusion(f32[4,512,7,1024]{3,1,2,0:T(8,128)} %fusion.7, f32[4,512,7]{1,2,0:T(8,128)S(1)} %slice.15, f32[4,512,7]{1,2,0:T(8,128)S(1)} %slice.13, bf16[1024,4,7,128]{3,0,2,1:T(8,128)(2,1)} %get-tuple-element.279, bf16[1024,4,128]{2,0,1:T(8,128)(2,1)} %get-tuple-element.280), kind=kOutput, calls=%fused_computation | convolution fusion | flops 3831496704 | bytes 92913664 | tf_op jit(solution)/shard_map/while/body/eval_jaxpr/cond/branch_0_fun/qkgd,skd->kqgs/dot_general | solution.py:13
  1273.8 16.6 fusion.9
  1290.5 16.4 fusion.18
  1316.8 15.9 add.112
  1342.4 60.0 %collective-permute-done.1 = bf16[1024,4,128]{2,0,1:T(8,128)(2,1)} collective-permute-done((bf16[1024,4,128]{2,0,1:T(8,128)(2,1)}, bf16[1024,4,128]{2,0,1:T(8,128)(2,1)}, u32[]{:S(2)}, u32[]{:S(2)}) %collective-permute-start.1) | collective-permute-done | bytes 1048608 | tf_op jit(solution)/shard_map/while/body/eval_jaxpr/ppermute | solution.py:60
  1413.7 122.9 %conditional.2 = (f32[4,1024,7,128]{3,1,2,0:T(8,128)}, f32[4,1024,128]{2,1,0:T(8,128)}, f32[4,1024,128]{2,1,0:T(8,128)S(1)}) conditional(s32[]{:T(128)} %convert_element_type.65, (bf16[1024,4,7,128]{3,0,2,1:T(8,128)(2,1)}, bf16[1024,4,128]{2,0,1:T(8,128)(2,1)S(1)}, f32[4,1024,7]{1,2,0:T(8,128)S(1)}, bf16[1024,4,7,128]{3,0,2,1:T(8,128)(2,1)}, ...), branch_computations={%region_1.1_spmd, %region_2.2_spmd} | conditional | flops 18907922432 | bytes 322781248 | solution.py:64
  1413.7 22.5 %fusion.7 = f32[4,512,7,1024]{3,1,2,0:T(8,128)} fusion(bf16[1024,4,7,128]{3,0,2,1:T(8,128)(2,1)} %get-tuple-element.276, bf16[1024,4,128]{2,0,1:T(8,128)(2,1)S(1)} %get-tuple-element.277), kind=kOutput, calls=%fused_computation.8 | convolution fusion | flops 3758096384 | bytes 63438848 | tf_op jit(solution)/shard_map/while/body/eval_jaxpr/cond/branch_0_fun/qkgd,skd->kqgs/dot_general | solution.py:9
  1436.2 23.1 %fusion.12 = f32[4,1024,128]{2,1,0:T(8,128)S(1)} fusion(bf16[1024,4,7,128]{3,0,2,1:T(8,128)(2,1)} %get-tuple-element.279, f32[4,512,7,1024]{3,1,2,0:T(8,128)} %fusion.7, f32[4,512,7]{1,2,0:T(8,128)S(1)} %slice.13), kind=kOutput, calls=%fused_computation.11 | convolution fusion | flops 3802136576 | bytes 64544768 | tf_op jit(solution)/shard_map/while/body/eval_jaxpr/cond/branch_0_fun/kqgs,qkgd->ksd/dot_general | solution.py:18
  1459.2 34.4 %multiply_convert_fusion = bf16[4,512,7,1024]{3,1,2,0:T(8,128)(2,1)} fusion(f32[4,512,7,1024]{3,1,2,0:T(8,128)} %fusion.7, f32[4,512,7]{1,2,0:T(8,128)S(1)} %slice.15, f32[4,512,7]{1,2,0:T(8,128)S(1)} %slice.13, bf16[1024,4,7,128]{3,0,2,1:T(8,128)(2,1)} %get-tuple-element.279, bf16[1024,4,128]{2,0,1:T(8,128)(2,1)} %get-tuple-element.280), kind=kOutput, calls=%fused_computation | convolution fusion | flops 3831496704 | bytes 92913664 | tf_op jit(solution)/shard_map/while/body/eval_jaxpr/cond/branch_0_fun/qkgd,skd->kqgs/dot_general | solution.py:13
  1493.6 16.6 fusion.9
  1510.3 16.4 fusion.18
  1536.6 15.9 add.112
  1562.3 60.0 %collective-permute-done.1 = bf16[1024,4,128]{2,0,1:T(8,128)(2,1)} collective-permute-done((bf16[1024,4,128]{2,0,1:T(8,128)(2,1)}, bf16[1024,4,128]{2,0,1:T(8,128)(2,1)}, u32[]{:S(2)}, u32[]{:S(2)}) %collective-permute-start.1) | collective-permute-done | bytes 1048608 | tf_op jit(solution)/shard_map/while/body/eval_jaxpr/ppermute | solution.py:60
  1622.2 11.2 collective-permute-done
  1633.5 122.9 %conditional.2 = (f32[4,1024,7,128]{3,1,2,0:T(8,128)}, f32[4,1024,128]{2,1,0:T(8,128)}, f32[4,1024,128]{2,1,0:T(8,128)S(1)}) conditional(s32[]{:T(128)} %convert_element_type.65, (bf16[1024,4,7,128]{3,0,2,1:T(8,128)(2,1)}, bf16[1024,4,128]{2,0,1:T(8,128)(2,1)S(1)}, f32[4,1024,7]{1,2,0:T(8,128)S(1)}, bf16[1024,4,7,128]{3,0,2,1:T(8,128)(2,1)}, ...), branch_computations={%region_1.1_spmd, %region_2.2_spmd} | conditional | flops 18907922432 | bytes 322781248 | solution.py:64
  1633.5 22.5 %fusion.7 = f32[4,512,7,1024]{3,1,2,0:T(8,128)} fusion(bf16[1024,4,7,128]{3,0,2,1:T(8,128)(2,1)} %get-tuple-element.276, bf16[1024,4,128]{2,0,1:T(8,128)(2,1)S(1)} %get-tuple-element.277), kind=kOutput, calls=%fused_computation.8 | convolution fusion | flops 3758096384 | bytes 63438848 | tf_op jit(solution)/shard_map/while/body/eval_jaxpr/cond/branch_0_fun/qkgd,skd->kqgs/dot_general | solution.py:9
  1656.0 23.1 %fusion.12 = f32[4,1024,128]{2,1,0:T(8,128)S(1)} fusion(bf16[1024,4,7,128]{3,0,2,1:T(8,128)(2,1)} %get-tuple-element.279, f32[4,512,7,1024]{3,1,2,0:T(8,128)} %fusion.7, f32[4,512,7]{1,2,0:T(8,128)S(1)} %slice.13), kind=kOutput, calls=%fused_computation.11 | convolution fusion | flops 3802136576 | bytes 64544768 | tf_op jit(solution)/shard_map/while/body/eval_jaxpr/cond/branch_0_fun/kqgs,qkgd->ksd/dot_general | solution.py:18
  1679.1 34.4 %multiply_convert_fusion = bf16[4,512,7,1024]{3,1,2,0:T(8,128)(2,1)} fusion(f32[4,512,7,1024]{3,1,2,0:T(8,128)} %fusion.7, f32[4,512,7]{1,2,0:T(8,128)S(1)} %slice.15, f32[4,512,7]{1,2,0:T(8,128)S(1)} %slice.13, bf16[1024,4,7,128]{3,0,2,1:T(8,128)(2,1)} %get-tuple-element.279, bf16[1024,4,128]{2,0,1:T(8,128)(2,1)} %get-tuple-element.280), kind=kOutput, calls=%fused_computation | convolution fusion | flops 3831496704 | bytes 92913664 | tf_op jit(solution)/shard_map/while/body/eval_jaxpr/cond/branch_0_fun/qkgd,skd->kqgs/dot_general | solution.py:13
  1713.4 16.6 fusion.9
  1730.1 16.4 fusion.18
  1756.4 15.9 add.112
  1804.0 24.3 %collective-permute-done.5 = bf16[4,1024,128]{2,0,1:T(4,128)(2,1)} collective-permute-done((bf16[4,1024,128]{2,0,1:T(4,128)(2,1)S(1)}, bf16[4,1024,128]{2,0,1:T(4,128)(2,1)}, u32[]{:S(2)}, u32[]{:S(2)}) %collective-permute-start.5) | collective-permute-done | bytes 1048608 | tf_op jit(solution)/shard_map/ppermute | solution.py:69
  (134 shorter events, 244.2 us)
Async XLA Ops:
  0.6 9.3 copy-start.5
  0.6 9.9 copy-start.2
  0.7 11.1 copy-start.4
  162.1 28.9 %copy-start.3 = (bf16[1024,4,128]{2,1,0:T(4,128)(2,1)S(1)}, bf16[1024,4,128]{2,1,0:T(4,128)(2,1)}, u32[]{:S(2)}) copy-start(bf16[1024,4,128]{2,1,0:T(4,128)(2,1)} %param.11) | copy-start | bytes 3145732
  242.2 214.5 %collective-permute-start.2 = (f32[4,1024,128]{2,1,0:T(8,128)}, f32[4,1024,128]{2,1,0:T(8,128)}, u32[]{:S(2)}, u32[]{:S(2)}) collective-permute-start(f32[4,1024,128]{2,1,0:T(8,128)} %get-tuple-element.453), channel_id=1, source_target_pairs={{0,1},{1,2},{2,3},{3,4},{4,5},{5,6},{6,7},{7,0}} | collective-permute-start | bytes 6291464 | tf_op jit(solution)/shard_map/while/body/eval_jaxpr/ppermute | solution.py:61
  243.0 216.9 %collective-permute-start.3 = (f32[4,1024,128]{2,1,0:T(8,128)}, f32[4,1024,128]{2,1,0:T(8,128)}, u32[]{:S(2)}, u32[]{:S(2)}) collective-permute-start(f32[4,1024,128]{2,1,0:T(8,128)} %get-tuple-element.454), channel_id=1, source_target_pairs={{0,1},{1,2},{2,3},{3,4},{4,5},{5,6},{6,7},{7,0}} | collective-permute-start | bytes 6291464 | tf_op jit(solution)/shard_map/while/body/eval_jaxpr/ppermute | solution.py:62
  245.6 57.7 %collective-permute-start.1 = (bf16[1024,4,128]{2,0,1:T(8,128)(2,1)}, bf16[1024,4,128]{2,0,1:T(8,128)(2,1)}, u32[]{:S(2)}, u32[]{:S(2)}) collective-permute-start(bf16[1024,4,128]{2,0,1:T(8,128)(2,1)} %get-tuple-element.452), channel_id=1, source_target_pairs={{0,1},{1,2},{2,3},{3,4},{4,5},{5,6},{6,7},{7,0}} | collective-permute-start | bytes 3145736 | tf_op jit(solution)/shard_map/while/body/eval_jaxpr/ppermute | solution.py:60
  245.7 68.9 %collective-permute-start = (bf16[1024,4,128]{2,0,1:T(8,128)(2,1)}, bf16[1024,4,128]{2,0,1:T(8,128)(2,1)S(1)}, u32[]{:S(2)}, u32[]{:S(2)}) collective-permute-start(bf16[1024,4,128]{2,0,1:T(8,128)(2,1)} %get-tuple-element.451), channel_id=1, source_target_pairs={{0,1},{1,2},{2,3},{3,4},{4,5},{5,6},{6,7},{7,0}} | collective-permute-start | bytes 3145736 | tf_op jit(solution)/shard_map/while/body/eval_jaxpr/ppermute | solution.py:59
  437.5 19.1 %copy-start = (f32[4,1024,128]{2,1,0:T(8,128)S(1)}, f32[4,1024,128]{2,1,0:T(8,128)}, u32[]{:S(2)}) copy-start(f32[4,1024,128]{2,1,0:T(8,128)} %get-tuple-element.426) | copy-start | bytes 6291460 | tf_op jit(solution)/shard_map/while
  463.1 213.4 %collective-permute-start.2 = (f32[4,1024,128]{2,1,0:T(8,128)}, f32[4,1024,128]{2,1,0:T(8,128)}, u32[]{:S(2)}, u32[]{:S(2)}) collective-permute-start(f32[4,1024,128]{2,1,0:T(8,128)} %get-tuple-element.453), channel_id=1, source_target_pairs={{0,1},{1,2},{2,3},{3,4},{4,5},{5,6},{6,7},{7,0}} | collective-permute-start | bytes 6291464 | tf_op jit(solution)/shard_map/while/body/eval_jaxpr/ppermute | solution.py:61
  463.1 216.6 %collective-permute-start.3 = (f32[4,1024,128]{2,1,0:T(8,128)}, f32[4,1024,128]{2,1,0:T(8,128)}, u32[]{:S(2)}, u32[]{:S(2)}) collective-permute-start(f32[4,1024,128]{2,1,0:T(8,128)} %get-tuple-element.454), channel_id=1, source_target_pairs={{0,1},{1,2},{2,3},{3,4},{4,5},{5,6},{6,7},{7,0}} | collective-permute-start | bytes 6291464 | tf_op jit(solution)/shard_map/while/body/eval_jaxpr/ppermute | solution.py:62
  463.1 60.1 %collective-permute-start.1 = (bf16[1024,4,128]{2,0,1:T(8,128)(2,1)}, bf16[1024,4,128]{2,0,1:T(8,128)(2,1)}, u32[]{:S(2)}, u32[]{:S(2)}) collective-permute-start(bf16[1024,4,128]{2,0,1:T(8,128)(2,1)} %get-tuple-element.452), channel_id=1, source_target_pairs={{0,1},{1,2},{2,3},{3,4},{4,5},{5,6},{6,7},{7,0}} | collective-permute-start | bytes 3145736 | tf_op jit(solution)/shard_map/while/body/eval_jaxpr/ppermute | solution.py:60
  463.1 71.3 %collective-permute-start = (bf16[1024,4,128]{2,0,1:T(8,128)(2,1)}, bf16[1024,4,128]{2,0,1:T(8,128)(2,1)S(1)}, u32[]{:S(2)}, u32[]{:S(2)}) collective-permute-start(bf16[1024,4,128]{2,0,1:T(8,128)(2,1)} %get-tuple-element.451), channel_id=1, source_target_pairs={{0,1},{1,2},{2,3},{3,4},{4,5},{5,6},{6,7},{7,0}} | collective-permute-start | bytes 3145736 | tf_op jit(solution)/shard_map/while/body/eval_jaxpr/ppermute | solution.py:59
  657.3 19.1 %copy-start = (f32[4,1024,128]{2,1,0:T(8,128)S(1)}, f32[4,1024,128]{2,1,0:T(8,128)}, u32[]{:S(2)}) copy-start(f32[4,1024,128]{2,1,0:T(8,128)} %get-tuple-element.426) | copy-start | bytes 6291460 | tf_op jit(solution)/shard_map/while
  682.9 213.4 %collective-permute-start.2 = (f32[4,1024,128]{2,1,0:T(8,128)}, f32[4,1024,128]{2,1,0:T(8,128)}, u32[]{:S(2)}, u32[]{:S(2)}) collective-permute-start(f32[4,1024,128]{2,1,0:T(8,128)} %get-tuple-element.453), channel_id=1, source_target_pairs={{0,1},{1,2},{2,3},{3,4},{4,5},{5,6},{6,7},{7,0}} | collective-permute-start | bytes 6291464 | tf_op jit(solution)/shard_map/while/body/eval_jaxpr/ppermute | solution.py:61
  682.9 216.6 %collective-permute-start.3 = (f32[4,1024,128]{2,1,0:T(8,128)}, f32[4,1024,128]{2,1,0:T(8,128)}, u32[]{:S(2)}, u32[]{:S(2)}) collective-permute-start(f32[4,1024,128]{2,1,0:T(8,128)} %get-tuple-element.454), channel_id=1, source_target_pairs={{0,1},{1,2},{2,3},{3,4},{4,5},{5,6},{6,7},{7,0}} | collective-permute-start | bytes 6291464 | tf_op jit(solution)/shard_map/while/body/eval_jaxpr/ppermute | solution.py:62
  682.9 60.1 %collective-permute-start.1 = (bf16[1024,4,128]{2,0,1:T(8,128)(2,1)}, bf16[1024,4,128]{2,0,1:T(8,128)(2,1)}, u32[]{:S(2)}, u32[]{:S(2)}) collective-permute-start(bf16[1024,4,128]{2,0,1:T(8,128)(2,1)} %get-tuple-element.452), channel_id=1, source_target_pairs={{0,1},{1,2},{2,3},{3,4},{4,5},{5,6},{6,7},{7,0}} | collective-permute-start | bytes 3145736 | tf_op jit(solution)/shard_map/while/body/eval_jaxpr/ppermute | solution.py:60
  682.9 71.3 %collective-permute-start = (bf16[1024,4,128]{2,0,1:T(8,128)(2,1)}, bf16[1024,4,128]{2,0,1:T(8,128)(2,1)S(1)}, u32[]{:S(2)}, u32[]{:S(2)}) collective-permute-start(bf16[1024,4,128]{2,0,1:T(8,128)(2,1)} %get-tuple-element.451), channel_id=1, source_target_pairs={{0,1},{1,2},{2,3},{3,4},{4,5},{5,6},{6,7},{7,0}} | collective-permute-start | bytes 3145736 | tf_op jit(solution)/shard_map/while/body/eval_jaxpr/ppermute | solution.py:59
  877.2 19.1 %copy-start = (f32[4,1024,128]{2,1,0:T(8,128)S(1)}, f32[4,1024,128]{2,1,0:T(8,128)}, u32[]{:S(2)}) copy-start(f32[4,1024,128]{2,1,0:T(8,128)} %get-tuple-element.426) | copy-start | bytes 6291460 | tf_op jit(solution)/shard_map/while
  902.7 213.4 %collective-permute-start.2 = (f32[4,1024,128]{2,1,0:T(8,128)}, f32[4,1024,128]{2,1,0:T(8,128)}, u32[]{:S(2)}, u32[]{:S(2)}) collective-permute-start(f32[4,1024,128]{2,1,0:T(8,128)} %get-tuple-element.453), channel_id=1, source_target_pairs={{0,1},{1,2},{2,3},{3,4},{4,5},{5,6},{6,7},{7,0}} | collective-permute-start | bytes 6291464 | tf_op jit(solution)/shard_map/while/body/eval_jaxpr/ppermute | solution.py:61
  902.7 216.6 %collective-permute-start.3 = (f32[4,1024,128]{2,1,0:T(8,128)}, f32[4,1024,128]{2,1,0:T(8,128)}, u32[]{:S(2)}, u32[]{:S(2)}) collective-permute-start(f32[4,1024,128]{2,1,0:T(8,128)} %get-tuple-element.454), channel_id=1, source_target_pairs={{0,1},{1,2},{2,3},{3,4},{4,5},{5,6},{6,7},{7,0}} | collective-permute-start | bytes 6291464 | tf_op jit(solution)/shard_map/while/body/eval_jaxpr/ppermute | solution.py:62
  902.7 60.1 %collective-permute-start.1 = (bf16[1024,4,128]{2,0,1:T(8,128)(2,1)}, bf16[1024,4,128]{2,0,1:T(8,128)(2,1)}, u32[]{:S(2)}, u32[]{:S(2)}) collective-permute-start(bf16[1024,4,128]{2,0,1:T(8,128)(2,1)} %get-tuple-element.452), channel_id=1, source_target_pairs={{0,1},{1,2},{2,3},{3,4},{4,5},{5,6},{6,7},{7,0}} | collective-permute-start | bytes 3145736 | tf_op jit(solution)/shard_map/while/body/eval_jaxpr/ppermute | solution.py:60
  902.8 71.3 %collective-permute-start = (bf16[1024,4,128]{2,0,1:T(8,128)(2,1)}, bf16[1024,4,128]{2,0,1:T(8,128)(2,1)S(1)}, u32[]{:S(2)}, u32[]{:S(2)}) collective-permute-start(bf16[1024,4,128]{2,0,1:T(8,128)(2,1)} %get-tuple-element.451), channel_id=1, source_target_pairs={{0,1},{1,2},{2,3},{3,4},{4,5},{5,6},{6,7},{7,0}} | collective-permute-start | bytes 3145736 | tf_op jit(solution)/shard_map/while/body/eval_jaxpr/ppermute | solution.py:59
  1097.0 19.1 %copy-start = (f32[4,1024,128]{2,1,0:T(8,128)S(1)}, f32[4,1024,128]{2,1,0:T(8,128)}, u32[]{:S(2)}) copy-start(f32[4,1024,128]{2,1,0:T(8,128)} %get-tuple-element.426) | copy-start | bytes 6291460 | tf_op jit(solution)/shard_map/while
  1122.5 213.4 %collective-permute-start.2 = (f32[4,1024,128]{2,1,0:T(8,128)}, f32[4,1024,128]{2,1,0:T(8,128)}, u32[]{:S(2)}, u32[]{:S(2)}) collective-permute-start(f32[4,1024,128]{2,1,0:T(8,128)} %get-tuple-element.453), channel_id=1, source_target_pairs={{0,1},{1,2},{2,3},{3,4},{4,5},{5,6},{6,7},{7,0}} | collective-permute-start | bytes 6291464 | tf_op jit(solution)/shard_map/while/body/eval_jaxpr/ppermute | solution.py:61
  1122.6 216.6 %collective-permute-start.3 = (f32[4,1024,128]{2,1,0:T(8,128)}, f32[4,1024,128]{2,1,0:T(8,128)}, u32[]{:S(2)}, u32[]{:S(2)}) collective-permute-start(f32[4,1024,128]{2,1,0:T(8,128)} %get-tuple-element.454), channel_id=1, source_target_pairs={{0,1},{1,2},{2,3},{3,4},{4,5},{5,6},{6,7},{7,0}} | collective-permute-start | bytes 6291464 | tf_op jit(solution)/shard_map/while/body/eval_jaxpr/ppermute | solution.py:62
  1122.6 60.1 %collective-permute-start.1 = (bf16[1024,4,128]{2,0,1:T(8,128)(2,1)}, bf16[1024,4,128]{2,0,1:T(8,128)(2,1)}, u32[]{:S(2)}, u32[]{:S(2)}) collective-permute-start(bf16[1024,4,128]{2,0,1:T(8,128)(2,1)} %get-tuple-element.452), channel_id=1, source_target_pairs={{0,1},{1,2},{2,3},{3,4},{4,5},{5,6},{6,7},{7,0}} | collective-permute-start | bytes 3145736 | tf_op jit(solution)/shard_map/while/body/eval_jaxpr/ppermute | solution.py:60
  1122.6 71.3 %collective-permute-start = (bf16[1024,4,128]{2,0,1:T(8,128)(2,1)}, bf16[1024,4,128]{2,0,1:T(8,128)(2,1)S(1)}, u32[]{:S(2)}, u32[]{:S(2)}) collective-permute-start(bf16[1024,4,128]{2,0,1:T(8,128)(2,1)} %get-tuple-element.451), channel_id=1, source_target_pairs={{0,1},{1,2},{2,3},{3,4},{4,5},{5,6},{6,7},{7,0}} | collective-permute-start | bytes 3145736 | tf_op jit(solution)/shard_map/while/body/eval_jaxpr/ppermute | solution.py:59
  1316.8 19.1 %copy-start = (f32[4,1024,128]{2,1,0:T(8,128)S(1)}, f32[4,1024,128]{2,1,0:T(8,128)}, u32[]{:S(2)}) copy-start(f32[4,1024,128]{2,1,0:T(8,128)} %get-tuple-element.426) | copy-start | bytes 6291460 | tf_op jit(solution)/shard_map/while
  1342.4 213.4 %collective-permute-start.2 = (f32[4,1024,128]{2,1,0:T(8,128)}, f32[4,1024,128]{2,1,0:T(8,128)}, u32[]{:S(2)}, u32[]{:S(2)}) collective-permute-start(f32[4,1024,128]{2,1,0:T(8,128)} %get-tuple-element.453), channel_id=1, source_target_pairs={{0,1},{1,2},{2,3},{3,4},{4,5},{5,6},{6,7},{7,0}} | collective-permute-start | bytes 6291464 | tf_op jit(solution)/shard_map/while/body/eval_jaxpr/ppermute | solution.py:61
  1342.4 216.6 %collective-permute-start.3 = (f32[4,1024,128]{2,1,0:T(8,128)}, f32[4,1024,128]{2,1,0:T(8,128)}, u32[]{:S(2)}, u32[]{:S(2)}) collective-permute-start(f32[4,1024,128]{2,1,0:T(8,128)} %get-tuple-element.454), channel_id=1, source_target_pairs={{0,1},{1,2},{2,3},{3,4},{4,5},{5,6},{6,7},{7,0}} | collective-permute-start | bytes 6291464 | tf_op jit(solution)/shard_map/while/body/eval_jaxpr/ppermute | solution.py:62
  1342.4 60.1 %collective-permute-start.1 = (bf16[1024,4,128]{2,0,1:T(8,128)(2,1)}, bf16[1024,4,128]{2,0,1:T(8,128)(2,1)}, u32[]{:S(2)}, u32[]{:S(2)}) collective-permute-start(bf16[1024,4,128]{2,0,1:T(8,128)(2,1)} %get-tuple-element.452), channel_id=1, source_target_pairs={{0,1},{1,2},{2,3},{3,4},{4,5},{5,6},{6,7},{7,0}} | collective-permute-start | bytes 3145736 | tf_op jit(solution)/shard_map/while/body/eval_jaxpr/ppermute | solution.py:60
  1342.4 71.3 %collective-permute-start = (bf16[1024,4,128]{2,0,1:T(8,128)(2,1)}, bf16[1024,4,128]{2,0,1:T(8,128)(2,1)S(1)}, u32[]{:S(2)}, u32[]{:S(2)}) collective-permute-start(bf16[1024,4,128]{2,0,1:T(8,128)(2,1)} %get-tuple-element.451), channel_id=1, source_target_pairs={{0,1},{1,2},{2,3},{3,4},{4,5},{5,6},{6,7},{7,0}} | collective-permute-start | bytes 3145736 | tf_op jit(solution)/shard_map/while/body/eval_jaxpr/ppermute | solution.py:59
  1536.6 19.1 %copy-start = (f32[4,1024,128]{2,1,0:T(8,128)S(1)}, f32[4,1024,128]{2,1,0:T(8,128)}, u32[]{:S(2)}) copy-start(f32[4,1024,128]{2,1,0:T(8,128)} %get-tuple-element.426) | copy-start | bytes 6291460 | tf_op jit(solution)/shard_map/while
  1562.2 213.4 %collective-permute-start.2 = (f32[4,1024,128]{2,1,0:T(8,128)}, f32[4,1024,128]{2,1,0:T(8,128)}, u32[]{:S(2)}, u32[]{:S(2)}) collective-permute-start(f32[4,1024,128]{2,1,0:T(8,128)} %get-tuple-element.453), channel_id=1, source_target_pairs={{0,1},{1,2},{2,3},{3,4},{4,5},{5,6},{6,7},{7,0}} | collective-permute-start | bytes 6291464 | tf_op jit(solution)/shard_map/while/body/eval_jaxpr/ppermute | solution.py:61
  1562.2 216.6 %collective-permute-start.3 = (f32[4,1024,128]{2,1,0:T(8,128)}, f32[4,1024,128]{2,1,0:T(8,128)}, u32[]{:S(2)}, u32[]{:S(2)}) collective-permute-start(f32[4,1024,128]{2,1,0:T(8,128)} %get-tuple-element.454), channel_id=1, source_target_pairs={{0,1},{1,2},{2,3},{3,4},{4,5},{5,6},{6,7},{7,0}} | collective-permute-start | bytes 6291464 | tf_op jit(solution)/shard_map/while/body/eval_jaxpr/ppermute | solution.py:62
  1562.2 60.1 %collective-permute-start.1 = (bf16[1024,4,128]{2,0,1:T(8,128)(2,1)}, bf16[1024,4,128]{2,0,1:T(8,128)(2,1)}, u32[]{:S(2)}, u32[]{:S(2)}) collective-permute-start(bf16[1024,4,128]{2,0,1:T(8,128)(2,1)} %get-tuple-element.452), channel_id=1, source_target_pairs={{0,1},{1,2},{2,3},{3,4},{4,5},{5,6},{6,7},{7,0}} | collective-permute-start | bytes 3145736 | tf_op jit(solution)/shard_map/while/body/eval_jaxpr/ppermute | solution.py:60
  1562.2 71.3 %collective-permute-start = (bf16[1024,4,128]{2,0,1:T(8,128)(2,1)}, bf16[1024,4,128]{2,0,1:T(8,128)(2,1)S(1)}, u32[]{:S(2)}, u32[]{:S(2)}) collective-permute-start(bf16[1024,4,128]{2,0,1:T(8,128)(2,1)} %get-tuple-element.451), channel_id=1, source_target_pairs={{0,1},{1,2},{2,3},{3,4},{4,5},{5,6},{6,7},{7,0}} | collective-permute-start | bytes 3145736 | tf_op jit(solution)/shard_map/while/body/eval_jaxpr/ppermute | solution.py:59
  1756.4 19.1 %copy-start = (f32[4,1024,128]{2,1,0:T(8,128)S(1)}, f32[4,1024,128]{2,1,0:T(8,128)}, u32[]{:S(2)}) copy-start(f32[4,1024,128]{2,1,0:T(8,128)} %get-tuple-element.426) | copy-start | bytes 6291460 | tf_op jit(solution)/shard_map/while
  1790.7 37.6 %collective-permute-start.4 = (f32[4,1024,128]{2,0,1:T(4,128)}, f32[4,1024,128]{2,0,1:T(4,128)S(1)}, u32[]{:S(2)}, u32[]{:S(2)}) collective-permute-start(f32[4,1024,128]{2,0,1:T(4,128)} %copy.33), channel_id=1, source_target_pairs={{0,1},{1,2},{2,3},{3,4},{4,5},{5,6},{6,7},{7,0}} | collective-permute-start | bytes 6291464 | tf_op jit(solution)/shard_map/ppermute | solution.py:68
  1793.6 34.6 %collective-permute-start.5 = (bf16[4,1024,128]{2,0,1:T(4,128)(2,1)S(1)}, bf16[4,1024,128]{2,0,1:T(4,128)(2,1)}, u32[]{:S(2)}, u32[]{:S(2)}) collective-permute-start(bf16[4,1024,128]{2,0,1:T(4,128)(2,1)S(1)} %copy.34), channel_id=1, source_target_pairs={{0,1},{1,2},{2,3},{3,4},{4,5},{5,6},{6,7},{7,0}} | collective-permute-start | bytes 3145736 | tf_op jit(solution)/shard_map/ppermute | solution.py:69
where the time goes:
time: 1840 us; the launch traced here: 1830 us
  matrix products  997 us (54%)
  waiting for transfers between devices  519 us (28%)
  other arithmetic  178 us (10%)
  local copies, waits for them, and re-layouts  104 us (6%)
  loops' own time  27.8 us (2%)
    ppermute x7, waiting for transfers between devices, step_body(): v_cur = lax.ppermute(v_cur, ctx_axes, shift_perm)  416 us
    dot_general x8, matrix products, block_grads(): jnp.einsum('qkgd,skd->kqgs', do_blk, v_blk, preferred_element_type=jnp.fl...  303 us
    dot_general x8, matrix products, block_grads(): jnp.einsum('kqgs,qkgd->ksd', prob_b16, do_blk, preferred_element_type=jnp...  207 us
    dot_general x8, matrix products, block_grads(): jnp.einsum('qkgd,skd->kqgs', q_blk, k_blk, preferred_element_type=jnp.flo...  199 us
    add x21, other arithmetic, step_body(): return (k_cur, v_cur, dk_cur + dk_part, dv_cur + dv_part, dq_cur + dq_part)  156 us
    dot_general x8, matrix products, block_grads(): jnp.einsum('kqgs,qkgd->ksd', dscore_b16, q_blk, preferred_element_type=jn...  145 us
    dot_general x8, matrix products, block_grads(): jnp.einsum('kqgs,skd->kqgd', dscore_b16, k_blk, preferred_element_type=jn...  143 us
    ppermute x7, waiting for transfers between devices, step_body(): k_cur = lax.ppermute(k_cur, ctx_axes, shift_perm)  78.6 us
  transfers between devices with their start and end apart: 30, of which 15 were waited for; matrix products, arithmetic and copies ran while one was open for 56% of the time, Pallas kernels for 0%

commit v1 on v0

v1 whole, which is shorter than its diff:
```python
import math
import jax
import jax.numpy as jnp
from jax import lax
from jax.experimental import pallas as pl
from jax.experimental.pallas import tpu as pltpu
from jax.sharding import PartitionSpec as P

LOG2E = math.log2(math.e)
F32 = jnp.float32
BF16 = jnp.bfloat16
Q_TILE = 256


def group_kernel(n_piece, tab_ref, q_ref, do_ref, lse_ref, delta_ref, k_ref, v_ref, dq_ref, dkv_ref, kt_scr, vt_scr, p_scr, ds_scr, dk_acc, dv_acc, dq_acc):
    n_head, tok_dev, head_dim = q_ref.shape
    half_tok = tok_dev // 2
    scaling = 1.0 / math.sqrt(head_dim)
    step = pl.program_id(0)
    q_half = tab_ref[step, 1]
    kind = tab_ref[step, 2]
    is_first = tab_ref[step, 3]
    is_last = tab_ref[step, 4]
    n_sub = half_tok // Q_TILE

    @pl.when(step == 0)
    def _():
        dq_acc[...] = jnp.zeros_like(dq_acc)

    @pl.when(is_first == 1)
    def _():
        dk_acc[...] = jnp.zeros_like(dk_acc)
        dv_acc[...] = jnp.zeros_like(dv_acc)

    def run_task(masked):
        kt_scr[...] = k_ref[...].T
        vt_scr[...] = v_ref[...].T
        row0 = pl.multiple_of(q_half * half_tok, half_tok)

        def scores(h, sub, slot):
            rows = pl.ds(row0 + sub * Q_TILE, Q_TILE)
            n_key = half_tok if not masked else (sub + 1) * Q_TILE
            s = jnp.dot(q_ref[h, rows, :], kt_scr[:, :n_key], preferred_element_type=F32)
            dp = jnp.dot(do_ref[h, rows, :], vt_scr[:, :n_key], preferred_element_type=F32)
            lse = jnp.tile(lse_ref[h, rows, :], (1, n_key // 128))
            dlt = jnp.tile(delta_ref[h, rows, :], (1, n_key // 128))
            prob = jnp.exp2(s * (scaling * LOG2E) - lse)
            if masked:
                qi = lax.broadcasted_iota(jnp.int32, s.shape, 0) + sub * Q_TILE
                kj = lax.broadcasted_iota(jnp.int32, s.shape, 1)
                prob = jnp.where(qi >= kj, prob, 0.0)
            p_scr[slot, :, :n_key] = prob.astype(BF16)
            ds_scr[slot, :, :n_key] = (prob * (dp - dlt)).astype(BF16)

        def grads(h, sub, slot):
            rows = pl.ds(row0 + sub * Q_TILE, Q_TILE)
            n_key = half_tok if not masked else (sub + 1) * Q_TILE
            prob = p_scr[slot, :, :n_key]
            ds = ds_scr[slot, :, :n_key]
            dv_acc[:, :n_key] += lax.dot_general(do_ref[h, rows, :], prob, (((0,), (0,)), ((), ())), preferred_element_type=F32)
            dk_acc[:, :n_key] += lax.dot_general(q_ref[h, rows, :], ds, (((0,), (0,)), ((), ())), preferred_element_type=F32)
            dq_acc[h, rows, :] += jnp.dot(ds, k_ref[:n_key, :], preferred_element_type=F32)

        tiles = [(h, sub) for h in range(n_head) for sub in range(n_sub)]
        scores(*tiles[0], 0)
        for idx, tile in enumerate(tiles):
            if idx + 1 < len(tiles):
                scores(*tiles[idx + 1], (idx + 1) % 2)
            grads(*tile, idx % 2)

    @pl.when(kind == 1)
    def _():
        run_task(False)

    @pl.when(kind == 2)
    def _():
        run_task(True)

    @pl.when(is_last == 1)
    def _():
        dkv_ref[0] = dk_acc[...].T * scaling
        dkv_ref[1] = dv_acc[...].T

    @pl.when(step == pl.num_programs(0) - 1)
    def _():
        dq_ref[...] = (dq_acc[...] * scaling).astype(BF16)


def solution(mesh):
    n_cx = mesh.shape['cx']
    n_ctx = mesh.shape['cy'] * n_cx
    ctx_axes = ('cy', 'cx')
    row_spec = P(('dp', 'cy', 'cx'), None, None)
    stat_spec = P(('dp', 'cy', 'cx'), None)

    def local_grads(query_rows, key_rows, value_rows, out_rows, grad_out, log_sum_exp):
        tok_dev, n_heads, head_dim = query_rows.shape
        kv_heads = key_rows.shape[1]
        group_size = n_heads // kv_heads
        half_tok = tok_dev // 2
        n_piece = 2 * n_ctx
        n_step = 2 * n_piece - n_ctx
        ctx_rank = lax.axis_index('cy') * n_cx + lax.axis_index('cx')

        step = jnp.arange(n_step, dtype=jnp.int32)
        both = step < 2 * ctx_rank + 2
        piece = jnp.where(both, step // 2, step - ctx_rank - 1)
        idle = piece > n_piece - 1
        piece = jnp.minimum(piece, n_piece - 1)
        q_half = jnp.where(both, step % 2, 1)
        late = n_piece - 1 - ctx_rank
        diag = jnp.where(q_half == 0, piece == ctx_rank, piece == late)
        kind = jnp.where(idle | (piece > late), 0, jnp.where(diag, 2, 1))
        first = jnp.where(idle, 0, jnp.where(both, 1 - q_half, 1))
        last = jnp.where(idle, 0, q_half)
        slot = jnp.where(piece < n_ctx, 2 * piece, 2 * (n_piece - 1 - piece) + 1)
        table = jnp.stack([slot, q_half, kind, first, last], axis=1).astype(jnp.int32)

        def heads_first(rows):
            return rows.reshape(tok_dev, kv_heads, group_size, head_dim).transpose(1, 2, 0, 3)

        def lanes(stat):
            stat_t = stat.reshape(tok_dev, kv_heads, group_size).transpose(1, 2, 0)
            return jnp.broadcast_to(stat_t[..., None], stat_t.shape + (128,))

        kv_rows = jnp.stack([key_rows, value_rows]).transpose(2, 0, 1, 3)
        kv_all = [lax.all_gather(kv_rows[g], ctx_axes) for g in range(kv_heads)]
        delta = jnp.einsum('thd,thd->th', grad_out, out_rows, preferred_element_type=F32)
        q_hf, do_hf = heads_first(query_rows), heads_first(grad_out)
        lse_l, delta_l = lanes(log_sum_exp * LOG2E), lanes(delta)

        call = pl.pallas_call(
            lambda *refs: group_kernel(n_piece, *refs),
            grid_spec=pltpu.PrefetchScalarGridSpec(
                num_scalar_prefetch=1,
                grid=(n_step,),
                in_specs=[
                    pl.BlockSpec((group_size, tok_dev, head_dim), lambda t, tab: (0, 0, 0), pipeline_mode=pl.Buffered(1)),
                    pl.BlockSpec((group_size, tok_dev, head_dim), lambda t, tab: (0, 0, 0), pipeline_mode=pl.Buffered(1)),
                    pl.BlockSpec((group_size, tok_dev, 128), lambda t, tab: (0, 0, 0), pipeline_mode=pl.Buffered(1)),
                    pl.BlockSpec((group_size, tok_dev, 128), lambda t, tab: (0, 0, 0), pipeline_mode=pl.Buffered(1)),
                    pl.BlockSpec((None, None, None, half_tok, head_dim), lambda t, tab: (tab[t, 0] // 2, 0, tab[t, 0] % 2, 0, 0)),
                    pl.BlockSpec((None, None, None, half_tok, head_dim), lambda t, tab: (tab[t, 0] // 2, 1, tab[t, 0] % 2, 0, 0)),
                ],
                out_specs=[
                    pl.BlockSpec((group_size, tok_dev, head_dim), lambda t, tab: (0, 0, 0), pipeline_mode=pl.Buffered(1)),
                    pl.BlockSpec((None, 2, None, half_tok, head_dim), lambda t, tab: (tab[t, 0] // 2, 0, tab[t, 0] % 2, 0, 0)),
                ],
                scratch_shapes=[
                    pltpu.VMEM((head_dim, half_tok), BF16),
                    pltpu.VMEM((head_dim, half_tok), BF16),
                    pltpu.VMEM((2, Q_TILE, half_tok), BF16),
                    pltpu.VMEM((2, Q_TILE, half_tok), BF16),
                    pltpu.VMEM((head_dim, half_tok), F32),
                    pltpu.VMEM((head_dim, half_tok), F32),
                    pltpu.VMEM((group_size, tok_dev, head_dim), F32),
                ],
            ),
            out_shape=[
                jax.ShapeDtypeStruct((group_size, tok_dev, head_dim), BF16),
                jax.ShapeDtypeStruct((n_ctx, 2, 2, half_tok, head_dim), F32),
            ],
            compiler_params=pltpu.CompilerParams(dimension_semantics=('arbitrary',), vmem_limit_bytes=48 * 1024 * 1024),
            cost_estimate=pl.CostEstimate(flops=17 * group_size * 10 * half_tok * half_tok * head_dim, bytes_accessed=32 * 1024 * 1024, transcendentals=17 * group_size * half_tok * half_tok),
            name='group_grads',
        )

        dq_parts, dkv_parts = [], []
        for g in range(kv_heads):
            kv_g = kv_all[g].reshape(n_ctx, 2, 2, half_tok, head_dim)
            dq_g, dkv_g = call(table, q_hf[g], do_hf[g], lse_l[g], delta_l[g], kv_g, kv_g)
            dq_parts.append(dq_g)
            dkv_parts.append(lax.psum_scatter(dkv_g, ctx_axes, scatter_dimension=0, tiled=False))
        grad_query = jnp.stack(dq_parts).transpose(2, 0, 1, 3).reshape(tok_dev, n_heads, head_dim)
        dkv = jnp.stack([x.reshape(2, tok_dev, head_dim) for x in dkv_parts], axis=2)
        dkv_b16 = dkv.astype(BF16)
        return grad_query, dkv_b16[0], dkv_b16[1]

    return jax.shard_map(local_grads, mesh=mesh, in_specs=(row_spec, row_spec, row_spec, row_spec, row_spec, stat_spec), out_specs=(row_spec, row_spec, row_spec), check_vma=False)
```

time: 1840 us -> 485 us (0.26)
  matrix products: 997 us -> 0 us
  waiting for transfers between devices: 519 us -> 71.2 us
  Pallas kernels: 0 us -> 322 us
  other arithmetic: 178 us -> 25.7 us
  local copies, waits for them, and re-layouts: 104 us -> 45.5 us
  loops' own time: 27.8 us -> 0 us
    dot_general x40 -> x0, matrix products: 997 us -> none  [the longest x8 303 us: block_grads(): jnp.einsum('qkgd,skd->kqgs', do_blk, v_blk, preferred_element_type=jnp.fl...]
    ppermute x30 -> x0, waiting for transfers between devices: 519 us -> none  [the longest x7 416 us: step_body(): v_cur = lax.ppermute(v_cur, ctx_axes, shift_perm)]
    pallas_call x0 -> x4, Pallas kernels: none -> 322 us  [local_grads(): call(table, q_hf[g], do_hf[g], lse_l[g], delta_l[g], kv_g, kv_g)]
    add x22 -> x0, other arithmetic: 156 us -> none  [the longest x21 156 us: step_body(): return (k_cur, v_cur, dk_cur + dk_part, dv_cur + dv_part, dq_cur + dq_part)]
    concatenate x7 -> x0, local copies, waits for them, and re-layouts: 69.7 us -> none  [src_after(): return (jnp.concatenate([zero_pad, dq_part], axis=1), dk_part, dv_part)]
    reduce_scatter x0 -> x4, waiting for transfers between devices: none -> 57.6 us  [local_grads(): lax.psum_scatter(dkv_g, ctx_axes, scatter_dimension=0, tiled=False)]
    while x32 -> x0, local copies, waits for them, and re-layouts: 32.1 us -> none
    another operation x8 -> x0, loops' own time: 27.8 us -> none  [the longest x1 27.7 us: local_grads(): lax.fori_loop(1, n_ctx, step_body, (key_rows, value_rows, dk_own, dv_own,...]
  transfers between devices with their start and end apart: 30 -> 8, of which waited for: 15 -> 2; matrix products, arithmetic and copies ran while one was open for 56% -> 11% of each run, Pallas kernels for 0% -> 67%
where the time goes in v1:
time: 485 us; the launch traced here: 480 us
  Pallas kernels  322 us (66%)
  waiting for transfers between devices  71.2 us (15%)
  local copies, waits for them, and re-layouts  45.5 us (9%)
  other arithmetic  25.7 us (5%)
  between operations  14.9 us (3%)
    pallas_call x4, Pallas kernels, local_grads(): call(table, q_hf[g], do_hf[g], lse_l[g], delta_l[g], kv_g, kv_g)  322 us
    reduce_scatter x4, waiting for transfers between devices, local_grads(): lax.psum_scatter(dkv_g, ctx_axes, scatter_dimension=0, tiled=False)  57.6 us
    broadcast_in_dim x10, local copies, waits for them, and re-layouts, lanes(): return jnp.broadcast_to(stat_t[..., None], stat_t.shape + (128,))  19.7 us
    all_gather x4, waiting for transfers between devices, local_grads(): kv_all = [lax.all_gather(kv_rows[g], ctx_axes) for g in range(kv_heads)]  11.7 us
    squeeze x1, local copies, waits for them, and re-layouts, local_grads(): do_hf[g]  10.7 us
  transfers between devices with their start and end apart: 8, of which 2 were waited for; matrix products, arithmetic and copies ran while one was open for 11% of the time, Pallas kernels for 67%

profile of v1, /device:TPU:0, one launch (start us, length us, event | category | flops | bytes accessed | tf_op | source)
XLA Modules:
  0.0 480.0 jit_solution(14526195930127496696)
XLA Ops:
  7.2 0.0 all-gather.5.cloned.1.call-start
  7.2 1.8 copy_bitcast_fusion
  9.0 0.2 maximum_bitcast_fusion
  9.2 0.0 copy-start.12
  9.2 1.3 fusion.4
  10.6 0.0 all-gather.5.cloned.1.call-update
  10.6 0.0 all-gather.7.cloned.1.call-start
  10.7 0.7 all-gather.7.cloned.1.call-update
  11.4 0.0 all-gather.9.cloned.1.call-start
  11.4 0.7 all-gather.9.cloned.1.call-update
  12.1 0.0 all-gather.11.cloned.1.call-start
  12.1 0.5 all-gather.11.cloned.1.call-update
  12.7 0.0 reduce-scatter.5.cloned.1.call-start
  12.8 0.1 copy.27.refs_0_
  12.9 0.0 copy-done.12
  12.9 9.0 %fusion = f32[1024,28]{0,1:T(8,128)S(1)} fusion(bf16[1024,28,128]{2,0,1:T(8,128)(2,1)} %param.10, bf16[1024,28,128]{2,0,1:T(8,128)(2,1)} %param.9), kind=kLoop, calls=%fused_computation.1 | loop fusion | flops 14651392 | bytes 14794752 | tf_op jit(solution)/shard_map/thd,thd->th/dot_general | solution.py:128
  22.0 10.7 %slice_bitcast_fusion.6 = (bf16[7,1024,128]{2,1,0:T(8,128)(2,1)}, bf16[7,1024,128]{2,1,0:T(8,128)(2,1)S(1)}, bf16[7,1024,128]{2,1,0:T(8,128)(2,1)}, bf16[7,1024,...) fusion(bf16[4,7,1024,128]{3,2,1,0:T(8,128)(2,1)} %bitcast.73, ...), kind=kLoop, calls=%fused_computation.11 | loop fusion | bytes 29360128 | tf_op jit(solution)/shard_map/squeeze | solution.py:171
  32.7 11.6 %all-gather.5.cloned.1.call-done = bf16[8,2,1024,128]{3,2,1,0:T(8,128)(2,1)} async-done(((bf16[1,2,1024,128]{3,2,1,0:T(8,128)(2,1)}), bf16[8,2,1024,128]{3,2,1,0:T(8,128)(2,1)}) %all-gather.5.cloned.1.call-update) | async-done | bytes 4194320 | tf_op jit(solution)/shard_map/all_gather | solution.py:127
  44.3 2.4 broadcast_in_dim.53.refs_3_
  46.8 2.4 broadcast_in_dim.55.refs_4_
  49.1 0.0 copy-done.5
  49.1 80.4 %group_grads.4 = (bf16[7,1024,128]{2,1,0:T(8,128)(2,1)S(1)}, f32[8,2,2,512,128]{4,3,2,1,0:T(8,128)}) custom-call(s32[24,5]{1,0:T(8,128)S(1)} %copy.27.refs_0_, bf16[7,1024,128]{2,1,0:T(8,128)(2,1)S(1)} %copy-done.6, bf16[7,1024,128]{2,1,0:T(8,128)(2,1)S(1)} %copy-done.5, f32[7,1024,128]{2,1,0:T(8,128)} %broadcast_in_dim.53.refs_3_, ...), custom_call_target="tpu_custom_call" | custom-call | flops 39929774080 | bytes 33554432 | tf_op jit(solution)/shard_map/group_grads/pallas_call | solution.py:171
  129.5 1.2 copy-done.7
  130.7 0.0 reduce-scatter.5.cloned.1.call-update
  130.7 0.0 reduce-scatter.7.cloned.1.call-start
  130.8 0.0 all-gather.7.cloned.1.call-done
  130.8 2.6 broadcast_in_dim.57.refs_3_
  133.4 2.4 broadcast_in_dim.59.refs_4_
  135.7 0.0 copy-done.4
  135.7 80.4 %group_grads.5 = (bf16[7,1024,128]{2,1,0:T(8,128)(2,1)S(1)}, f32[8,2,2,512,128]{4,3,2,1,0:T(8,128)}) custom-call(s32[24,5]{1,0:T(8,128)S(1)} %copy.27.refs_0_, bf16[7,1024,128]{2,1,0:T(8,128)(2,1)S(1)} %copy-done.4, bf16[7,1024,128]{2,1,0:T(8,128)(2,1)S(1)} %copy-done.3, f32[7,1024,128]{2,1,0:T(8,128)} %broadcast_in_dim.57.refs_3_, ...), custom_call_target="tpu_custom_call" | custom-call | flops 39929774080 | bytes 33554432 | tf_op jit(solution)/shard_map/group_grads/pallas_call | solution.py:171
  216.1 1.3 copy-done.9
  217.4 0.0 reduce-scatter.7.cloned.1.call-update
  217.4 0.0 reduce-scatter.9.cloned.1.call-start
  217.5 0.0 all-gather.9.cloned.1.call-done
  217.5 2.6 broadcast_in_dim.61.refs_3_
  220.1 2.4 broadcast_in_dim.63.refs_4_
  222.5 0.0 copy-done.2
  222.5 80.4 %group_grads.6 = (bf16[7,1024,128]{2,1,0:T(8,128)(2,1)S(1)}, f32[8,2,2,512,128]{4,3,2,1,0:T(8,128)}) custom-call(s32[24,5]{1,0:T(8,128)S(1)} %copy.27.refs_0_, bf16[7,1024,128]{2,1,0:T(8,128)(2,1)S(1)} %copy-done.2, bf16[7,1024,128]{2,1,0:T(8,128)(2,1)S(1)} %copy-done.1, f32[7,1024,128]{2,1,0:T(8,128)} %broadcast_in_dim.61.refs_3_, ...), custom_call_target="tpu_custom_call" | custom-call | flops 39929774080 | bytes 33554432 | tf_op jit(solution)/shard_map/group_grads/pallas_call | solution.py:171
  302.9 1.3 copy-done.10
  304.1 0.0 reduce-scatter.9.cloned.1.call-update
  304.2 0.0 reduce-scatter.11.cloned.1.call-start
  304.2 0.0 all-gather.11.cloned.1.call-done
  304.2 0.0 copy-start
  304.2 2.6 broadcast_in_dim.65.refs_3_
  306.9 2.3 broadcast_in_dim.67.refs_4_
  309.2 81.3 %group_grads.7 = (bf16[7,1024,128]{2,1,0:T(8,128)(2,1)S(1)}, f32[8,2,2,512,128]{4,3,2,1,0:T(8,128)}) custom-call(s32[24,5]{1,0:T(8,128)S(1)} %copy.27.refs_0_, bf16[7,1024,128]{2,1,0:T(8,128)(2,1)S(1)} %copy-done, bf16[7,1024,128]{2,1,0:T(8,128)(2,1)S(1)} %get-tuple-element.20.refs_2_, f32[7,1024,128]{2,1,0:T(8,128)} %broadcast_in_dim.65.refs_3_, ...), custom_call_target="tpu_custom_call" | custom-call | flops 39929774080 | bytes 33554432 | tf_op jit(solution)/shard_map/group_grads/pallas_call | solution.py:171
  390.6 1.2 copy-done.11
  391.8 0.0 reduce-scatter.11.cloned.1.call-update
  391.8 1.5 copy-done.8
  393.3 6.4 %pad_maximum_fusion = bf16[4,7,1024,128]{3,2,1,0:T(8,128)(2,1)} fusion(bf16[1,7,1024,128]{3,2,1,0:T(8,128)(2,1)} %bitcast.72, bf16[1,7,1024,128]{3,2,1,0:T(8,128)(2,1)} %bitcast.71, bf16[1,7,1024,128]{3,2,1,0:T(8,128)(2,1)} %bitcast.70, bf16[1,7,1024,128]{3,2,1,0:T(8,128)(2,1)S(1)} %bitcast.69), kind=kLoop, calls=%fused_computation.2 | loop fusion | flops 11010048 | bytes 14680064 | tf_op jit(solution)/shard_map/stack | solution.py:174
  399.7 0.0 reduce-scatter.5.cloned.1.call-done
  399.7 1.3 convert.16
  401.0 0.8 copy.31
  401.8 0.0 reduce-scatter.7.cloned.1.call-done
  401.9 1.3 convert.17
  403.2 0.8 copy.32
  404.0 0.0 reduce-scatter.9.cloned.1.call-done
  404.0 1.3 convert.18
  405.3 0.8 copy.33
  406.1 57.5 %reduce-scatter.11.cloned.1.call-done = f32[1,2,2,512,128]{4,3,2,1,0:T(8,128)} async-done(((f32[8,2,2,512,128]{4,3,2,1,0:T(8,128)}), f32[1,2,2,512,128]{4,3,2,1,0:T(8,128)}) %reduce-scatter.11.cloned.1.call-update) | async-done | bytes 1048592 | tf_op jit(solution)/shard_map/reduce_scatter | solution.py:173
  463.6 1.3 convert.19
  464.9 0.8 copy.34
  465.7 4.9 %pad_maximum_fusion.1 = bf16[2,1024,4,128]{3,2,1,0:T(4,128)(2,1)S(1)} fusion(bf16[2,1024,1,128]{3,2,1,0:T(2,128)(2,1)S(1)} %copy.34, bf16[2,1024,1,128]{3,2,1,0:T(2,128)(2,1)S(1)} %copy.33, bf16[2,1024,1,128]{3,2,1,0:T(2,128)(2,1)S(1)} %copy.32, bf16[2,1024,1,128]{3,2,1,0:T(2,128)(2,1)S(1)} %copy.31), kind=kLoop, calls=%fused_computation.4 | loop fusion | flops 8388608 | bytes 4194304 | tf_op jit(solution)/shard_map/stack | solution.py:175
  470.7 2.0 slice_bitcast_fusion.8
  (24 shorter events, 0.2 us)
Async XLA Ops:
  7.2 37.2 %all-gather.5.cloned.1.call-start = ((), (), s32[]{:S(2)}) async-start(), calls=%async_computation.4 | async-start | bytes 4718592 | tf_op jit(solution)/shard_map/all_gather | solution.py:127
  9.2 3.7 copy-start.12
  10.6 120.2 %all-gather.7.cloned.1.call-start = ((), (), s32[]{:S(2)}) async-start(), calls=%async_computation.5 | async-start | bytes 4718592 | tf_op jit(solution)/shard_map/all_gather | solution.py:127
  11.4 206.1 %all-gather.9.cloned.1.call-start = ((), (), s32[]{:S(2)}) async-start(), calls=%async_computation.6 | async-start | bytes 4718592 | tf_op jit(solution)/shard_map/all_gather | solution.py:127
  12.1 292.1 %all-gather.11.cloned.1.call-start = ((), (), s32[]{:S(2)}) async-start(), calls=%async_computation.7 | async-start | bytes 4718592 | tf_op jit(solution)/shard_map/all_gather | solution.py:127
  12.7 387.0 %reduce-scatter.5.cloned.1.call-start = ((), (), s32[]{:S(2)}) async-start(), calls=%async_computation.8 | async-start | bytes 9437184 | tf_op jit(solution)/shard_map/reduce_scatter | solution.py:173
  44.3 4.8 copy-start.5
  44.3 4.8 copy-start.6
  129.5 1.2 copy-start.7
  130.7 271.1 %reduce-scatter.7.cloned.1.call-start = ((), (), s32[]{:S(2)}) async-start(), calls=%async_computation.9 | async-start | bytes 9437184 | tf_op jit(solution)/shard_map/reduce_scatter | solution.py:173
  130.8 5.0 %copy-start.3 = (bf16[7,1024,128]{2,1,0:T(8,128)(2,1)S(1)}, bf16[7,1024,128]{2,1,0:T(8,128)(2,1)}, u32[]{:S(2)}) copy-start(bf16[7,1024,128]{2,1,0:T(8,128)(2,1)} %get-tuple-element.22.refs_2_) | copy-start | bytes 5505028
  130.8 5.0 %copy-start.4 = (bf16[7,1024,128]{2,1,0:T(8,128)(2,1)S(1)}, bf16[7,1024,128]{2,1,0:T(8,128)(2,1)}, u32[]{:S(2)}) copy-start(bf16[7,1024,128]{2,1,0:T(8,128)(2,1)} %get-tuple-element.47.refs_1_) | copy-start | bytes 5505028
  216.1 1.3 copy-start.9
  217.4 186.6 %reduce-scatter.9.cloned.1.call-start = ((), (), s32[]{:S(2)}) async-start(), calls=%async_computation.10 | async-start | bytes 9437184 | tf_op jit(solution)/shard_map/reduce_scatter | solution.py:173
  217.5 5.0 %copy-start.1 = (bf16[7,1024,128]{2,1,0:T(8,128)(2,1)S(1)}, bf16[7,1024,128]{2,1,0:T(8,128)(2,1)}, u32[]{:S(2)}) copy-start(bf16[7,1024,128]{2,1,0:T(8,128)(2,1)} %get-tuple-element.21.refs_2_) | copy-start | bytes 5505028
  217.5 5.0 %copy-start.2 = (bf16[7,1024,128]{2,1,0:T(8,128)(2,1)S(1)}, bf16[7,1024,128]{2,1,0:T(8,128)(2,1)}, u32[]{:S(2)}) copy-start(bf16[7,1024,128]{2,1,0:T(8,128)(2,1)} %get-tuple-element.48.refs_1_) | copy-start | bytes 5505028
  302.9 1.3 copy-start.10
  304.2 159.5 %reduce-scatter.11.cloned.1.call-start = ((), (), s32[]{:S(2)}) async-start(), calls=%async_computation.11 | async-start | bytes 9437184 | tf_op jit(solution)/shard_map/reduce_scatter | solution.py:173
  304.2 5.0 %copy-start = (bf16[7,1024,128]{2,1,0:T(8,128)(2,1)S(1)}, bf16[7,1024,128]{2,1,0:T(8,128)(2,1)}, u32[]{:S(2)}) copy-start(bf16[7,1024,128]{2,1,0:T(8,128)(2,1)} %get-tuple-element.49.refs_1_) | copy-start | bytes 5505028
  390.6 1.2 copy-start.11
  391.8 1.5 copy-start.8
Sparse Core Ops, SparseCore 0:
  10.7 33.5 all-gather.4
  46.2 30.7 all-gather.6
  78.8 30.7 all-gather.8
  111.8 30.7 all-gather.10
  145.8 62.2 reduce-scatter.4
  217.5 66.8 reduce-scatter.6
  304.3 69.2 reduce-scatter.8
  391.9 71.6 reduce-scatter.10

commit v2 on v0

v2 whole, which is shorter than its diff:
```python
import functools
import math
import numpy as np
import jax
import jax.numpy as jnp
from jax import lax
from jax.experimental import pallas as pl
from jax.experimental.pallas import tpu as pltpu
from jax.sharding import PartitionSpec as P

LOG2E = math.log2(math.e)
F32 = jnp.float32
BF16 = jnp.bfloat16
Q_TILE = 256
N_PART = 3


def task_table(n_ctx, peers):
    tables = []
    for rank in range(n_ctx):
        chip, core = rank // 2, rank % 2

        def ids(chip_id):
            devs = (2 * chip_id + core, 2 * chip_id + 1 - core)
            return [dev if half == 0 else 2 * n_ctx - 1 - dev for dev in devs for half in range(2)]

        rows = []
        keys = [piece for peer in peers for piece in ids(chip ^ peer)]
        for q_slot, q_id in enumerate(ids(chip)):
            todo = [(k_slot, 2 if k_id == q_id else 1) for k_slot, k_id in enumerate(keys) if k_id <= q_id]
            todo = todo or [(rows[-1][1] if rows else 0, 0)]
            for n, (k_slot, kind) in enumerate(todo):
                rows.append([q_slot, k_slot, kind, int(n == 0), int(n == len(todo) - 1)])
        tables.append(rows)
    n_step = max(len(rows) for rows in tables)
    for rows in tables:
        while len(rows) < n_step:
            rows.append([rows[-1][0], rows[-1][1], 3, 0, 0])
    return np.array(tables, np.int32)


def block_kernel(has_in, is_end, has_diag, tab_ref, q_ref, do_ref, aug_ref, k_ref, v_ref, *refs):
    if has_in:
        dqi_ref, *refs = refs
    dq_ref, dkv_ref, kt_scr, vt_scr, p_scr, ds_scr, *refs = refs
    dq_acc = refs[0] if is_end else dq_ref
    n_head, n_row, head_dim = q_ref.shape
    scaling = 1.0 / math.sqrt(head_dim)
    step = pl.program_id(0)
    k_slot = tab_ref[step, 1]
    kind = tab_ref[step, 2]
    is_first = tab_ref[step, 3]
    is_last = tab_ref[step, 4]
    n_sub = n_row // Q_TILE

    @pl.when(step == 0)
    def _():
        dkv_ref[...] = jnp.zeros_like(dkv_ref)
        row_id = lax.broadcasted_iota(jnp.int32, (head_dim, n_row), 0)
        kt_scr[head_dim:, :] = jnp.where(row_id < N_PART, -1.0, 0.0).astype(BF16)
        vt_scr[head_dim:, :] = jnp.where((row_id >= N_PART) & (row_id < 2 * N_PART), -1.0, 0.0).astype(BF16)

    def run_task(masked):
        kt_scr[:head_dim, :] = k_ref[...].T
        vt_scr[:head_dim, :] = v_ref[...].T
        fresh = is_first == 1

        def scores(h, sub, slot):
            rows = pl.ds(sub * Q_TILE, Q_TILE)
            n_key = n_row if not masked else (sub + 1) * Q_TILE
            aug = aug_ref[h, rows, :]
            s = jnp.dot(jnp.concatenate([q_ref[h, rows, :], aug], axis=1), kt_scr[:, :n_key], preferred_element_type=F32)
            dp = jnp.dot(jnp.concatenate([do_ref[h, rows, :], aug], axis=1), vt_scr[:, :n_key], preferred_element_type=F32)
            prob = jnp.exp2(s * (scaling * LOG2E))
            if masked:
                qi = lax.broadcasted_iota(jnp.int32, s.shape, 0) + sub * Q_TILE
                kj = lax.broadcasted_iota(jnp.int32, s.shape, 1)
                prob = jnp.where(qi >= kj, prob, 0.0)
            p_scr[slot, :, :n_key] = prob.astype(BF16)
            ds_scr[slot, :, :n_key] = (prob * dp).astype(BF16)

        def grads(h, sub, slot):
            rows = pl.ds(sub * Q_TILE, Q_TILE)
            n_key = n_row if not masked else (sub + 1) * Q_TILE
            prob = p_scr[slot, :, :n_key]
            ds = ds_scr[slot, :, :n_key]
            dkv_ref[1, k_slot, :, :n_key] += lax.dot_general(do_ref[h, rows, :], prob, (((0,), (0,)), ((), ())), preferred_element_type=F32)
            dkv_ref[0, k_slot, :, :n_key] += lax.dot_general(q_ref[h, rows, :], ds, (((0,), (0,)), ((), ())), preferred_element_type=F32)
            base = jnp.where(fresh, dqi_ref[h, :, rows] if has_in else 0.0, dq_acc[h, :, rows])
            dq_acc[h, :, rows] = base + lax.dot_general(kt_scr[:head_dim, :n_key], ds, (((1,), (1,)), ((), ())), preferred_element_type=F32)

        tiles = [(h, sub) for h in range(n_head) for sub in range(n_sub)]
        scores(*tiles[0], 0)
        for idx, tile in enumerate(tiles):
            if idx + 1 < len(tiles):
                scores(*tiles[idx + 1], (idx + 1) % 2)
            grads(*tile, idx % 2)

    @pl.when(kind == 1)
    def _():
        run_task(False)

    if has_diag:
        @pl.when(kind == 2)
        def _():
            run_task(True)
    else:
        @pl.when(kind == 0)
        def _():
            dq_acc[...] = dqi_ref[...] if has_in else jnp.zeros_like(dq_acc)

    if is_end:
        @pl.when(is_last == 1)
        def _():
            for h in range(n_head):
                dq_ref[h] = (dq_acc[h].T * scaling).astype(BF16)


def block_call(table, q, do, aug, kv, dq_in, is_end, has_diag, name):
    n_q, n_head, n_row, head_dim = q.shape
    n_key = kv.shape[1]
    n_step = table.shape[0]
    has_in = dq_in is not None
    q_spec = pl.BlockSpec((None, n_head, n_row, head_dim), lambda t, tab: (tab[t, 0], 0, 0, 0))
    qt_spec = pl.BlockSpec((None, n_head, head_dim, n_row), lambda t, tab: (tab[t, 0], 0, 0, 0))
    kv_specs = [pl.BlockSpec((None, None, n_row, head_dim), lambda t, tab, i=i: (i, tab[t, 1], 0, 0)) for i in range(2)]
    n_task = 8 * (n_key // 4)
    return pl.pallas_call(
        functools.partial(block_kernel, has_in, is_end, has_diag),
        grid_spec=pltpu.PrefetchScalarGridSpec(
            num_scalar_prefetch=1,
            grid=(n_step,),
            in_specs=[q_spec, q_spec, q_spec] + kv_specs + ([qt_spec] if has_in else []),
            out_specs=[q_spec if is_end else qt_spec, pl.BlockSpec((2, n_key, head_dim, n_row), lambda t, tab: (0, 0, 0, 0), pipeline_mode=pl.Buffered(1))],
            scratch_shapes=[
                pltpu.VMEM((2 * head_dim, n_row), BF16),
                pltpu.VMEM((2 * head_dim, n_row), BF16),
                pltpu.VMEM((2, Q_TILE, n_row), BF16),
                pltpu.VMEM((2, Q_TILE, n_row), BF16),
            ] + ([pltpu.VMEM((n_head, head_dim, n_row), F32)] if is_end else []),
        ),
        out_shape=[
            jax.ShapeDtypeStruct(q.shape, BF16) if is_end else jax.ShapeDtypeStruct((n_q, n_head, head_dim, n_row), F32),
            jax.ShapeDtypeStruct((2, n_key, head_dim, n_row), F32),
        ],
        compiler_params=pltpu.CompilerParams(dimension_semantics=('arbitrary',), vmem_limit_bytes=40 * 1024 * 1024),
        cost_estimate=pl.CostEstimate(flops=n_task * n_head * 10 * n_row * n_row * head_dim, bytes_accessed=16 * 1024 * 1024, transcendentals=n_task * n_head * n_row * n_row),
        name=name,
    )(table, q, do, aug, kv, kv, *([dq_in] if has_in else []))


def split_parts(x):
    parts = []
    for _ in range(N_PART):
        part = lax.reduce_precision(x, 8, 7)
        parts.append(part)
        x = x - part
    return parts


def solution(mesh):
    n_cx = mesh.shape['cx']
    n_ctx = mesh.shape['cy'] * n_cx
    ctx_axes = ('cy', 'cx')
    row_spec = P(('dp', 'cy', 'cx'), None, None)
    stat_spec = P(('dp', 'cy', 'cx'), None)

    def swap(x, bit):
        return lax.ppermute(x, ctx_axes, [(dev, dev ^ bit) for dev in range(n_ctx)])

    def local_grads(query_rows, key_rows, value_rows, out_rows, grad_out, log_sum_exp):
        tok_dev, n_heads, head_dim = query_rows.shape
        kv_heads = key_rows.shape[1]
        group_size = n_heads // kv_heads
        half_tok = tok_dev // 2
        scaling = 1.0 / math.sqrt(head_dim)
        n_grp = kv_heads // 2
        ctx_rank = lax.axis_index('cy') * n_cx + lax.axis_index('cx')
        core = ctx_rank % 2

        def pick(x, mine):
            sel = core if mine else 1 - core
            return lax.dynamic_slice_in_dim(x, sel * n_grp, n_grp, axis=0)

        def pieces_first(rows):
            return rows.reshape(2, half_tok, kv_heads, group_size, head_dim).transpose(2, 0, 3, 1, 4)

        kv_rows = jnp.stack([key_rows, value_rows]).reshape(2, 2, half_tok, kv_heads, head_dim).transpose(3, 0, 1, 2, 4)
        kv_mine, kv_send = pick(kv_rows, True), pick(kv_rows, False)
        kv_chip = [jnp.concatenate([kv_mine[g], swap(kv_send[g], 1)], axis=1) for g in range(n_grp)]

        q_pf, do_pf = pieces_first(query_rows), pieces_first(grad_out)
        delta = jnp.einsum('thd,thd->th', grad_out, out_rows, preferred_element_type=F32)
        stats = jnp.stack([log_sum_exp * math.sqrt(head_dim), delta])
        stats = stats.reshape(2, 2, half_tok, kv_heads, group_size).transpose(3, 0, 1, 4, 2)

        def chip_rows(x, g, axis=0):
            mine, send = pick(x, True)[g], pick(x, False)[g]
            return jnp.concatenate([mine, swap(send, 1)], axis=axis)

        tables = {name: jnp.asarray(task_table(n_ctx, peers))[ctx_rank] for name, peers in (('own', (0,)), ('far', (3,)), ('near', (1, 2)))}

        def far(g):
            return swap(kv_chip[g], 6)

        def near(g):
            return jnp.concatenate([swap(kv_chip[g], 2), swap(kv_chip[g], 4)], axis=1)

        dq_out, dkv_out = [], []
        kv_far = [far(g) for g in range(n_grp)]
        kv_near = [near(g) for g in range(n_grp)]
        for g in range(n_grp):
            q, do, st = chip_rows(q_pf, g), chip_rows(do_pf, g), chip_rows(stats, g, axis=1)
            parts = jnp.stack(split_parts(st[0]) + split_parts(st[1]), axis=-1).astype(BF16)
            aug = jnp.pad(parts, ((0, 0), (0, 0), (0, 0), (0, 128 - 2 * N_PART)))
            run = functools.partial
            own = lambda dq_in, is_end: block_call(tables['own'], q, do, aug, kv_chip[g], dq_in, is_end, True, 'own_grads')
            farther = lambda dq_in: block_call(tables['far'], q, do, aug, kv_far[g], dq_in, False, False, 'far_grads')
            nearer = lambda dq_in, is_end: block_call(tables['near'], q, do, aug, kv_near[g], dq_in, is_end, False, 'near_grads')
            last = g == n_grp - 1
            dq = None
            if not last:
                dq, dkv_own = own(dq, False)
            dq, dkv_far = farther(dq)
            dq, dkv_near = nearer(dq, not last)
            if last:
                dq, dkv_own = own(dq, True)
            dkv_x, dkv_y = dkv_near[:, :4], dkv_near[:, 4:]
            dkv = dkv_own + swap(dkv_far, 6) + swap(dkv_x, 2) + swap(dkv_y, 4)
            dkv = jnp.stack([dkv[0] * scaling, dkv[1]]).astype(BF16)
            dq_home = jnp.stack([dq[:2], swap(dq[2:], 1)])
            dkv_home = jnp.stack([dkv[:, :2], swap(dkv[:, 2:], 1)])
            dq_out.append(dq_home)
            dkv_out.append(dkv_home)

        def by_core(x):
            return jnp.where(core == 0, x, x[::-1])

        dq_all = by_core(jnp.stack(dq_out, axis=1))
        grad_query = dq_all.transpose(2, 4, 0, 1, 3, 5).reshape(tok_dev, n_heads, head_dim)
        dkv_all = by_core(jnp.stack(dkv_out, axis=1))
        grad_kv = dkv_all.transpose(2, 3, 5, 0, 1, 4).reshape(2, tok_dev, kv_heads, head_dim)
        return grad_query, grad_kv[0], grad_kv[1]

    return jax.shard_map(local_grads, mesh=mesh, in_specs=(row_spec, row_spec, row_spec, row_spec, row_spec, stat_spec), out_specs=(row_spec, row_spec, row_spec), check_vma=False)
```

time: 1840 us -> 760 us (0.41)
  matrix products: 997 us -> 0 us
  waiting for transfers between devices: 519 us -> 169 us
  Pallas kernels: 0 us -> 319 us
  other arithmetic: 178 us -> 96.3 us
  local copies, waits for them, and re-layouts: 104 us -> 150 us
  loops' own time: 27.8 us -> 0 us
    dot_general x40 -> x0, matrix products: 997 us -> none  [the longest x8 303 us: block_grads(): jnp.einsum('qkgd,skd->kqgs', do_blk, v_blk, preferred_element_type=jnp.fl...]
    ppermute x30 -> x24, waiting for transfers between devices: 519 us -> 169 us  [swap(): return lax.ppermute(x, ctx_axes, [(dev, dev ^ bit) for dev in range(n_ctx)])]
    pallas_call x0 -> x6, Pallas kernels: none -> 319 us  [block_call(): pl.pallas_call(functools.partial(block_kernel, has_in, is_end, has_diag),...]
    add x22 -> x2, other arithmetic: 156 us -> 7.78 us  [local_grads(): dkv = dkv_own + swap(dkv_far, 6) + swap(dkv_x, 2) + swap(dkv_y, 4)]
    concatenate x7 -> x0, local copies, waits for them, and re-layouts: 69.7 us -> none  [src_after(): return (jnp.concatenate([zero_pad, dq_part], axis=1), dk_part, dv_part)]
    another operation x0 -> x13, local copies, waits for them, and re-layouts: none -> 65 us  [the longest x2 42.7 us: local_grads(): jnp.stack(split_parts(st[0]) + split_parts(st[1]), axis=-1).astype(BF16)]
    another operation x0 -> x17, other arithmetic: none -> 55.2 us
    while x32 -> x0, local copies, waits for them, and re-layouts: 32.1 us -> none
  transfers between devices with their start and end apart: 30 -> 24, of which waited for: 15 -> 3; matrix products, arithmetic and copies ran while one was open for 56% -> 29% of each run, Pallas kernels for 0% -> 42%
where the time goes in v2:
time: 760 us; the launch traced here: 754 us
  Pallas kernels  319 us (42%)
  waiting for transfers between devices  169 us (22%)
  local copies, waits for them, and re-layouts  150 us (20%)
  other arithmetic  96.3 us (13%)
  starting transfers between devices  18.3 us (2%)
    pallas_call x6, Pallas kernels, block_call(): pl.pallas_call(functools.partial(block_kernel, has_in, is_end, has_diag),...  319 us
    ppermute x24, waiting for transfers between devices, swap(): return lax.ppermute(x, ctx_axes, [(dev, dev ^ bit) for dev in range(n_ctx)])  169 us
    another operation x9, other arithmetic  42.8 us
    another operation x2, local copies, waits for them, and re-layouts, local_grads(): jnp.stack(split_parts(st[0]) + split_parts(st[1]), axis=-1).astype(BF16)  42.7 us
    reduce_precision x4, local copies, waits for them, and re-layouts, split_parts(): part = lax.reduce_precision(x, 8, 7)  18.5 us
    another operation x6, local copies, waits for them, and re-layouts  18.5 us
    ppermute x24, starting transfers between devices, swap(): return lax.ppermute(x, ctx_axes, [(dev, dev ^ bit) for dev in range(n_ctx)])  18.3 us
  transfers between devices with their start and end apart: 24, of which 3 were waited for; matrix products, arithmetic and copies ran while one was open for 29% of the time, Pallas kernels for 42%

profile of v2, /device:TPU:0, one launch (start us, length us, event | category | flops | bytes accessed | tf_op | source)
XLA Modules:
  0.0 753.6 jit_solution(666769445306937866)
XLA Ops:
  1.7 9.0 %fusion = f32[1024,28]{0,1:T(8,128)S(1)} fusion(bf16[1024,28,128]{2,0,1:T(8,128)(2,1)} %param.13, bf16[1024,28,128]{2,0,1:T(8,128)(2,1)} %param.12), kind=kLoop, calls=%fused_computation.1 | loop fusion | flops 14651392 | bytes 14794752 | tf_op jit(solution)/shard_map/thd,thd->th/dot_general | solution.py:193
  12.4 6.3 constant_dynamic-slice_fusion.2
  19.1 2.2 slice_bitcast_fusion.6
  22.3 2.2 slice_bitcast_fusion.4
  26.8 1.6 slice_bitcast_fusion.7
  28.8 2.2 slice_bitcast_fusion.5
  33.4 1.6 fusion.27
  35.0 5.0 copy.201
  40.1 5.1 copy.202
  45.2 5.0 copy.205
  50.2 1.5 fusion.23
  51.7 5.1 copy.204
  56.8 4.2 copy.214
  61.0 4.2 copy.215
  65.2 10.2 %fusion.2 = (bf16[4,7,512,1]{3,2,1,0:T(8,128)(2,1)}, bf16[4,7,512,1]{3,2,1,0:T(8,128)(2,1)}) fusion(f32[4,7,512,1]{3,2,1,0:T(8,128)} %copy.201, f32[4,7,512,1]{3,2,1,0:T(8,128)} %copy.202), kind=kLoop, calls=%fused_computation.12 | loop fusion | flops 86016 | bytes 172032 | tf_op jit(solution)/shard_map/convert.14
  75.4 10.3 %fusion.4 = (bf16[4,7,512,1]{3,2,1,0:T(8,128)(2,1)}, bf16[4,7,512,1]{3,2,1,0:T(8,128)(2,1)}) fusion(f32[4,7,512,1]{3,2,1,0:T(8,128)} %copy.204, f32[4,7,512,1]{3,2,1,0:T(8,128)} %copy.205), kind=kLoop, calls=%fused_computation.14 | loop fusion | flops 86016 | bytes 172032 | tf_op jit(solution)/shard_map/convert.17
  85.7 2.1 pad_maximum_fusion.8.k_ref.v_ref
  87.8 3.0 collective-permute-start.4
  90.8 10.2 %fusion.6 = (bf16[4,7,512,1]{3,2,1,0:T(8,128)(2,1)}, bf16[4,7,512,1]{3,2,1,0:T(8,128)(2,1)}) fusion(f32[4,7,512,1]{3,2,1,0:T(8,128)} %copy.214, f32[4,7,512,1]{3,2,1,0:T(8,128)} %copy.215), kind=kLoop, calls=%fused_computation.16 | loop fusion | flops 86016 | bytes 172032 | tf_op jit(solution)/shard_map/convert.8
  101.0 1.5 collective-permute-start.5
  104.3 10.6 %collective-permute-done.4 = bf16[2,4,512,128]{3,2,1,0:T(8,128)(2,1)} collective-permute-done((bf16[2,4,512,128]{3,2,1,0:T(8,128)(2,1)}, bf16[2,4,512,128]{3,2,1,0:T(8,128)(2,1)}, u32[]{:S(2)}, u32[]{:S(2)}) %collective-permute-start.4) | collective-permute-done | bytes 1048608 | tf_op jit(solution)/shard_map/ppermute | solution.py:169
  114.8 2.1 collective-permute-start.13
  116.9 3.0 copy.206
  119.9 3.1 copy.207
  123.1 4.2 copy.218
  127.3 4.2 copy.217
  131.5 3.0 copy.219
  134.5 3.0 copy.220
  137.5 21.6 %stack.105 = bf16[4,7,512,6]{3,2,1,0:T(8,128)(2,1)} concatenate(bf16[4,7,512,1]{3,2,1,0:T(8,128)(2,1)} %copy.206, bf16[4,7,512,1]{3,2,1,0:T(8,128)(2,1)} %get-tuple-element.59, bf16[4,7,512,1]{3,2,1,0:T(8,128)(2,1)} %get-tuple-element.58, bf16[4,7,512,1]{3,2,1,0:T(8,128)(2,1)} %copy.207, bf16[4,7,512,1]{3,2,1,0:T(8,128)(2,1)} %get-tuple-element.57, ...), dimensions={3} | concatenate | bytes 344064 | tf_op jit(solution)/shard_map/stack | solution.py:214
  159.1 4.8 pad.7.aug_ref
  163.9 10.2 %fusion.8 = (bf16[4,7,512,1]{3,2,1,0:T(8,128)(2,1)}, bf16[4,7,512,1]{3,2,1,0:T(8,128)(2,1)}) fusion(f32[4,7,512,1]{3,2,1,0:T(8,128)} %copy.217, f32[4,7,512,1]{3,2,1,0:T(8,128)} %copy.218), kind=kLoop, calls=%fused_computation.18 | loop fusion | flops 86016 | bytes 172032 | tf_op jit(solution)/shard_map/convert.11
  174.2 21.1 %stack.113 = bf16[4,7,512,6]{3,2,1,0:T(8,128)(2,1)} concatenate(bf16[4,7,512,1]{3,2,1,0:T(8,128)(2,1)} %copy.219, bf16[4,7,512,1]{3,2,1,0:T(8,128)(2,1)} %get-tuple-element.63, bf16[4,7,512,1]{3,2,1,0:T(8,128)(2,1)} %get-tuple-element.62, bf16[4,7,512,1]{3,2,1,0:T(8,128)(2,1)} %copy.220, bf16[4,7,512,1]{3,2,1,0:T(8,128)(2,1)} %get-tuple-element.61, ...), dimensions={3} | concatenate | bytes 344064 | tf_op jit(solution)/shard_map/stack | solution.py:214
  195.3 4.9 pad.8.aug_ref
  200.2 1.7 pad_maximum_fusion.5.k_ref.v_ref
  203.9 3.1 pad_maximum_fusion.6.k_ref.v_ref
  207.1 1.5 collective-permute-start.14
  208.6 1.9 pad_maximum_fusion.1.q_ref
  210.6 2.0 pad_maximum_fusion.2.do_ref
  213.2 42.0 %own_grads.2 = (f32[4,7,128,512]{3,2,1,0:T(8,128)}, f32[2,4,128,512]{3,2,1,0:T(8,128)S(1)}) custom-call(s32[10,5]{1,0:T(8,128)S(1)} %copy.210.tab_ref, bf16[4,7,512,128]{3,2,1,0:T(8,128)(2,1)S(1)} %pad_maximum_fusion.1.q_ref, bf16[4,7,512,128]{3,2,1,0:T(8,128)(2,1)S(1)} %pad_maximum_fusion.2.do_ref, bf16[4,7,512,128]{3,2,1,0:T(8,128)(2,1)S(1)} %copy-done.3, ...), custom_call_target="tpu_custom_call" | custom-call | flops 18790481920 | bytes 16777216 | tf_op jit(solution)/shard_map/own_grads/pallas_call | solution.py:128
  255.2 41.3 %far_grads.2 = (f32[4,7,128,512]{3,2,1,0:T(8,128)}, f32[2,4,128,512]{3,2,1,0:T(8,128)}) custom-call(s32[10,5]{1,0:T(8,128)S(1)} %copy.211.tab_ref, bf16[4,7,512,128]{3,2,1,0:T(8,128)(2,1)S(1)} %pad_maximum_fusion.1.q_ref, bf16[4,7,512,128]{3,2,1,0:T(8,128)(2,1)S(1)} %pad_maximum_fusion.2.do_ref, bf16[4,7,512,128]{3,2,1,0:T(8,128)(2,1)S(1)} %copy-done.3, ...), custom_call_target="tpu_custom_call" | custom-call | flops 18790481920 | bytes 16777216 | tf_op jit(solution)/shard_map/far_grads/pallas_call | solution.py:128
  296.6 2.0 copy-done.1
  298.6 76.3 %near_grads.2 = (bf16[4,7,512,128]{3,2,1,0:T(8,128)(2,1)S(1)}, f32[2,8,128,512]{3,2,1,0:T(8,128)}) custom-call(s32[18,5]{1,0:T(8,128)S(1)} %copy.212.tab_ref, bf16[4,7,512,128]{3,2,1,0:T(8,128)(2,1)S(1)} %pad_maximum_fusion.1.q_ref, bf16[4,7,512,128]{3,2,1,0:T(8,128)(2,1)S(1)} %copy-done.1, bf16[4,7,512,128]{3,2,1,0:T(8,128)(2,1)} %pad.7.aug_ref, ...), custom_call_target="tpu_custom_call" | custom-call | flops 37580963840 | bytes 16777216 | tf_op jit(solution)/shard_map/near_grads/pallas_call | solution.py:128
  374.9 5.0 fusion.31
  380.1 2.0 pad_maximum_fusion.4.do_ref
  382.2 2.0 pad_maximum_fusion.3.q_ref
  384.8 39.1 %far_grads.3 = (f32[4,7,128,512]{3,2,1,0:T(8,128)}, f32[2,4,128,512]{3,2,1,0:T(8,128)}) custom-call(s32[10,5]{1,0:T(8,128)S(1)} %copy.211.tab_ref, bf16[4,7,512,128]{3,2,1,0:T(8,128)(2,1)S(1)} %pad_maximum_fusion.3.q_ref, bf16[4,7,512,128]{3,2,1,0:T(8,128)(2,1)S(1)} %pad_maximum_fusion.4.do_ref, bf16[4,7,512,128]{3,2,1,0:T(8,128)(2,1)S(1)} %copy-done.2, ...), custom_call_target="tpu_custom_call" | custom-call | flops 18790481920 | bytes 16777216 | tf_op jit(solution)/shard_map/far_grads/pallas_call | solution.py:128
  423.9 76.2 %near_grads.3 = (f32[4,7,128,512]{3,2,1,0:T(8,128)}, f32[2,8,128,512]{3,2,1,0:T(8,128)}) custom-call(s32[18,5]{1,0:T(8,128)S(1)} %copy.212.tab_ref, bf16[4,7,512,128]{3,2,1,0:T(8,128)(2,1)S(1)} %pad_maximum_fusion.3.q_ref, bf16[4,7,512,128]{3,2,1,0:T(8,128)(2,1)S(1)} %pad_maximum_fusion.4.do_ref, bf16[4,7,512,128]{3,2,1,0:T(8,128)(2,1)S(1)} %copy-done.2, ...), custom_call_target="tpu_custom_call" | custom-call | flops 37580963840 | bytes 16777216 | tf_op jit(solution)/shard_map/near_grads/pallas_call | solution.py:128
  500.0 43.7 %own_grads.3 = (bf16[4,7,512,128]{3,2,1,0:T(8,128)(2,1)S(1)}, f32[2,4,128,512]{3,2,1,0:T(8,128)S(1)}) custom-call(s32[10,5]{1,0:T(8,128)S(1)} %copy.210.tab_ref, bf16[4,7,512,128]{3,2,1,0:T(8,128)(2,1)S(1)} %pad_maximum_fusion.3.q_ref, bf16[4,7,512,128]{3,2,1,0:T(8,128)(2,1)S(1)} %pad_maximum_fusion.4.do_ref, bf16[4,7,512,128]{3,2,1,0:T(8,128)(2,1)} %pad.8.aug_ref, ...), custom_call_target="tpu_custom_call" | custom-call | flops 18790481920 | bytes 16777216 | tf_op jit(solution)/shard_map/own_grads/pallas_call | solution.py:128
  543.8 1.9 slice_bitcast_fusion.9
  545.7 1.6 slice_bitcast_fusion.8
  548.6 2.5 fusion.32
  551.1 2.8 collective-permute-start.21
  553.9 1.5 collective-permute-start.20
  555.4 4.3 maximum_bitcast_fusion
  559.7 3.7 maximum_bitcast_fusion.1
  563.4 3.8 pad_maximum_fusion
  567.2 74.4 %collective-permute-done.18 = f32[2,4,128,512]{3,2,1,0:T(8,128)} collective-permute-done((f32[2,4,128,512]{3,2,1,0:T(8,128)}, f32[2,4,128,512]{3,2,1,0:T(8,128)}, u32[]{:S(2)}, u32[]{:S(2)}) %collective-permute-start.18) | collective-permute-done | bytes 2097184 | tf_op jit(solution)/shard_map/ppermute | solution.py:169
  641.6 3.9 add_add_fusion.1
  645.7 84.3 %collective-permute-done.22 = f32[2,4,128,512]{3,2,1,0:T(8,128)} collective-permute-done((f32[2,4,128,512]{3,2,1,0:T(8,128)}, f32[2,4,128,512]{3,2,1,0:T(8,128)}, u32[]{:S(2)}, u32[]{:S(2)}) %collective-permute-start.22) | collective-permute-done | bytes 2097184 | tf_op jit(solution)/shard_map/ppermute | solution.py:169
  730.0 3.9 add_add_fusion
  734.9 5.4 fusion.9
  740.2 7.0 copy.224
  749.0 1.8 copy.227
  751.4 1.8 copy.228
  (122 shorter events, 19.1 us)
Async XLA Ops:
  11.5 21.9 %collective-permute-start.10 = (f32[2,2,7,512]{3,1,2,0:T(2,128)}, f32[2,2,7,512]{3,1,2,0:T(2,128)}, u32[]{:S(2)}, u32[]{:S(2)}) collective-permute-start(f32[2,2,7,512]{3,1,2,0:T(2,128)} %get-tuple-element.103), channel_id=1, source_target_pairs={{0,1},{1,0},{2,3},{3,2},{4,5},{5,4},{6,7},{7,6}} | collective-permute-start | bytes 172040 | tf_op jit(solution)/shard_map/ppermute | solution.py:169
  12.4 21.0 %collective-permute-start.2 = (f32[2,2,7,512]{3,1,2,0:T(2,128)}, f32[2,2,7,512]{3,1,2,0:T(2,128)}, u32[]{:S(2)}, u32[]{:S(2)}) collective-permute-start(f32[2,2,7,512]{3,1,2,0:T(2,128)} %get-tuple-element.102), channel_id=1, source_target_pairs={{0,1},{1,0},{2,3},{3,2},{4,5},{5,4},{6,7},{7,6}} | collective-permute-start | bytes 172040 | tf_op jit(solution)/shard_map/ppermute | solution.py:169
  21.3 185.8 %collective-permute-start = (bf16[2,7,512,128]{3,2,1,0:T(8,128)(2,1)}, bf16[2,7,512,128]{3,2,1,0:T(8,128)(2,1)}, u32[]{:S(2)}, u32[]{:S(2)}) collective-permute-start(bf16[2,7,512,128]{3,2,1,0:T(8,128)(2,1)} %get-tuple-element.80), channel_id=1, source_target_pairs={{0,1},{1,0},{2,3},{3,2},{4,5},{5,4},{6,7},{7,6}} | collective-permute-start | bytes 5505032 | tf_op jit(solution)/shard_map/ppermute | solution.py:169
  22.2 2.3 copy-start.13
  22.2 2.4 copy-start.14
  24.5 186.1 %collective-permute-start.1 = (bf16[2,7,512,128]{3,2,1,0:T(8,128)(2,1)}, bf16[2,7,512,128]{3,2,1,0:T(8,128)(2,1)}, u32[]{:S(2)}, u32[]{:S(2)}) collective-permute-start(bf16[2,7,512,128]{3,2,1,0:T(8,128)(2,1)} %get-tuple-element.76), channel_id=1, source_target_pairs={{0,1},{1,0},{2,3},{3,2},{4,5},{5,4},{6,7},{7,6}} | collective-permute-start | bytes 5505032 | tf_op jit(solution)/shard_map/ppermute | solution.py:169
  25.9 59.9 %collective-permute-start.3 = (bf16[2,2,512,128]{3,2,1,0:T(8,128)(2,1)}, bf16[2,2,512,128]{3,2,1,0:T(8,128)(2,1)}, u32[]{:S(2)}, u32[]{:S(2)}) collective-permute-start(bf16[2,2,512,128]{3,2,1,0:T(8,128)(2,1)} %get-tuple-element.94), channel_id=1, source_target_pairs={{0,1},{1,0},{2,3},{3,2},{4,5},{5,4},{6,7},{7,6}} | collective-permute-start | bytes 1572872 | tf_op jit(solution)/shard_map/ppermute | solution.py:169
  33.4 69.1 %collective-permute-start.11 = (bf16[2,2,512,128]{3,2,1,0:T(8,128)(2,1)S(1)}, bf16[2,2,512,128]{3,2,1,0:T(8,128)(2,1)}, u32[]{:S(2)}, u32[]{:S(2)}) collective-permute-start(bf16[2,2,512,128]{3,2,1,0:T(8,128)(2,1)S(1)} %get-tuple-element.95), channel_id=1, source_target_pairs={{0,1},{1,0},{2,3},{3,2},{4,5},{5,4},{6,7},{7,6}} | collective-permute-start | bytes 1572872 | tf_op jit(solution)/shard_map/ppermute | solution.py:169
  51.6 5.1 copy-start.15
  56.8 4.2 copy-start.18
  87.8 13.2 %copy-start.16 = (f32[1,4,7,512]{3,1,2,0:T(4,128)S(1)}, f32[1,4,7,512]{3,1,2,0:T(4,128)}, u32[]{:S(2)}) copy-start(f32[1,4,7,512]{3,1,2,0:T(4,128)} %get-tuple-element.99) | copy-start | bytes 172036
  87.8 27.0 %collective-permute-start.4 = (bf16[2,4,512,128]{3,2,1,0:T(8,128)(2,1)}, bf16[2,4,512,128]{3,2,1,0:T(8,128)(2,1)}, u32[]{:S(2)}, u32[]{:S(2)}) collective-permute-start(bf16[2,4,512,128]{3,2,1,0:T(8,128)(2,1)} %pad_maximum_fusion.8.k_ref.v_ref), channel_id=1, source_target_pairs={{0,2},{1,3},{2,0},{3,1},{4,6},{5,7},{6,4},{7,5}} | collective-permute-start | bytes 3145736 | tf_op jit(solution)/shard_map/ppermute | solution.py:169
  101.0 18.9 %copy-start.21 = (bf16[4,7,512,1]{2,0,3,1:T(4,128)(2,1)S(1)}, bf16[4,7,512,1]{2,0,3,1:T(4,128)(2,1)}, u32[]{:S(2)}) copy-start(bf16[4,7,512,1]{2,0,3,1:T(4,128)(2,1)} %get-tuple-element.48) | copy-start | bytes 86020
  101.0 99.2 %collective-permute-start.5 = (bf16[2,4,512,128]{3,2,1,0:T(8,128)(2,1)}, bf16[2,4,512,128]{3,2,1,0:T(8,128)(2,1)}, u32[]{:S(2)}, u32[]{:S(2)}) collective-permute-start(bf16[2,4,512,128]{3,2,1,0:T(8,128)(2,1)} %pad_maximum_fusion.8.k_ref.v_ref), channel_id=1, source_target_pairs={{0,4},{1,5},{2,6},{3,7},{4,0},{5,1},{6,2},{7,3}} | collective-permute-start | bytes 3145736 | tf_op jit(solution)/shard_map/ppermute | solution.py:169
  103.7 98.3 %collective-permute-start.12 = (bf16[2,4,512,128]{3,2,1,0:T(8,128)(2,1)S(1)}, bf16[2,4,512,128]{3,2,1,0:T(8,128)(2,1)}, u32[]{:S(2)}, u32[]{:S(2)}) collective-permute-start(bf16[2,4,512,128]{3,2,1,0:T(8,128)(2,1)S(1)} %pad_maximum_fusion.9.k_ref.v_ref), channel_id=1, source_target_pairs={{0,2},{1,3},{2,0},{3,1},{4,6},{5,7},{6,4},{7,5}} | collective-permute-start | bytes 3145736 | tf_op jit(solution)/shard_map/ppermute | solution.py:169
  114.8 87.7 %collective-permute-start.13 = (bf16[2,4,512,128]{3,2,1,0:T(8,128)(2,1)S(1)}, bf16[2,4,512,128]{3,2,1,0:T(8,128)(2,1)}, u32[]{:S(2)}, u32[]{:S(2)}) collective-permute-start(bf16[2,4,512,128]{3,2,1,0:T(8,128)(2,1)S(1)} %pad_maximum_fusion.9.k_ref.v_ref), channel_id=1, source_target_pairs={{0,4},{1,5},{2,6},{3,7},{4,0},{5,1},{6,2},{7,3}} | collective-permute-start | bytes 3145736 | tf_op jit(solution)/shard_map/ppermute | solution.py:169
  116.9 6.2 copy-start.17
  123.1 4.2 copy-start.19
  131.5 3.0 copy-start.20
  195.3 5.0 copy-start.12
  200.2 179.9 %collective-permute-start.9 = (bf16[2,7,512,128]{3,2,1,0:T(8,128)(2,1)S(1)}, bf16[2,7,512,128]{3,2,1,0:T(8,128)(2,1)}, u32[]{:S(2)}, u32[]{:S(2)}) collective-permute-start(bf16[2,7,512,128]{3,2,1,0:T(8,128)(2,1)S(1)} %copy-done.12), channel_id=1, source_target_pairs={{0,1},{1,0},{2,3},{3,2},{4,5},{5,4},{6,7},{7,6}} | collective-permute-start | bytes 5505032 | tf_op jit(solution)/shard_map/ppermute | solution.py:169
  202.0 180.1 %collective-permute-start.8 = (bf16[2,7,512,128]{3,2,1,0:T(8,128)(2,1)}, bf16[2,7,512,128]{3,2,1,0:T(8,128)(2,1)}, u32[]{:S(2)}, u32[]{:S(2)}) collective-permute-start(bf16[2,7,512,128]{3,2,1,0:T(8,128)(2,1)} %get-tuple-element.81), channel_id=1, source_target_pairs={{0,1},{1,0},{2,3},{3,2},{4,5},{5,4},{6,7},{7,6}} | collective-permute-start | bytes 5505032 | tf_op jit(solution)/shard_map/ppermute | solution.py:169
  202.5 52.7 %collective-permute-start.6 = (bf16[2,4,512,128]{3,2,1,0:T(8,128)(2,1)}, bf16[2,4,512,128]{3,2,1,0:T(8,128)(2,1)S(1)}, u32[]{:S(2)}, u32[]{:S(2)}) collective-permute-start(bf16[2,4,512,128]{3,2,1,0:T(8,128)(2,1)} %pad_maximum_fusion.8.k_ref.v_ref), channel_id=1, source_target_pairs={{0,6},{1,7},{2,4},{3,5},{4,2},{5,3},{6,0},{7,1}} | collective-permute-start | bytes 3145736 | tf_op jit(solution)/shard_map/ppermute | solution.py:169
  207.1 177.1 %collective-permute-start.14 = (bf16[2,4,512,128]{3,2,1,0:T(8,128)(2,1)S(1)}, bf16[2,4,512,128]{3,2,1,0:T(8,128)(2,1)}, u32[]{:S(2)}, u32[]{:S(2)}) collective-permute-start(bf16[2,4,512,128]{3,2,1,0:T(8,128)(2,1)S(1)} %pad_maximum_fusion.9.k_ref.v_ref), channel_id=1, source_target_pairs={{0,6},{1,7},{2,4},{3,5},{4,2},{5,3},{6,0},{7,1}} | collective-permute-start | bytes 3145736 | tf_op jit(solution)/shard_map/ppermute | solution.py:169
  208.6 2.1 copy-start.9
  210.6 2.6 copy-start.3
  213.2 42.0 %copy-start = (bf16[4,7,512,128]{3,2,1,0:T(8,128)(2,1)}, bf16[4,7,512,128]{3,2,1,0:T(8,128)(2,1)S(1)}, u32[]{:S(2)}) copy-start(bf16[4,7,512,128]{3,2,1,0:T(8,128)(2,1)S(1)} %pad_maximum_fusion.2.do_ref) | copy-start | bytes 11010052
  296.6 2.0 copy-start.1
  374.9 5.2 copy-start.8
  379.9 174.0 %collective-permute-start.17 = (f32[2,4,128,512]{3,2,1,0:T(8,128)}, f32[2,4,128,512]{3,2,1,0:T(8,128)}, u32[]{:S(2)}, u32[]{:S(2)}) collective-permute-start(f32[2,4,128,512]{3,2,1,0:T(8,128)} %get-tuple-element.68), channel_id=1, source_target_pairs={{0,2},{1,3},{2,0},{3,1},{4,6},{5,7},{6,4},{7,5}} | collective-permute-start | bytes 6291464 | tf_op jit(solution)/shard_map/ppermute | solution.py:169
  380.1 2.1 copy-start.7
  382.2 2.6 copy-start.2
  384.2 39.7 %copy-start.6 = (bf16[2,8,512,128]{3,2,1,0:T(8,128)(2,1)S(1)}, bf16[2,8,512,128]{3,2,1,0:T(8,128)(2,1)}, u32[]{:S(2)}) copy-start(bf16[2,8,512,128]{3,2,1,0:T(8,128)(2,1)} %pad_maximum_fusion.6.k_ref.v_ref) | copy-start | bytes 6291460
  543.8 1.9 copy-start.4
  545.7 5.4 collective-permute-start.7
  545.7 2.9 copy-start.11
  547.3 6.5 collective-permute-start.15
  547.9 93.7 %collective-permute-start.18 = (f32[2,4,128,512]{3,2,1,0:T(8,128)}, f32[2,4,128,512]{3,2,1,0:T(8,128)}, u32[]{:S(2)}, u32[]{:S(2)}) collective-permute-start(f32[2,4,128,512]{3,2,1,0:T(8,128)} %get-tuple-element.69), channel_id=1, source_target_pairs={{0,4},{1,5},{2,6},{3,7},{4,0},{5,1},{6,2},{7,3}} | collective-permute-start | bytes 6291464 | tf_op jit(solution)/shard_map/ppermute | solution.py:169
  547.9 93.7 %collective-permute-start.16 = (f32[2,4,128,512]{3,2,1,0:T(8,128)}, f32[2,4,128,512]{3,2,1,0:T(8,128)}, u32[]{:S(2)}, u32[]{:S(2)}) collective-permute-start(f32[2,4,128,512]{3,2,1,0:T(8,128)} %get-tuple-element.22), channel_id=1, source_target_pairs={{0,6},{1,7},{2,4},{3,5},{4,2},{5,3},{6,0},{7,1}} | collective-permute-start | bytes 6291464 | tf_op jit(solution)/shard_map/ppermute | solution.py:169
  551.1 94.6 %collective-permute-start.21 = (f32[2,4,128,512]{3,2,1,0:T(8,128)}, f32[2,4,128,512]{3,2,1,0:T(8,128)}, u32[]{:S(2)}, u32[]{:S(2)}) collective-permute-start(f32[2,4,128,512]{3,2,1,0:T(8,128)} %get-tuple-element.70), channel_id=1, source_target_pairs={{0,2},{1,3},{2,0},{3,1},{4,6},{5,7},{6,4},{7,5}} | collective-permute-start | bytes 6291464 | tf_op jit(solution)/shard_map/ppermute | solution.py:169
  553.9 176.1 %collective-permute-start.22 = (f32[2,4,128,512]{3,2,1,0:T(8,128)}, f32[2,4,128,512]{3,2,1,0:T(8,128)}, u32[]{:S(2)}, u32[]{:S(2)}) collective-permute-start(f32[2,4,128,512]{3,2,1,0:T(8,128)} %get-tuple-element.71), channel_id=1, source_target_pairs={{0,4},{1,5},{2,6},{3,7},{4,0},{5,1},{6,2},{7,3}} | collective-permute-start | bytes 6291464 | tf_op jit(solution)/shard_map/ppermute | solution.py:169
  553.9 176.1 %collective-permute-start.20 = (f32[2,4,128,512]{3,2,1,0:T(8,128)}, f32[2,4,128,512]{3,2,1,0:T(8,128)}, u32[]{:S(2)}, u32[]{:S(2)}) collective-permute-start(f32[2,4,128,512]{3,2,1,0:T(8,128)} %get-tuple-element.25), channel_id=1, source_target_pairs={{0,6},{1,7},{2,4},{3,5},{4,2},{5,3},{6,0},{7,1}} | collective-permute-start | bytes 6291464 | tf_op jit(solution)/shard_map/ppermute | solution.py:169
  555.4 4.3 copy-start.10
  645.5 84.5 %copy-start.5 = (f32[2,4,128,512]{3,2,1,0:T(8,128)S(1)}, f32[2,4,128,512]{3,2,1,0:T(8,128)}, u32[]{:S(2)}) copy-start(f32[2,4,128,512]{3,2,1,0:T(8,128)} %copy-done.4) | copy-start | bytes 6291460
  734.2 13.0 %collective-permute-start.19 = (bf16[2,2,128,512]{3,2,1,0:T(8,128)(2,1)S(1)}, bf16[2,2,128,512]{3,2,1,0:T(8,128)(2,1)S(1)}, u32[]{:S(2)}, u32[]{:S(2)}) collective-permute-start(bf16[2,2,128,512]{3,2,1,0:T(8,128)(2,1)S(1)} %get-tuple-element.89), channel_id=1, source_target_pairs={{0,1},{1,0},{2,3},{3,2},{4,5},{5,4},{6,7},{7,6}} | collective-permute-start | bytes 1572872 | tf_op jit(solution)/shard_map/ppermute | solution.py:169
  734.3 13.0 %collective-permute-start.23 = (bf16[2,2,128,512]{3,2,1,0:T(8,128)(2,1)S(1)}, bf16[2,2,128,512]{3,2,1,0:T(8,128)(2,1)S(1)}, u32[]{:S(2)}, u32[]{:S(2)}) collective-permute-start(bf16[2,2,128,512]{3,2,1,0:T(8,128)(2,1)S(1)} %get-tuple-element.91), channel_id=1, source_target_pairs={{0,1},{1,0},{2,3},{3,2},{4,5},{5,4},{6,7},{7,6}} | collective-permute-start | bytes 1572872 | tf_op jit(solution)/shard_map/ppermute | solution.py:169

commit v3 on v2

v3 whole, which is shorter than its diff:
```python
import functools
import math
import numpy as np
import jax
import jax.numpy as jnp
from jax import lax
from jax.experimental import pallas as pl
from jax.experimental.pallas import tpu as pltpu
from jax.sharding import PartitionSpec as P

LOG2E = math.log2(math.e)
F32 = jnp.float32
BF16 = jnp.bfloat16
Q_TILE = 256


def task_table(n_ctx, peers):
    tables = []
    for rank in range(n_ctx):
        chip, core = rank // 2, rank % 2

        def ids(chip_id):
            devs = (2 * chip_id + core, 2 * chip_id + 1 - core)
            return [dev if half == 0 else 2 * n_ctx - 1 - dev for dev in devs for half in range(2)]

        rows = []
        keys = [piece for peer in peers for piece in ids(chip ^ peer)]
        for q_slot, q_id in enumerate(ids(chip)):
            todo = [(k_slot, 2 if k_id == q_id else 1) for k_slot, k_id in enumerate(keys) if k_id <= q_id]
            todo = todo or [(rows[-1][1] if rows else 0, 0)]
            for n, (k_slot, kind) in enumerate(todo):
                rows.append([q_slot, k_slot, kind, int(n == 0), int(n == len(todo) - 1)])
        tables.append(rows)
    n_step = max(len(rows) for rows in tables)
    for rows in tables:
        while len(rows) < n_step:
            rows.append([rows[-1][0], rows[-1][1], 3, 0, 0])
    return np.array(tables, np.int32)


def block_kernel(has_in, is_end, has_diag, n_peer, tab_ref, q_ref, do_ref, lse_ref, delta_ref, k_ref, v_ref, *refs):
    if has_in:
        dqi_ref, *refs = refs
    dq_ref, *refs = refs
    dkv_refs, (dkv_acc, kt_scr, vt_scr, p_scr, ds_scr, out_sem, *refs) = refs[:n_peer], refs[n_peer:]
    dq_acc = refs[0] if is_end else dq_ref
    n_head, n_row, head_dim = q_ref.shape
    scaling = 1.0 / math.sqrt(head_dim)
    step = pl.program_id(0)
    k_slot = tab_ref[step, 1]
    kind = tab_ref[step, 2]
    is_first = tab_ref[step, 3]
    is_last = tab_ref[step, 4]
    n_sub = n_row // Q_TILE

    @pl.when(step == 0)
    def _():
        dkv_acc[...] = jnp.zeros_like(dkv_acc)

    def run_task(masked):
        kt_scr[...] = k_ref[...].T
        vt_scr[...] = v_ref[...].T
        fresh = is_first == 1

        def scores(h, sub, slot):
            rows = pl.ds(sub * Q_TILE, Q_TILE)
            n_key = n_row if not masked else (sub + 1) * Q_TILE
            s = jnp.dot(q_ref[h, rows, :], kt_scr[:, :n_key], preferred_element_type=F32)
            dp = jnp.dot(do_ref[h, rows, :], vt_scr[:, :n_key], preferred_element_type=F32)
            lse = jnp.tile(lse_ref[h, rows, :], (1, n_key // 128))
            dlt = jnp.tile(delta_ref[h, rows, :], (1, n_key // 128))
            prob = jnp.exp2(s * (scaling * LOG2E) - lse)
            if masked:
                qi = lax.broadcasted_iota(jnp.int32, s.shape, 0) + sub * Q_TILE
                kj = lax.broadcasted_iota(jnp.int32, s.shape, 1)
                prob = jnp.where(qi >= kj, prob, 0.0)
            p_scr[slot, :, :n_key] = prob.astype(BF16)
            ds_scr[slot, :, :n_key] = (prob * (dp - dlt)).astype(BF16)

        def grads(h, sub, slot):
            rows = pl.ds(sub * Q_TILE, Q_TILE)
            n_key = n_row if not masked else (sub + 1) * Q_TILE
            prob = p_scr[slot, :, :n_key]
            ds = ds_scr[slot, :, :n_key]
            dkv_acc[k_slot, 1, :, :n_key] += lax.dot_general(do_ref[h, rows, :], prob, (((0,), (0,)), ((), ())), preferred_element_type=F32)
            dkv_acc[k_slot, 0, :, :n_key] += lax.dot_general(q_ref[h, rows, :], ds, (((0,), (0,)), ((), ())), preferred_element_type=F32)
            base = jnp.where(fresh, dqi_ref[h, rows, :] if has_in else 0.0, dq_acc[h, rows, :])
            dq_acc[h, rows, :] = base + jnp.dot(ds, k_ref[:n_key, :], preferred_element_type=F32)

        tiles = [(h, sub) for h in range(n_head) for sub in range(n_sub)]
        scores(*tiles[0], 0)
        for idx, tile in enumerate(tiles):
            if idx + 1 < len(tiles):
                scores(*tiles[idx + 1], (idx + 1) % 2)
            grads(*tile, idx % 2)

    @pl.when(kind == 1)
    def _():
        run_task(False)

    if has_diag:
        @pl.when(kind == 2)
        def _():
            run_task(True)
    else:
        @pl.when(kind == 0)
        def _():
            dq_acc[...] = dqi_ref[...] if has_in else jnp.zeros_like(dq_acc)

    if is_end:
        @pl.when(is_last == 1)
        def _():
            dq_ref[...] = (dq_acc[...] * scaling).astype(BF16)

    @pl.when(step == pl.num_programs(0) - 1)
    def _():
        copies = [pltpu.make_async_copy(dkv_acc.at[pl.ds(4 * i, 4)], dkv_refs[i], out_sem.at[i]) for i in range(n_peer)]
        for copy in copies:
            copy.start()
        for copy in copies:
            copy.wait()


def block_call(table, q, do, lse, delta, kv, dq_in, is_end, has_diag):
    _, n_head, n_row, head_dim = q.shape
    n_key = kv.shape[1]
    n_peer = n_key // 4
    n_step = table.shape[0]
    has_in = dq_in is not None
    q_spec = pl.BlockSpec((None, n_head, n_row, head_dim), lambda t, tab: (tab[t, 0], 0, 0, 0))
    kv_specs = [pl.BlockSpec((None, None, n_row, head_dim), lambda t, tab, i=i: (i, tab[t, 1], 0, 0)) for i in range(2)]
    n_task = 8 * n_peer
    return pl.pallas_call(
        functools.partial(block_kernel, has_in, is_end, has_diag, n_peer),
        grid_spec=pltpu.PrefetchScalarGridSpec(
            num_scalar_prefetch=1,
            grid=(n_step,),
            in_specs=[q_spec] * 4 + kv_specs + ([q_spec] if has_in else []),
            out_specs=[q_spec] + [pl.BlockSpec(memory_space=pl.ANY)] * n_peer,
            scratch_shapes=[
                pltpu.VMEM((n_key, 2, head_dim, n_row), F32),
                pltpu.VMEM((head_dim, n_row), BF16),
                pltpu.VMEM((head_dim, n_row), BF16),
                pltpu.VMEM((2, Q_TILE, n_row), BF16),
                pltpu.VMEM((2, Q_TILE, n_row), BF16),
                pltpu.SemaphoreType.DMA((n_peer,)),
            ] + ([pltpu.VMEM((n_head, n_row, head_dim), F32)] if is_end else []),
        ),
        out_shape=[jax.ShapeDtypeStruct(q.shape, BF16 if is_end else F32)] + [jax.ShapeDtypeStruct((4, 2, head_dim, n_row), F32)] * n_peer,
        compiler_params=pltpu.CompilerParams(dimension_semantics=('arbitrary',), vmem_limit_bytes=48 * 1024 * 1024),
        cost_estimate=pl.CostEstimate(flops=n_task * n_head * 10 * n_row * n_row * head_dim, bytes_accessed=32 * 1024 * 1024, transcendentals=n_task * n_head * n_row * n_row),
    )(table, q, do, lse, delta, kv, kv, *([dq_in] if has_in else []))


def solution(mesh):
    n_cx = mesh.shape['cx']
    n_ctx = mesh.shape['cy'] * n_cx
    ctx_axes = ('cy', 'cx')
    row_spec = P(('dp', 'cy', 'cx'), None, None)
    stat_spec = P(('dp', 'cy', 'cx'), None)

    def swap(x, bit):
        return lax.ppermute(x, ctx_axes, [(dev, dev ^ bit) for dev in range(n_ctx)])

    def local_grads(query_rows, key_rows, value_rows, out_rows, grad_out, log_sum_exp):
        tok_dev, n_heads, head_dim = query_rows.shape
        kv_heads = key_rows.shape[1]
        group_size = n_heads // kv_heads
        half_tok = tok_dev // 2
        scaling = 1.0 / math.sqrt(head_dim)
        n_grp = kv_heads // 2
        ctx_rank = lax.axis_index('cy') * n_cx + lax.axis_index('cx')
        core = ctx_rank % 2

        def pick(x, g, mine):
            sel = core if mine else 1 - core
            return lax.dynamic_index_in_dim(x, sel * n_grp + g, axis=0, keepdims=False)

        def pieces_first(rows):
            return rows.reshape(2, half_tok, kv_heads, group_size, head_dim).transpose(2, 0, 3, 1, 4)

        def chip_rows(x, g, axis=0):
            return jnp.concatenate([pick(x, g, True), swap(pick(x, g, False), 1)], axis=axis)

        kv_rows = jnp.stack([key_rows, value_rows]).reshape(2, 2, half_tok, kv_heads, head_dim).transpose(3, 0, 1, 2, 4)
        kv_chip = [chip_rows(kv_rows, g, axis=1) for g in range(n_grp)]
        kv_far = [swap(kv_chip[g], 6) for g in range(n_grp)]
        kv_near = [jnp.concatenate([swap(kv_chip[g], 2), swap(kv_chip[g], 4)], axis=1) for g in range(n_grp)]

        q_pf, do_pf = pieces_first(query_rows), pieces_first(grad_out)
        q_pf, do_pf = lax.optimization_barrier((q_pf, do_pf))
        delta = jnp.einsum('thd,thd->th', grad_out, out_rows, preferred_element_type=F32)

        def stat_first(stat):
            return stat.reshape(2, half_tok, kv_heads, group_size).transpose(2, 0, 3, 1)

        stats = jnp.stack([stat_first(log_sum_exp * LOG2E), stat_first(delta)], axis=1)
        tables = {name: jnp.asarray(task_table(n_ctx, peers))[ctx_rank] for name, peers in (('own', (0,)), ('far', (3,)), ('near', (1, 2)))}

        def lanes(stat):
            return jnp.broadcast_to(stat[..., None], stat.shape + (128,))

        dq_all = jnp.zeros((kv_heads, 2, group_size, half_tok, head_dim), BF16)
        dkv_all = jnp.zeros((kv_heads, 2, 2, head_dim, half_tok), BF16)
        for g in range(n_grp):
            q = chip_rows(q_pf, g)
            do = chip_rows(do_pf, g)
            stat = chip_rows(stats, g, axis=1)
            rows = (q, do, lanes(stat[0]), lanes(stat[1]))

            def run(kind, kv, dq_in, is_end):
                return block_call(tables[kind], *rows, kv, dq_in, is_end, kind == 'own')

            last = g == n_grp - 1
            dq = None
            if not last:
                dq, dkv_own = run('own', kv_chip[g], None, False)
            dq, dkv_far = run('far', kv_far[g], dq, False)
            dq, dkv_x, dkv_y = run('near', kv_near[g], dq, not last)
            if last:
                dq, dkv_own = run('own', kv_chip[g], dq, True)
            dkv = dkv_own + swap(dkv_far, 6) + swap(dkv_x, 2) + swap(dkv_y, 4)
            dkv = (dkv * jnp.array([scaling, 1.0], F32)[None, :, None, None]).astype(BF16)
            dq_all = lax.dynamic_update_index_in_dim(dq_all, dq[:2], core * n_grp + g, 0)
            dq_all = lax.dynamic_update_index_in_dim(dq_all, swap(dq[2:], 1), (1 - core) * n_grp + g, 0)
            dkv_all = lax.dynamic_update_index_in_dim(dkv_all, dkv[:2], core * n_grp + g, 0)
            dkv_all = lax.dynamic_update_index_in_dim(dkv_all, swap(dkv[2:], 1), (1 - core) * n_grp + g, 0)

        grad_query = dq_all.transpose(1, 3, 0, 2, 4).reshape(tok_dev, n_heads, head_dim)
        grad_kv = dkv_all.transpose(2, 1, 4, 0, 3).reshape(2, tok_dev, kv_heads, head_dim)
        return grad_query, grad_kv[0], grad_kv[1]

    return jax.shard_map(local_grads, mesh=mesh, in_specs=(row_spec, row_spec, row_spec, row_spec, row_spec, stat_spec), out_specs=(row_spec, row_spec, row_spec), check_vma=False)
```

time: 760 us -> 678 us (0.89)
  other arithmetic: 96.3 us -> 34.8 us
  local copies, waits for them, and re-layouts: 150 us -> 106 us
  Pallas kernels: 319 us -> 344 us
    another operation x13 -> x1, local copies, waits for them, and re-layouts: 65 us -> 0.29 us  [local_grads(): jnp.stack([key_rows, value_rows])]
    another operation x17 -> x1, other arithmetic: 55.2 us -> 0.12 us  [local_grads(): jnp.stack([stat_first(log_sum_exp * LOG2E), stat_first(delta)], axis=1)]
    dynamic_update_slice x0 -> x10, local copies, waits for them, and re-layouts: none -> 43.1 us  [the longest x2 24.2 us: local_grads(): lax.dynamic_update_index_in_dim(dkv_all, swap(dkv[2:], 1), (1 - core) * n...]
    pallas_call x6, Pallas kernels: 319 us -> 344 us  [block_call(): pl.pallas_call(functools.partial(block_kernel, has_in, is_end, has_diag,...]
    broadcast_in_dim x0 -> x7, local copies, waits for them, and re-layouts: none -> 25.4 us  [the longest x4 16.8 us: lanes(): return jnp.broadcast_to(stat[..., None], stat.shape + (128,))]
    reduce_precision x4 -> x0, local copies, waits for them, and re-layouts: 18.5 us -> none  [split_parts(): part = lax.reduce_precision(x, 8, 7)]
    squeeze x12 -> x4, local copies, waits for them, and re-layouts: 28.5 us -> 13.9 us  [pick(): return lax.dynamic_index_in_dim(x, sel * n_grp + g, axis=0, keepdims=False)]
    pad x2 -> x0, local copies, waits for them, and re-layouts: 9.79 us -> none  [local_grads(): aug = jnp.pad(parts, ((0, 0), (0, 0), (0, 0), (0, 128 - 2 * N_PART)))]
  transfers between devices with their start and end apart: 24 -> 24, of which waited for: 3 -> 7; matrix products, arithmetic and copies ran while one was open for 29% -> 14% of each run, Pallas kernels for 42% -> 51%
where the time goes in v3:
time: 678 us; the launch traced here: 671 us
  Pallas kernels  344 us (51%)
  waiting for transfers between devices  165 us (24%)
  local copies, waits for them, and re-layouts  106 us (16%)
  other arithmetic  34.8 us (5%)
  starting transfers between devices  18.9 us (3%)
    pallas_call x6, Pallas kernels, block_call(): pl.pallas_call(functools.partial(block_kernel, has_in, is_end, has_diag,...  344 us
    ppermute x24, waiting for transfers between devices, swap(): return lax.ppermute(x, ctx_axes, [(dev, dev ^ bit) for dev in range(n_ctx)])  165 us
    dynamic_update_slice x2, local copies, waits for them, and re-layouts, local_grads(): lax.dynamic_update_index_in_dim(dkv_all, swap(dkv[2:], 1), (1 - core) * n...  24.2 us
    ppermute x24, starting transfers between devices, swap(): return lax.ppermute(x, ctx_axes, [(dev, dev ^ bit) for dev in range(n_ctx)])  18.9 us
    broadcast_in_dim x4, local copies, waits for them, and re-layouts, lanes(): return jnp.broadcast_to(stat[..., None], stat.shape + (128,))  16.8 us
    squeeze x4, local copies, waits for them, and re-layouts, pick(): return lax.dynamic_index_in_dim(x, sel * n_grp + g, axis=0, keepdims=False)  13.9 us
    concatenate x6, other arithmetic, chip_rows(): jnp.concatenate([pick(x, g, True), swap(pick(x, g, False), 1)], axis=axis)  13.7 us
  transfers between devices with their start and end apart: 24, of which 7 were waited for; matrix products, arithmetic and copies ran while one was open for 14% of the time, Pallas kernels for 51%

profile of v3, /device:TPU:0, one launch (start us, length us, event | category | flops | bytes accessed | tf_op | source)
XLA Modules:
  0.0 670.6 jit_solution(3134462452416596438)
XLA Ops:
  0.7 10.7 %copy_bitcast_fusion = (bf16[4,2,7,512,128]{4,3,2,1,0:T(8,128)(2,1)}, bf16[4,2,7,512,128]{4,3,2,1,0:T(8,128)(2,1)}) fusion(bf16[2,512,4,7,128]{4,1,0,3,2:T(8,128)(2,1)} %bitcast.92, bf16[2,512,4,7,128]{4,1,0,3,2:T(8,128)(2,1)} %bitcast.94), kind=kLoop, calls=%fused_computation.2 | loop fusion | bytes 29360128 | tf_op jit(solution)/shard_map/transpose | solution.py:180
  11.3 6.4 dynamic-slice_bitcast_fusion.1
  17.7 0.8 collective-permute-start.9
  18.9 0.3 copy_dynamic-update-slice_fusion.1
  19.2 1.1 dynamic-slice_bitcast_fusion.9
  20.4 0.8 collective-permute-start.11
  21.2 9.0 %fusion = f32[1024,28]{0,1:T(8,128)S(1)} fusion(bf16[1024,28,128]{2,0,1:T(8,128)(2,1)} %param.15, bf16[1024,28,128]{2,0,1:T(8,128)(2,1)} %param.14), kind=kLoop, calls=%fused_computation.1 | loop fusion | flops 14651392 | bytes 14794752 | tf_op jit(solution)/shard_map/thd,thd->th/dot_general | solution.py:192
  30.4 2.5 collective-permute-start.12
  33.5 0.3 collective-permute-start.3
  33.8 1.5 collective-permute-start.13
  35.3 6.4 dynamic-slice_bitcast_fusion.3
  41.7 0.5 collective-permute-start.2
  42.3 3.5 collective-permute-done.2
  45.8 0.8 collective-permute-start.4
  46.6 10.4 %collective-permute-done.12 = bf16[2,4,512,128]{3,2,1,0:T(8,128)(2,1)} collective-permute-done((bf16[2,4,512,128]{3,2,1,0:T(8,128)(2,1)S(1)}, bf16[2,4,512,128]{3,2,1,0:T(8,128)(2,1)}, u32[]{:S(2)}, u32[]{:S(2)}) %collective-permute-start.12) | collective-permute-done | bytes 1048608 | tf_op jit(solution)/shard_map/ppermute | solution.py:163
  57.0 2.0 collective-permute-start.5
  59.0 0.7 fusion.14
  59.8 0.7 fusion.13
  60.6 1.5 collective-permute-start.14
  62.1 0.7 fusion.15
  62.9 3.1 pad_maximum_fusion.5.k_ref.v_ref
  66.0 13.4 %collective-permute-done.4 = bf16[2,4,512,128]{3,2,1,0:T(8,128)(2,1)} collective-permute-done((bf16[2,4,512,128]{3,2,1,0:T(8,128)(2,1)S(1)}, bf16[2,4,512,128]{3,2,1,0:T(8,128)(2,1)}, u32[]{:S(2)}, u32[]{:S(2)}) %collective-permute-start.4) | collective-permute-done | bytes 1048608 | tf_op jit(solution)/shard_map/ppermute | solution.py:163
  79.5 24.9 %collective-permute-done.5 = bf16[2,4,512,128]{3,2,1,0:T(8,128)(2,1)} collective-permute-done((bf16[2,4,512,128]{3,2,1,0:T(8,128)(2,1)S(1)}, bf16[2,4,512,128]{3,2,1,0:T(8,128)(2,1)}, u32[]{:S(2)}, u32[]{:S(2)}) %collective-permute-start.5) | collective-permute-done | bytes 1048608 | tf_op jit(solution)/shard_map/ppermute | solution.py:163
  104.4 3.2 pad_maximum_fusion.4.k_ref.v_ref
  107.6 2.4 collective-permute-start.6
  110.0 3.9 pad_maximum_fusion.3.do_ref
  113.9 3.6 pad_maximum_fusion.2.q_ref
  117.5 4.1 broadcast_in_dim.70.lse_ref
  121.7 4.3 broadcast_in_dim.72.delta_ref
  126.0 45.5 %shard_map.133 = (f32[4,7,512,128]{3,2,1,0:T(8,128)}, f32[4,2,128,512]{3,2,1,0:T(8,128)S(1)}) custom-call(s32[10,5]{1,0:T(8,128)S(1)} %copy.21.tab_ref, bf16[4,7,512,128]{3,2,1,0:T(8,128)(2,1)} %pad_maximum_fusion.2.q_ref, bf16[4,7,512,128]{3,2,1,0:T(8,128)(2,1)} %pad_maximum_fusion.3.do_ref, f32[4,7,512,128]{3,2,1,0:T(8,128)} %broadcast_in_dim.70.lse_ref, ...), custom_call_target="tpu_custom_call" | custom-call | flops 18790481920 | bytes 33554432 | tf_op jit(solution)/shard_map/pallas_call | solution.py:133
  171.4 81.3 %shard_map.134 = (f32[4,7,512,128]{3,2,1,0:T(8,128)}, f32[4,2,128,512]{3,2,1,0:T(8,128)S(1)}, f32[4,2,128,512]{3,2,1,0:T(8,128)S(1)}) custom-call(s32[18,5]{1,0:T(8,128)S(1)} %copy.22.tab_ref, bf16[4,7,512,128]{3,2,1,0:T(8,128)(2,1)} %pad_maximum_fusion.2.q_ref, bf16[4,7,512,128]{3,2,1,0:T(8,128)(2,1)} %pad_maximum_fusion.3.do_ref, ...), custom_call_target="tpu_custom_call" | custom-call | flops 37580963840 | bytes 33554432 | tf_op jit(solution)/shard_map/pallas_call | solution.py:133
  252.9 3.8 pad_maximum_fusion.1.do_ref
  256.7 2.2 pad_maximum_fusion.q_ref
  258.8 4.1 broadcast_in_dim.64.lse_ref
  263.0 4.3 broadcast_in_dim.66.delta_ref
  267.2 43.4 %shard_map.130 = (f32[4,7,512,128]{3,2,1,0:T(8,128)}, f32[4,2,128,512]{3,2,1,0:T(8,128)S(1)}) custom-call(s32[10,5]{1,0:T(8,128)S(1)} %copy.20.tab_ref, bf16[4,7,512,128]{3,2,1,0:T(8,128)(2,1)} %pad_maximum_fusion.q_ref, bf16[4,7,512,128]{3,2,1,0:T(8,128)(2,1)} %pad_maximum_fusion.1.do_ref, f32[4,7,512,128]{3,2,1,0:T(8,128)} %broadcast_in_dim.64.lse_ref, ...), custom_call_target="tpu_custom_call" | custom-call | flops 18790481920 | bytes 33554432 | tf_op jit(solution)/shard_map/pallas_call | solution.py:133
  310.6 48.0 %shard_map.131 = (f32[4,7,512,128]{3,2,1,0:T(8,128)}, f32[4,2,128,512]{3,2,1,0:T(8,128)}) custom-call(s32[10,5]{1,0:T(8,128)S(1)} %copy.21.tab_ref, bf16[4,7,512,128]{3,2,1,0:T(8,128)(2,1)} %pad_maximum_fusion.q_ref, bf16[4,7,512,128]{3,2,1,0:T(8,128)(2,1)} %pad_maximum_fusion.1.do_ref, f32[4,7,512,128]{3,2,1,0:T(8,128)} %broadcast_in_dim.64.lse_ref, ...), custom_call_target="tpu_custom_call" | custom-call | flops 18790481920 | bytes 33554432 | tf_op jit(solution)/shard_map/pallas_call | solution.py:133
  358.6 82.0 %shard_map.132 = (bf16[4,7,512,128]{3,2,1,0:T(8,128)(2,1)}, f32[4,2,128,512]{3,2,1,0:T(8,128)}, f32[4,2,128,512]{3,2,1,0:T(8,128)}) custom-call(s32[18,5]{1,0:T(8,128)S(1)} %copy.22.tab_ref, bf16[4,7,512,128]{3,2,1,0:T(8,128)(2,1)} %pad_maximum_fusion.q_ref, bf16[4,7,512,128]{3,2,1,0:T(8,128)(2,1)} %pad_maximum_fusion.1.do_ref, ...), custom_call_target="tpu_custom_call" | custom-call | flops 37580963840 | bytes 33554432 | tf_op jit(solution)/shard_map/pallas_call | solution.py:133
  440.6 1.6 slice.47
  442.4 3.5 collective-permute-start.17
  446.1 1.3 collective-permute-start.16
  447.4 44.3 %shard_map.135 = (bf16[4,7,512,128]{3,2,1,0:T(8,128)(2,1)}, f32[4,2,128,512]{3,2,1,0:T(8,128)S(1)}) custom-call(s32[10,5]{1,0:T(8,128)S(1)} %copy.20.tab_ref, bf16[4,7,512,128]{3,2,1,0:T(8,128)(2,1)} %pad_maximum_fusion.2.q_ref, bf16[4,7,512,128]{3,2,1,0:T(8,128)(2,1)} %pad_maximum_fusion.3.do_ref, f32[4,7,512,128]{3,2,1,0:T(8,128)} %broadcast_in_dim.70.lse_ref, ...), custom_call_target="tpu_custom_call" | custom-call | flops 18790481920 | bytes 33554432 | tf_op jit(solution)/shard_map/pallas_call | solution.py:133
  491.6 2.9 slice.51
  494.5 41.5 %collective-permute-done.22 = f32[4,2,128,512]{3,2,1,0:T(8,128)S(1)} collective-permute-done((f32[4,2,128,512]{3,2,1,0:T(8,128)S(1)}, f32[4,2,128,512]{3,2,1,0:T(8,128)S(1)}, u32[]{:S(2)}, u32[]{:S(2)}) %collective-permute-start.22) | collective-permute-done | bytes 2097184 | tf_op jit(solution)/shard_map/ppermute | solution.py:163
  536.0 4.6 broadcast_in_dim.62
  540.6 1.4 bitcast_dynamic-update-slice_fusion.2
  542.1 0.7 copy-done.7
  542.8 1.4 bitcast_dynamic-update-slice_fusion.1
  544.2 1.3 copy-done.5
  545.5 1.4 bitcast_dynamic-update-slice_fusion
  546.9 7.0 %copy.28 = bf16[4,2,7,512,128]{4,3,1,2,0:T(8,128)(2,1)} copy(bf16[4,2,7,512,128]{4,3,2,1,0:T(8,128)(2,1)} %bitcast_dynamic-update-slice_fusion) | data formatting | bytes 14680064 | tf_op jit(solution)/shard_map/jit(dynamic_update_index_in_dim)/dynamic_update_slice | solution.py:224
  553.9 71.4 %collective-permute-done.18 = f32[4,2,128,512]{3,2,1,0:T(8,128)} collective-permute-done((f32[4,2,128,512]{3,2,1,0:T(8,128)}, f32[4,2,128,512]{3,2,1,0:T(8,128)}, u32[]{:S(2)}, u32[]{:S(2)}) %collective-permute-start.18) | collective-permute-done | bytes 2097184 | tf_op jit(solution)/shard_map/ppermute | solution.py:163
  625.3 5.6 multiply_convert_fusion
  631.0 2.9 copy_dynamic-update-slice_fusion
  633.9 0.5 collective-permute-start.23
  634.4 1.5 broadcast_in_dim.75
  636.0 0.8 fusion.2
  636.8 0.8 bitcast_dynamic-update-slice_fusion.3
  637.7 0.9 fusion.1
  638.5 3.1 copy.30
  641.7 0.8 copy-done.10
  642.4 2.4 copy.31
  644.8 23.4 %dynamic_update_slice.33 = bf16[4,2,2,128,512]{3,0,4,1,2:T(4,128)(2,1)S(1)} dynamic-update-slice(bf16[4,2,2,128,512]{3,0,4,1,2:T(4,128)(2,1)S(1)} %copy.30, bf16[1,2,2,128,512]{3,0,4,1,2:T(2,128)(2,1)S(1)} %copy.31, s32[]{:T(128)S(6)} %select_n.54, s32[]{:T(128)} %constant.96.clone.1, s32[]{:T(128)} %constant.96.clone.1, s32[]{:T(128)} %constant.96.clone.1, s32[]{:T(128)} %constant.96.clone.1) | dynamic-update-slice | bytes 1048580 | tf_op jit(solution)/shard_map/jit(dynamic_update_index_in_dim)/dynamic_update_slice | solution.py:227
  668.2 2.0 fusion.16
  (69 shorter events, 2.1 us)
Async XLA Ops:
  11.3 7.2 %copy-start.8 = (bf16[1024,4,128]{2,1,0:T(4,128)(2,1)S(1)}, bf16[1024,4,128]{2,1,0:T(4,128)(2,1)}, u32[]{:S(2)}) copy-start(bf16[1024,4,128]{2,1,0:T(4,128)(2,1)} %param.12) | copy-start | bytes 3145732
  17.7 1.2 copy-start.9
  17.7 89.9 %collective-permute-start.9 = (bf16[2,7,512,128]{3,2,1,0:T(8,128)(2,1)}, bf16[2,7,512,128]{3,2,1,0:T(8,128)(2,1)}, u32[]{:S(2)}, u32[]{:S(2)}) collective-permute-start(bf16[2,7,512,128]{3,2,1,0:T(8,128)(2,1)} %get-tuple-element.36), channel_id=1, source_target_pairs={{0,1},{1,0},{2,3},{3,2},{4,5},{5,4},{6,7},{7,6}} | collective-permute-start | bytes 5505032 | tf_op jit(solution)/shard_map/ppermute | solution.py:163
  20.4 9.9 %collective-permute-start.11 = (bf16[2,2,512,128]{3,2,1,0:T(8,128)(2,1)}, bf16[2,2,512,128]{3,2,1,0:T(8,128)(2,1)S(1)}, u32[]{:S(2)}, u32[]{:S(2)}) collective-permute-start(bf16[2,2,512,128]{3,2,1,0:T(8,128)(2,1)} %get-tuple-element.46), channel_id=1, source_target_pairs={{0,1},{1,0},{2,3},{3,2},{4,5},{5,4},{6,7},{7,6}} | collective-permute-start | bytes 1572872 | tf_op jit(solution)/shard_map/ppermute | solution.py:163
  30.2 2.6 copy-start.11
  30.4 26.6 %collective-permute-start.12 = (bf16[2,4,512,128]{3,2,1,0:T(8,128)(2,1)S(1)}, bf16[2,4,512,128]{3,2,1,0:T(8,128)(2,1)}, u32[]{:S(2)}, u32[]{:S(2)}) collective-permute-start(bf16[2,4,512,128]{3,2,1,0:T(8,128)(2,1)S(1)} %pad_maximum_fusion.7.k_ref.v_ref), channel_id=1, source_target_pairs={{0,2},{1,3},{2,0},{3,1},{4,6},{5,7},{6,4},{7,5}} | collective-permute-start | bytes 3145736 | tf_op jit(solution)/shard_map/ppermute | solution.py:163
  33.2 8.4 %collective-permute-start.10 = (f32[2,2,7,512]{3,2,1,0:T(8,128)S(1)}, f32[2,2,7,512]{3,2,1,0:T(8,128)S(1)}, u32[]{:S(2)}, u32[]{:S(2)}) collective-permute-start(f32[2,2,7,512]{3,2,1,0:T(8,128)S(1)} %bitcast.103), channel_id=1, source_target_pairs={{0,1},{1,0},{2,3},{3,2},{4,5},{5,4},{6,7},{7,6}} | collective-permute-start | bytes 172040 | tf_op jit(solution)/shard_map/ppermute | solution.py:163
  33.5 8.2 %collective-permute-start.3 = (bf16[2,2,512,128]{3,2,1,0:T(8,128)(2,1)}, bf16[2,2,512,128]{3,2,1,0:T(8,128)(2,1)S(1)}, u32[]{:S(2)}, u32[]{:S(2)}) collective-permute-start(bf16[2,2,512,128]{3,2,1,0:T(8,128)(2,1)} %get-tuple-element.47), channel_id=1, source_target_pairs={{0,1},{1,0},{2,3},{3,2},{4,5},{5,4},{6,7},{7,6}} | collective-permute-start | bytes 1572872 | tf_op jit(solution)/shard_map/ppermute | solution.py:163
  33.8 26.9 %collective-permute-start.13 = (bf16[2,4,512,128]{3,2,1,0:T(8,128)(2,1)S(1)}, bf16[2,4,512,128]{3,2,1,0:T(8,128)(2,1)}, u32[]{:S(2)}, u32[]{:S(2)}) collective-permute-start(bf16[2,4,512,128]{3,2,1,0:T(8,128)(2,1)S(1)} %pad_maximum_fusion.7.k_ref.v_ref), channel_id=1, source_target_pairs={{0,4},{1,5},{2,6},{3,7},{4,0},{5,1},{6,2},{7,3}} | collective-permute-start | bytes 3145736 | tf_op jit(solution)/shard_map/ppermute | solution.py:163
  41.7 72.2 %collective-permute-start.8 = (bf16[2,7,512,128]{3,2,1,0:T(8,128)(2,1)}, bf16[2,7,512,128]{3,2,1,0:T(8,128)(2,1)}, u32[]{:S(2)}, u32[]{:S(2)}) collective-permute-start(bf16[2,7,512,128]{3,2,1,0:T(8,128)(2,1)} %get-tuple-element.40), channel_id=1, source_target_pairs={{0,1},{1,0},{2,3},{3,2},{4,5},{5,4},{6,7},{7,6}} | collective-permute-start | bytes 5505032 | tf_op jit(solution)/shard_map/ppermute | solution.py:163
  41.7 4.1 collective-permute-start.2
  45.8 33.7 %collective-permute-start.4 = (bf16[2,4,512,128]{3,2,1,0:T(8,128)(2,1)S(1)}, bf16[2,4,512,128]{3,2,1,0:T(8,128)(2,1)}, u32[]{:S(2)}, u32[]{:S(2)}) collective-permute-start(bf16[2,4,512,128]{3,2,1,0:T(8,128)(2,1)S(1)} %pad_maximum_fusion.6.k_ref.v_ref), channel_id=1, source_target_pairs={{0,2},{1,3},{2,0},{3,1},{4,6},{5,7},{6,4},{7,5}} | collective-permute-start | bytes 3145736 | tf_op jit(solution)/shard_map/ppermute | solution.py:163
  57.0 47.4 %collective-permute-start.5 = (bf16[2,4,512,128]{3,2,1,0:T(8,128)(2,1)S(1)}, bf16[2,4,512,128]{3,2,1,0:T(8,128)(2,1)}, u32[]{:S(2)}, u32[]{:S(2)}) collective-permute-start(bf16[2,4,512,128]{3,2,1,0:T(8,128)(2,1)S(1)} %pad_maximum_fusion.6.k_ref.v_ref), channel_id=1, source_target_pairs={{0,4},{1,5},{2,6},{3,7},{4,0},{5,1},{6,2},{7,3}} | collective-permute-start | bytes 3145736 | tf_op jit(solution)/shard_map/ppermute | solution.py:163
  60.6 56.9 %collective-permute-start.14 = (bf16[2,4,512,128]{3,2,1,0:T(8,128)(2,1)S(1)}, bf16[2,4,512,128]{3,2,1,0:T(8,128)(2,1)S(1)}, u32[]{:S(2)}, u32[]{:S(2)}) collective-permute-start(bf16[2,4,512,128]{3,2,1,0:T(8,128)(2,1)S(1)} %pad_maximum_fusion.7.k_ref.v_ref), channel_id=1, source_target_pairs={{0,6},{1,7},{2,4},{3,5},{4,2},{5,3},{6,0},{7,1}} | collective-permute-start | bytes 3145736 | tf_op jit(solution)/shard_map/ppermute | solution.py:163
  79.5 173.4 %collective-permute-start.1 = (bf16[2,7,512,128]{3,2,1,0:T(8,128)(2,1)}, bf16[2,7,512,128]{3,2,1,0:T(8,128)(2,1)}, u32[]{:S(2)}, u32[]{:S(2)}) collective-permute-start(bf16[2,7,512,128]{3,2,1,0:T(8,128)(2,1)} %get-tuple-element.37), channel_id=1, source_target_pairs={{0,1},{1,0},{2,3},{3,2},{4,5},{5,4},{6,7},{7,6}} | collective-permute-start | bytes 5505032 | tf_op jit(solution)/shard_map/ppermute | solution.py:163
  104.4 5.6 copy-start.1
  104.4 152.3 %collective-permute-start = (bf16[2,7,512,128]{3,2,1,0:T(8,128)(2,1)}, bf16[2,7,512,128]{3,2,1,0:T(8,128)(2,1)S(1)}, u32[]{:S(2)}, u32[]{:S(2)}) collective-permute-start(bf16[2,7,512,128]{3,2,1,0:T(8,128)(2,1)} %get-tuple-element.41), channel_id=1, source_target_pairs={{0,1},{1,0},{2,3},{3,2},{4,5},{5,4},{6,7},{7,6}} | collective-permute-start | bytes 5505032 | tf_op jit(solution)/shard_map/ppermute | solution.py:163
  107.6 203.0 %collective-permute-start.6 = (bf16[2,4,512,128]{3,2,1,0:T(8,128)(2,1)S(1)}, bf16[2,4,512,128]{3,2,1,0:T(8,128)(2,1)S(1)}, u32[]{:S(2)}, u32[]{:S(2)}) collective-permute-start(bf16[2,4,512,128]{3,2,1,0:T(8,128)(2,1)S(1)} %pad_maximum_fusion.6.k_ref.v_ref), channel_id=1, source_target_pairs={{0,6},{1,7},{2,4},{3,5},{4,2},{5,3},{6,0},{7,1}} | collective-permute-start | bytes 3145736 | tf_op jit(solution)/shard_map/ppermute | solution.py:163
  110.0 3.9 copy-start.3
  171.4 81.4 %copy-start = (bf16[2,7,512,128]{3,2,1,0:T(8,128)(2,1)S(1)}, bf16[2,7,512,128]{3,2,1,0:T(8,128)(2,1)}, u32[]{:S(2)}) copy-start(bf16[2,7,512,128]{3,2,1,0:T(8,128)(2,1)} %get-tuple-element.38) | copy-start | bytes 5505028
  252.8 193.3 %collective-permute-start.21 = (f32[4,2,128,512]{3,2,1,0:T(8,128)S(1)}, f32[4,2,128,512]{3,2,1,0:T(8,128)}, u32[]{:S(2)}, u32[]{:S(2)}) collective-permute-start(f32[4,2,128,512]{3,2,1,0:T(8,128)S(1)} %get-tuple-element.33), channel_id=1, source_target_pairs={{0,2},{1,3},{2,0},{3,1},{4,6},{5,7},{6,4},{7,5}} | collective-permute-start | bytes 6291464 | tf_op jit(solution)/shard_map/ppermute | solution.py:163
  252.8 3.8 copy-start.2
  442.3 3.8 collective-permute-start.7
  442.4 93.6 %collective-permute-start.22 = (f32[4,2,128,512]{3,2,1,0:T(8,128)S(1)}, f32[4,2,128,512]{3,2,1,0:T(8,128)S(1)}, u32[]{:S(2)}, u32[]{:S(2)}) collective-permute-start(f32[4,2,128,512]{3,2,1,0:T(8,128)S(1)} %get-tuple-element.34), channel_id=1, source_target_pairs={{0,4},{1,5},{2,6},{3,7},{4,0},{5,1},{6,2},{7,3}} | collective-permute-start | bytes 6291464 | tf_op jit(solution)/shard_map/ppermute | solution.py:163
  442.4 111.5 %collective-permute-start.20 = (f32[4,2,128,512]{3,2,1,0:T(8,128)S(1)}, f32[4,2,128,512]{3,2,1,0:T(8,128)S(1)}, u32[]{:S(2)}, u32[]{:S(2)}) collective-permute-start(f32[4,2,128,512]{3,2,1,0:T(8,128)S(1)} %get-tuple-element.32), channel_id=1, source_target_pairs={{0,6},{1,7},{2,4},{3,5},{4,2},{5,3},{6,0},{7,1}} | collective-permute-start | bytes 6291464 | tf_op jit(solution)/shard_map/ppermute | solution.py:163
  442.4 111.5 %collective-permute-start.17 = (f32[4,2,128,512]{3,2,1,0:T(8,128)}, f32[4,2,128,512]{3,2,1,0:T(8,128)}, u32[]{:S(2)}, u32[]{:S(2)}) collective-permute-start(f32[4,2,128,512]{3,2,1,0:T(8,128)} %get-tuple-element.29), channel_id=1, source_target_pairs={{0,2},{1,3},{2,0},{3,1},{4,6},{5,7},{6,4},{7,5}} | collective-permute-start | bytes 6291464 | tf_op jit(solution)/shard_map/ppermute | solution.py:163
  446.1 1.3 copy-start.6
  446.1 179.2 %collective-permute-start.18 = (f32[4,2,128,512]{3,2,1,0:T(8,128)}, f32[4,2,128,512]{3,2,1,0:T(8,128)}, u32[]{:S(2)}, u32[]{:S(2)}) collective-permute-start(f32[4,2,128,512]{3,2,1,0:T(8,128)} %get-tuple-element.30), channel_id=1, source_target_pairs={{0,4},{1,5},{2,6},{3,7},{4,0},{5,1},{6,2},{7,3}} | collective-permute-start | bytes 6291464 | tf_op jit(solution)/shard_map/ppermute | solution.py:163
  446.1 179.2 %collective-permute-start.16 = (f32[4,2,128,512]{3,2,1,0:T(8,128)}, f32[4,2,128,512]{3,2,1,0:T(8,128)}, u32[]{:S(2)}, u32[]{:S(2)}) collective-permute-start(f32[4,2,128,512]{3,2,1,0:T(8,128)} %get-tuple-element.28), channel_id=1, source_target_pairs={{0,6},{1,7},{2,4},{3,5},{4,2},{5,3},{6,0},{7,1}} | collective-permute-start | bytes 6291464 | tf_op jit(solution)/shard_map/ppermute | solution.py:163
  494.5 46.1 %copy-start.4 = (bf16[4,7,512,128]{3,2,1,0:T(8,128)(2,1)S(1)}, bf16[4,7,512,128]{3,2,1,0:T(8,128)(2,1)}, u32[]{:S(2)}) copy-start(bf16[4,7,512,128]{3,2,1,0:T(8,128)(2,1)} %get-tuple-element.23) | copy-start | bytes 11010052
  536.0 95.0 %collective-permute-start.15 = (bf16[2,7,512,128]{3,2,1,0:T(8,128)(2,1)}, bf16[2,7,512,128]{3,2,1,0:T(8,128)(2,1)}, u32[]{:S(2)}, u32[]{:S(2)}) collective-permute-start(bf16[2,7,512,128]{3,2,1,0:T(8,128)(2,1)} %slice.51), channel_id=1, source_target_pairs={{0,1},{1,0},{2,3},{3,2},{4,5},{5,4},{6,7},{7,6}} | collective-permute-start | bytes 5505032 | tf_op jit(solution)/shard_map/ppermute | solution.py:163
  540.6 2.2 copy-start.7
  542.8 2.7 copy-start.5
  546.9 78.4 %copy-start.12 = (f32[2]{0:T(128)S(1)}, f32[2]{0:T(128)}, u32[]{:S(2)}) copy-start(f32[2]{0:T(128)} %constant.105.clone) | copy-start | bytes 28
  630.9 5.9 collective-permute-start.19
  633.9 7.7 %collective-permute-start.23 = (bf16[2,2,128,512]{3,2,1,0:T(8,128)(2,1)S(1)}, bf16[2,2,128,512]{3,2,1,0:T(8,128)(2,1)S(1)}, u32[]{:S(2)}, u32[]{:S(2)}) collective-permute-start(bf16[2,2,128,512]{3,2,1,0:T(8,128)(2,1)S(1)} %slice.65), channel_id=1, source_target_pairs={{0,1},{1,0},{2,3},{3,2},{4,5},{5,4},{6,7},{7,6}} | collective-permute-start | bytes 1572872 | tf_op jit(solution)/shard_map/ppermute | solution.py:163
  641.6 0.8 copy-start.10

commit v4 on v3

v4 whole, which is shorter than its diff:
```python
import functools
import math
import numpy as np
import jax
import jax.numpy as jnp
from jax import lax
from jax.experimental import pallas as pl
from jax.experimental.pallas import tpu as pltpu
from jax.sharding import PartitionSpec as P

LOG2E = math.log2(math.e)
F32 = jnp.float32
BF16 = jnp.bfloat16
Q_TILE = 256
FULL_TILE = 512
N_PART = 3


def task_table(n_ctx, peers):
    tables = []
    for rank in range(n_ctx):
        chip, core = rank // 2, rank % 2

        def ids(chip_id):
            devs = (2 * chip_id + core, 2 * chip_id + 1 - core)
            return [dev if half == 0 else 2 * n_ctx - 1 - dev for dev in devs for half in range(2)]

        rows = []
        keys = [piece for peer in peers for piece in ids(chip ^ peer)]
        for q_slot, q_id in enumerate(ids(chip)):
            todo = [(k_slot, 2 if k_id == q_id else 1) for k_slot, k_id in enumerate(keys) if k_id <= q_id]
            todo = todo or [(rows[-1][1] if rows else 0, 0)]
            for n, (k_slot, kind) in enumerate(todo):
                rows.append([q_slot, k_slot, kind, int(n == 0), int(n == len(todo) - 1)])
        tables.append(rows)
    n_step = max(len(rows) for rows in tables)
    for rows in tables:
        while len(rows) < n_step:
            rows.append([rows[-1][0], rows[-1][1], 3, 0, 0])
    return np.array(tables, np.int32)


def block_kernel(has_in, is_end, has_diag, n_peer, tab_ref, q_ref, do_ref, aug_ref, k_ref, v_ref, *refs):
    if has_in:
        dqi_ref, *refs = refs
    dq_ref, *refs = refs
    dkv_refs, (dkv_acc, kt_scr, vt_scr, p_scr, ds_scr, dkv_rows, out_sem, *refs) = refs[:n_peer], refs[n_peer:]
    dq_acc = refs[0] if is_end else dq_ref
    n_head, n_row, head_dim = q_ref.shape
    scaling = 1.0 / math.sqrt(head_dim)
    step = pl.program_id(0)
    k_slot = tab_ref[step, 1]
    kind = tab_ref[step, 2]
    is_first = tab_ref[step, 3]
    is_last = tab_ref[step, 4]

    @pl.when(step == 0)
    def _():
        dkv_acc[...] = jnp.zeros_like(dkv_acc)
        row_id = lax.broadcasted_iota(jnp.int32, (head_dim, n_row), 0)
        kt_scr[head_dim:, :] = jnp.where(row_id < N_PART, -1.0, 0.0).astype(BF16)
        vt_scr[head_dim:, :] = jnp.where((row_id >= N_PART) & (row_id < 2 * N_PART), -1.0, 0.0).astype(BF16)

    if has_in:
        @pl.when(is_first == 1)
        def _():
            dq_acc[...] = dqi_ref[...]

    def run_task(masked):
        tile = Q_TILE if masked else FULL_TILE
        kt_scr[:head_dim, :] = k_ref[...].T
        vt_scr[:head_dim, :] = v_ref[...].T
        fresh = is_first == 1

        def scores(h, sub, slot):
            rows = pl.ds(sub * tile, tile)
            n_key = n_row if not masked else (sub + 1) * tile
            aug = aug_ref[h, rows, :]
            s = jnp.dot(jnp.concatenate([q_ref[h, rows, :], aug], axis=1), kt_scr[:, :n_key], preferred_element_type=F32)
            dp = jnp.dot(jnp.concatenate([do_ref[h, rows, :], aug], axis=1), vt_scr[:, :n_key], preferred_element_type=F32)
            prob = jnp.exp2(s * (scaling * LOG2E))
            if masked:
                qi = lax.broadcasted_iota(jnp.int32, s.shape, 0) + sub * tile
                kj = lax.broadcasted_iota(jnp.int32, s.shape, 1)
                prob = jnp.where(qi >= kj, prob, 0.0)
            p_scr[slot, :tile, :n_key] = prob.astype(BF16)
            ds_scr[slot, :tile, :n_key] = (prob * dp).astype(BF16)

        def grads(h, sub, slot):
            rows = pl.ds(sub * tile, tile)
            n_key = n_row if not masked else (sub + 1) * tile
            prob = p_scr[slot, :tile, :n_key]
            ds = ds_scr[slot, :tile, :n_key]
            dkv_acc[k_slot, 1, :, :n_key] += lax.dot_general(do_ref[h, rows, :], prob, (((0,), (0,)), ((), ())), preferred_element_type=F32)
            dkv_acc[k_slot, 0, :, :n_key] += lax.dot_general(q_ref[h, rows, :], ds, (((0,), (0,)), ((), ())), preferred_element_type=F32)
            base = dq_acc[h, :, rows] if has_in else jnp.where(fresh, 0.0, dq_acc[h, :, rows])
            dq_acc[h, :, rows] = base + lax.dot_general(kt_scr[:head_dim, :n_key], ds, (((1,), (1,)), ((), ())), preferred_element_type=F32)

        tiles = [(h, sub) for h in range(n_head) for sub in range(n_row // tile)]
        scores(*tiles[0], 0)
        for idx, tile_id in enumerate(tiles):
            if idx + 1 < len(tiles):
                scores(*tiles[idx + 1], (idx + 1) % 2)
            grads(*tile_id, idx % 2)

    @pl.when(kind == 1)
    def _():
        run_task(False)

    if has_diag:
        @pl.when(kind == 2)
        def _():
            run_task(True)
    elif not has_in:
        @pl.when(kind == 0)
        def _():
            dq_acc[...] = jnp.zeros_like(dq_acc)

    if is_end:
        @pl.when(is_last == 1)
        def _():
            for h in range(n_head):
                dq_ref[h] = (dq_acc[h].T * scaling).astype(BF16)

    @pl.when(step == pl.num_programs(0) - 1)
    def _():
        for i in range(n_peer):
            @pl.loop(0, 4)
            def _(j):
                dkv_rows[i, 0, j] = dkv_acc[4 * i + j, 0].T * scaling
                dkv_rows[i, 1, j] = dkv_acc[4 * i + j, 1].T

            pltpu.make_async_copy(dkv_rows.at[i], dkv_refs[i], out_sem.at[i]).start()
        for i in range(n_peer):
            pltpu.make_async_copy(dkv_rows.at[i], dkv_refs[i], out_sem.at[i]).wait()


def block_call(table, q, do, aug, kv, dq_in, is_end, has_diag):
    n_q, n_head, n_row, head_dim = q.shape
    n_key = kv.shape[1]
    n_peer = n_key // 4
    n_step = table.shape[0]
    has_in = dq_in is not None
    q_spec = pl.BlockSpec((None, n_head, n_row, head_dim), lambda t, tab: (tab[t, 0], 0, 0, 0))
    kv_specs = [pl.BlockSpec((None, None, n_row, head_dim), lambda t, tab, i=i: (i, tab[t, 1], 0, 0)) for i in range(2)]
    qt_spec = pl.BlockSpec((None, n_head, head_dim, n_row), lambda t, tab: (tab[t, 0], 0, 0, 0))
    n_task = 8 * n_peer
    return pl.pallas_call(
        functools.partial(block_kernel, has_in, is_end, has_diag, n_peer),
        grid_spec=pltpu.PrefetchScalarGridSpec(
            num_scalar_prefetch=1,
            grid=(n_step,),
            in_specs=[q_spec] * 3 + kv_specs + ([qt_spec] if has_in else []),
            out_specs=[q_spec if is_end else qt_spec] + [pl.BlockSpec(memory_space=pl.ANY)] * n_peer,
            scratch_shapes=[
                pltpu.VMEM((n_key, 2, head_dim, n_row), F32),
                pltpu.VMEM((2 * head_dim, n_row), BF16),
                pltpu.VMEM((2 * head_dim, n_row), BF16),
                pltpu.VMEM((2, FULL_TILE, n_row), BF16),
                pltpu.VMEM((2, FULL_TILE, n_row), BF16),
                pltpu.VMEM((n_peer, 2, 4, n_row, head_dim), F32),
                pltpu.SemaphoreType.DMA((n_peer,)),
            ] + ([pltpu.VMEM((n_head, head_dim, n_row), F32)] if is_end else []),
        ),
        out_shape=[jax.ShapeDtypeStruct(q.shape, BF16) if is_end else jax.ShapeDtypeStruct((n_q, n_head, head_dim, n_row), F32)] + [jax.ShapeDtypeStruct((2, 4, n_row, head_dim), F32)] * n_peer,
        compiler_params=pltpu.CompilerParams(dimension_semantics=('arbitrary',), vmem_limit_bytes=50 * 1024 * 1024),
        cost_estimate=pl.CostEstimate(flops=n_task * n_head * 10 * n_row * n_row * head_dim, bytes_accessed=32 * 1024 * 1024, transcendentals=n_task * n_head * n_row * n_row),
    )(table, q, do, aug, kv, kv, *([dq_in] if has_in else []))


def lane_parts(lse, delta):
    lane = lax.broadcasted_iota(jnp.int32, lse.shape + (128,), lse.ndim)
    rest = jnp.where(lane < N_PART, lse[..., None], delta[..., None])
    part = lax.reduce_precision(rest, 8, 7)
    out = part
    for n in range(1, N_PART):
        rest = rest - part
        part = lax.reduce_precision(rest, 8, 7)
        out = jnp.where(lane % N_PART == n, part, out)
    return jnp.where(lane < 2 * N_PART, out, 0.0).astype(BF16)


def solution(mesh):
    n_cx = mesh.shape['cx']
    n_ctx = mesh.shape['cy'] * n_cx
    ctx_axes = ('cy', 'cx')
    row_spec = P(('dp', 'cy', 'cx'), None, None)
    stat_spec = P(('dp', 'cy', 'cx'), None)

    def swap(x, bit):
        return lax.ppermute(x, ctx_axes, [(dev, dev ^ bit) for dev in range(n_ctx)])

    def local_grads(query_rows, key_rows, value_rows, out_rows, grad_out, log_sum_exp):
        tok_dev, n_heads, head_dim = query_rows.shape
        kv_heads = key_rows.shape[1]
        group_size = n_heads // kv_heads
        half_tok = tok_dev // 2
        n_grp = kv_heads // 2
        ctx_rank = lax.axis_index('cy') * n_cx + lax.axis_index('cx')
        core = ctx_rank % 2

        def pick(x, g, mine):
            sel = core if mine else 1 - core
            return lax.dynamic_index_in_dim(x, sel * n_grp + g, axis=0, keepdims=False)

        def pieces_first(rows):
            return rows.reshape(2, half_tok, kv_heads, group_size, head_dim).transpose(2, 0, 3, 1, 4)

        def chip_rows(x, g, axis=0):
            return jnp.concatenate([pick(x, g, True), swap(pick(x, g, False), 1)], axis=axis)

        kv_rows = jnp.stack([key_rows, value_rows]).reshape(2, 2, half_tok, kv_heads, head_dim).transpose(3, 0, 1, 2, 4)
        kv_chip = [chip_rows(kv_rows, g, axis=1) for g in range(n_grp)]
        kv_far = [swap(kv_chip[g], 6) for g in range(n_grp)]
        kv_near = [jnp.concatenate([swap(kv_chip[g], 2), swap(kv_chip[g], 4)], axis=1) for g in range(n_grp)]

        q_pf, do_pf = pieces_first(query_rows), pieces_first(grad_out)
        q_pf, do_pf = lax.optimization_barrier((q_pf, do_pf))
        delta = jnp.einsum('thd,thd->th', grad_out, out_rows, preferred_element_type=F32)

        def stat_first(stat):
            return stat.reshape(2, half_tok, kv_heads, group_size).transpose(2, 0, 3, 1)

        stats = jnp.stack([stat_first(log_sum_exp * math.sqrt(head_dim)), stat_first(delta)], axis=1)
        tables = {name: jnp.asarray(task_table(n_ctx, peers))[ctx_rank] for name, peers in (('own', (0,)), ('far', (3,)), ('near', (1, 2)))}

        dq_all, dkv_all = q_pf, kv_rows
        for g in range(n_grp):
            q = chip_rows(q_pf, g)
            do = chip_rows(do_pf, g)
            stat = chip_rows(stats, g, axis=1)
            rows = (q, do, lane_parts(stat[0], stat[1]))

            def run(kind, kv, dq_in, is_end):
                return block_call(tables[kind], *rows, kv, dq_in, is_end, kind == 'own')

            last = g == n_grp - 1
            dq = None
            if not last:
                dq, dkv_own = run('own', kv_chip[g], None, False)
            dq, dkv_far = run('far', kv_far[g], dq, False)
            dq, dkv_x, dkv_y = run('near', kv_near[g], dq, not last)
            if last:
                dq, dkv_own = run('own', kv_chip[g], dq, True)
            dkv = dkv_own + swap(dkv_far, 6) + swap(dkv_x, 2) + swap(dkv_y, 4)
            dkv = dkv.astype(BF16)
            dq_all = lax.dynamic_update_index_in_dim(dq_all, dq[:2], core * n_grp + g, 0)
            dq_all = lax.dynamic_update_index_in_dim(dq_all, swap(dq[2:], 1), (1 - core) * n_grp + g, 0)
            dkv_all = lax.dynamic_update_index_in_dim(dkv_all, dkv[:, :2], core * n_grp + g, 0)
            dkv_all = lax.dynamic_update_index_in_dim(dkv_all, swap(dkv[:, 2:], 1), (1 - core) * n_grp + g, 0)

        grad_query = dq_all.transpose(1, 3, 0, 2, 4).reshape(tok_dev, n_heads, head_dim)
        grad_kv = dkv_all.transpose(1, 2, 3, 0, 4).reshape(2, tok_dev, kv_heads, head_dim)
        return grad_query, grad_kv[0], grad_kv[1]

    return jax.shard_map(local_grads, mesh=mesh, in_specs=(row_spec, row_spec, row_spec, row_spec, row_spec, stat_spec), out_specs=(row_spec, row_spec, row_spec), check_vma=False)
```

time: 678 us -> 551 us (0.81)
  waiting for transfers between devices: 165 us -> 79.2 us
  local copies, waits for them, and re-layouts: 106 us -> 51 us
  other arithmetic: 34.8 us -> 45.4 us
    ppermute x24, waiting for transfers between devices: 165 us -> 79.2 us  [swap(): return lax.ppermute(x, ctx_axes, [(dev, dev ^ bit) for dev in range(n_ctx)])]
    dynamic_update_slice x5 -> x4, local copies, waits for them, and re-layouts: 29 us -> 0.28 us  [the longest x2 0.14 us: local_grads(): lax.dynamic_update_index_in_dim(dkv_all, swap(dkv[:, 2:], 1), (1 - core)...]
    broadcast_in_dim x7 -> x0, local copies, waits for them, and re-layouts: 25.4 us -> none  [the longest x4 16.8 us: lanes(): return jnp.broadcast_to(stat[..., None], stat.shape + (128,))]
    convert_element_type x1 -> x3, other arithmetic: 5.62 us -> 16.7 us  [the longest x1 10 us: lane_parts(): return jnp.where(lane < 2 * N_PART, out, 0.0).astype(BF16)]
    dynamic_update_slice x3 -> x1, local copies, waits for them, and re-layouts: 9.81 us -> 1.39 us  [local_grads(): lax.dynamic_update_index_in_dim(dq_all, dq[:2], core * n_grp + g, 0)]
    transpose x0 -> x1, local copies, waits for them, and re-layouts: none -> 6.99 us  [local_grads(): dq_all.transpose(1, 3, 0, 2, 4).reshape(tok_dev, n_heads, head_dim)]
    squeeze x4 -> x5, local copies, waits for them, and re-layouts: 13.9 us -> 15.9 us  [pick(): return lax.dynamic_index_in_dim(x, sel * n_grp + g, axis=0, keepdims=False)]
  transfers between devices with their start and end apart: 24 -> 24, of which waited for: 7 -> 7; matrix products, arithmetic and copies ran while one was open for 14% -> 14% of each run, Pallas kernels for 51% -> 64%
where the time goes in v4:
time: 551 us; the launch traced here: 544 us
  Pallas kernels  348 us (63%)
  waiting for transfers between devices  79.2 us (14%)
  local copies, waits for them, and re-layouts  51 us (9%)
  other arithmetic  45.4 us (8%)
  starting transfers between devices  18.9 us (3%)
    pallas_call x6, Pallas kernels, block_call(): pl.pallas_call(functools.partial(block_kernel, has_in, is_end, has_diag,...  348 us
    ppermute x24, waiting for transfers between devices, swap(): return lax.ppermute(x, ctx_axes, [(dev, dev ^ bit) for dev in range(n_ctx)])  79.2 us
    ppermute x24, starting transfers between devices, swap(): return lax.ppermute(x, ctx_axes, [(dev, dev ^ bit) for dev in range(n_ctx)])  18.9 us
    squeeze x5, local copies, waits for them, and re-layouts, pick(): return lax.dynamic_index_in_dim(x, sel * n_grp + g, axis=0, keepdims=False)  15.9 us
    concatenate x6, other arithmetic, chip_rows(): jnp.concatenate([pick(x, g, True), swap(pick(x, g, False), 1)], axis=axis)  13.6 us
  transfers between devices with their start and end apart: 24, of which 7 were waited for; matrix products, arithmetic and copies ran while one was open for 14% of the time, Pallas kernels for 64%

profile of v4, /device:TPU:0, one launch (start us, length us, event | category | flops | bytes accessed | tf_op | source)
XLA Modules:
  0.0 544.3 jit_solution(3033832336351574575)
XLA Ops:
  0.7 10.7 %copy_bitcast_fusion = (bf16[4,2,7,512,128]{4,3,2,1,0:T(8,128)(2,1)}, bf16[4,2,7,512,128]{4,3,2,1,0:T(8,128)(2,1)}) fusion(bf16[2,512,4,7,128]{4,1,0,3,2:T(8,128)(2,1)} %bitcast.92, bf16[2,512,4,7,128]{4,1,0,3,2:T(8,128)(2,1)} %bitcast.95), kind=kLoop, calls=%fused_computation.18 | loop fusion | bytes 29360128 | tf_op jit(solution)/shard_map/transpose | solution.py:207
  11.4 4.3 dynamic-slice_bitcast_fusion.7
  15.7 0.8 collective-permute-start
  16.5 5.8 %dynamic-slice_bitcast_fusion.1 = (bf16[2,7,512,128]{3,2,1,0:T(8,128)(2,1)S(1)}, bf16[2,7,512,128]{3,2,1,0:T(8,128)(2,1)}, bf16[2,7,512,128]{3,2,1,0:T(8,128)(2,1)}, bf16[2,7,512,128]{3,2,1,0:T(8,128)(2,1)}) fusion(bf16[4,2,7,512,128]{4,3,2,1,0:T(8,128)(2,1)} %get-tuple-element.20, s32[]{:T(128)S(6)} %select_n.103, s32[]{:T(128)S(6)} %select_n.104, ...), kind=kLoop, calls=%fused_computation.33 | loop fusion | bytes 14680080 | tf_op jit(solution)/shard_map/jit(dynamic_index_in_dim)/squeeze | solution.py:204
  22.4 9.1 %fusion = f32[1024,28]{0,1:T(8,128)S(1)} fusion(bf16[1024,28,128]{2,0,1:T(8,128)(2,1)} %param.13, bf16[1024,28,128]{2,0,1:T(8,128)(2,1)} %param.12), kind=kLoop, calls=%fused_computation.1 | loop fusion | flops 14651392 | bytes 14794752 | tf_op jit(solution)/shard_map/thd,thd->th/dot_general | solution.py:219
  31.5 0.1 reshape.46
  31.6 0.1 fusion.20
  31.8 0.6 copy.42
  32.4 0.5 collective-permute-start.10
  32.9 0.6 copy.43
  33.6 0.1 copy_dynamic-update-slice_fusion.1
  33.7 0.3 copy_dynamic-update-slice_fusion
  34.0 1.3 dynamic-slice_bitcast_fusion.9
  35.3 0.4 copy-done
  35.7 0.5 collective-permute-start.3
  36.2 0.6 iota_remainder_fusion
  36.8 0.6 compare_and_fusion
  37.4 0.7 fusion.21
  38.0 0.1 copy.20.tab_ref
  38.1 0.7 fusion.22
  38.8 0.1 copy.19.tab_ref
  38.9 0.7 fusion.23
  39.6 0.1 copy.18.tab_ref
  39.8 0.8 fusion.12
  40.6 0.8 fusion.14
  41.5 3.0 collective-permute-start.5
  44.5 1.5 collective-permute-start.4
  46.1 10.0 %fusion.8 = (bf16[4,7,512,128]{3,2,1,0:T(8,128)(2,1)}, bf16[4,7,512,128]{3,2,1,0:T(8,128)(2,1)}) fusion(f32[4,7,512]{2,1,0:T(8,128)S(1)} %get-tuple-element.55, f32[4,7,512]{2,1,0:T(8,128)S(1)} %get-tuple-element.54, s32[128]{0:T(128)S(1)} %copy-done.10, s32[128]{0:T(128)S(1)} %copy-done.11, pred[128]{0:T(512)(128)(4,1)S(1)} %copy-done.13, ...), kind=kLoop, calls=%fused_computation.17 | loop fusion | flops 42205184 | bytes 7570816 | tf_op jit(solution)/shard_map/convert_element_type | solution.py:180
  56.1 11.8 %collective-permute-done.5 = bf16[2,4,512,128]{3,2,1,0:T(8,128)(2,1)S(1)} collective-permute-done((bf16[2,4,512,128]{3,2,1,0:T(8,128)(2,1)S(1)}, bf16[2,4,512,128]{3,2,1,0:T(8,128)(2,1)S(1)}, u32[]{:S(2)}, u32[]{:S(2)}) %collective-permute-start.5) | collective-permute-done | bytes 1048608 | tf_op jit(solution)/shard_map/ppermute | solution.py:191
  67.9 1.4 collective-permute-done.4
  69.3 1.4 collective-permute-start.6
  70.8 1.5 pad_maximum_fusion.4.k_ref.v_ref
  72.3 3.8 pad_maximum_fusion.q_ref
  76.1 3.7 pad_maximum_fusion.1.do_ref
  79.9 44.3 %shard_map.112 = (f32[4,7,128,512]{3,2,1,0:T(8,128)}, f32[2,4,512,128]{3,2,1,0:T(8,128)S(1)}) custom-call(s32[10,5]{1,0:T(8,128)S(1)} %copy.18.tab_ref, bf16[4,7,512,128]{3,2,1,0:T(8,128)(2,1)} %pad_maximum_fusion.q_ref, bf16[4,7,512,128]{3,2,1,0:T(8,128)(2,1)} %pad_maximum_fusion.1.do_ref, bf16[4,7,512,128]{3,2,1,0:T(8,128)(2,1)} %get-tuple-element.59.aug_ref, ...), custom_call_target="tpu_custom_call" | custom-call | flops 18790481920 | bytes 33554432 | tf_op jit(solution)/shard_map/pallas_call | solution.py:148
  124.2 45.7 %shard_map.113 = (f32[4,7,128,512]{3,2,1,0:T(8,128)}, f32[2,4,512,128]{3,2,1,0:T(8,128)S(1)}) custom-call(s32[10,5]{1,0:T(8,128)S(1)} %copy.19.tab_ref, bf16[4,7,512,128]{3,2,1,0:T(8,128)(2,1)} %pad_maximum_fusion.q_ref, bf16[4,7,512,128]{3,2,1,0:T(8,128)(2,1)} %pad_maximum_fusion.1.do_ref, bf16[4,7,512,128]{3,2,1,0:T(8,128)(2,1)} %get-tuple-element.59.aug_ref, ...), custom_call_target="tpu_custom_call" | custom-call | flops 18790481920 | bytes 33554432 | tf_op jit(solution)/shard_map/pallas_call | solution.py:148
  169.9 84.0 %shard_map.114 = (bf16[4,7,512,128]{3,2,1,0:T(8,128)(2,1)}, f32[2,4,512,128]{3,2,1,0:T(8,128)S(1)}, f32[2,4,512,128]{3,2,1,0:T(8,128)}) custom-call(s32[18,5]{1,0:T(8,128)S(1)} %copy.20.tab_ref, bf16[4,7,512,128]{3,2,1,0:T(8,128)(2,1)} %pad_maximum_fusion.q_ref, bf16[4,7,512,128]{3,2,1,0:T(8,128)(2,1)} %pad_maximum_fusion.1.do_ref, ...), custom_call_target="tpu_custom_call" | custom-call | flops 37580963840 | bytes 33554432 | tf_op jit(solution)/shard_map/pallas_call | solution.py:148
  253.9 4.5 dynamic-slice_bitcast_fusion.3
  258.6 3.4 collective-permute-start.14
  262.0 22.1 %collective-permute-done.13 = bf16[2,4,512,128]{3,2,1,0:T(8,128)(2,1)S(1)} collective-permute-done((bf16[2,4,512,128]{3,2,1,0:T(8,128)(2,1)S(1)}, bf16[2,4,512,128]{3,2,1,0:T(8,128)(2,1)S(1)}, u32[]{:S(2)}, u32[]{:S(2)}) %collective-permute-start.13) | collective-permute-done | bytes 1048608 | tf_op jit(solution)/shard_map/ppermute | solution.py:191
  284.1 0.5 collective-permute-done.12
  284.6 1.5 pad_maximum_fusion.5.k_ref.v_ref
  286.2 1.4 slice.47
  287.5 2.0 collective-permute-start.18
  289.5 3.7 pad_maximum_fusion.3.do_ref
  293.2 1.5 collective-permute-start.16
  294.7 2.2 pad_maximum_fusion.2.q_ref
  296.9 11.7 %collective-permute-done.14.k_ref.v_ref = bf16[2,4,512,128]{3,2,1,0:T(8,128)(2,1)S(1)} collective-permute-done((bf16[2,4,512,128]{3,2,1,0:T(8,128)(2,1)S(1)}, bf16[2,4,512,128]{3,2,1,0:T(8,128)(2,1)S(1)}, u32[]{:S(2)}, u32[]{:S(2)}) %collective-permute-start.14) | collective-permute-done | bytes 1048608 | tf_op jit(solution)/shard_map/ppermute | solution.py:191
  308.6 43.4 %shard_map.115 = (f32[4,7,128,512]{3,2,1,0:T(8,128)}, f32[2,4,512,128]{3,2,1,0:T(8,128)S(1)}) custom-call(s32[10,5]{1,0:T(8,128)S(1)} %copy.19.tab_ref, bf16[4,7,512,128]{3,2,1,0:T(8,128)(2,1)} %pad_maximum_fusion.2.q_ref, bf16[4,7,512,128]{3,2,1,0:T(8,128)(2,1)} %pad_maximum_fusion.3.do_ref, bf16[4,7,512,128]{3,2,1,0:T(8,128)(2,1)} %get-tuple-element.58.aug_ref, ...), custom_call_target="tpu_custom_call" | custom-call | flops 18790481920 | bytes 33554432 | tf_op jit(solution)/shard_map/pallas_call | solution.py:148
  352.0 83.6 %shard_map.116 = (f32[4,7,128,512]{3,2,1,0:T(8,128)}, f32[2,4,512,128]{3,2,1,0:T(8,128)}, f32[2,4,512,128]{3,2,1,0:T(8,128)}) custom-call(s32[18,5]{1,0:T(8,128)S(1)} %copy.20.tab_ref, bf16[4,7,512,128]{3,2,1,0:T(8,128)(2,1)} %pad_maximum_fusion.2.q_ref, bf16[4,7,512,128]{3,2,1,0:T(8,128)(2,1)} %pad_maximum_fusion.3.do_ref, ...), custom_call_target="tpu_custom_call" | custom-call | flops 37580963840 | bytes 33554432 | tf_op jit(solution)/shard_map/pallas_call | solution.py:148
  435.7 3.4 collective-permute-start.20
  439.1 47.2 %shard_map.117 = (bf16[4,7,512,128]{3,2,1,0:T(8,128)(2,1)}, f32[2,4,512,128]{3,2,1,0:T(8,128)S(1)}) custom-call(s32[10,5]{1,0:T(8,128)S(1)} %copy.18.tab_ref, bf16[4,7,512,128]{3,2,1,0:T(8,128)(2,1)} %pad_maximum_fusion.2.q_ref, bf16[4,7,512,128]{3,2,1,0:T(8,128)(2,1)} %pad_maximum_fusion.3.do_ref, bf16[4,7,512,128]{3,2,1,0:T(8,128)(2,1)} %get-tuple-element.58.aug_ref, ...), custom_call_target="tpu_custom_call" | custom-call | flops 18790481920 | bytes 33554432 | tf_op jit(solution)/shard_map/pallas_call | solution.py:148
  486.3 1.6 slice.51
  488.0 2.9 bitcast_dynamic-update-slice_fusion.2
  490.9 3.4 add_convert_fusion.1
  494.4 0.6 collective-permute-start.19
  495.0 1.4 bitcast_dynamic-update-slice_fusion.1
  496.6 31.6 %collective-permute-done.20 = f32[2,4,512,128]{3,2,1,0:T(8,128)} collective-permute-done((f32[2,4,512,128]{3,2,1,0:T(8,128)S(1)}, f32[2,4,512,128]{3,2,1,0:T(8,128)}, u32[]{:S(2)}, u32[]{:S(2)}) %collective-permute-start.20) | collective-permute-done | bytes 2097184 | tf_op jit(solution)/shard_map/ppermute | solution.py:191
  528.2 3.3 add_convert_fusion
  531.6 1.4 bitcast_dynamic-update-slice_fusion
  533.0 7.0 %copy.26 = bf16[2,512,4,7,128]{4,1,0,3,2:T(8,128)(2,1)} copy(bf16[2,512,4,7,128]{4,1,3,0,2:T(8,128)(2,1)} %bitcast.37) | data formatting | bytes 14680064 | tf_op jit(solution)/shard_map/transpose | solution.py:252
  540.2 0.1 fusion.24
  540.3 1.8 copy.27
  542.1 1.8 copy.28
  (70 shorter events, 1.1 us)
Async XLA Ops:
  15.7 56.6 %collective-permute-start = (bf16[2,7,512,128]{3,2,1,0:T(8,128)(2,1)}, bf16[2,7,512,128]{3,2,1,0:T(8,128)(2,1)}, u32[]{:S(2)}, u32[]{:S(2)}) collective-permute-start(bf16[2,7,512,128]{3,2,1,0:T(8,128)(2,1)} %get-tuple-element.43), channel_id=1, source_target_pairs={{0,1},{1,0},{2,3},{3,2},{4,5},{5,4},{6,7},{7,6}} | collective-permute-start | bytes 5505032 | tf_op jit(solution)/shard_map/ppermute | solution.py:191
  16.5 5.8 %copy-start.9 = (f32[1024,28]{0,1:T(8,128)S(1)}, f32[1024,28]{0,1:T(8,128)}, u32[]{:S(2)}) copy-start(f32[1024,28]{0,1:T(8,128)} %param.14) | copy-start | bytes 344068
  22.3 53.8 %collective-permute-start.1 = (bf16[2,7,512,128]{3,2,1,0:T(8,128)(2,1)}, bf16[2,7,512,128]{3,2,1,0:T(8,128)(2,1)}, u32[]{:S(2)}, u32[]{:S(2)}) collective-permute-start(bf16[2,7,512,128]{3,2,1,0:T(8,128)(2,1)} %get-tuple-element.37), channel_id=1, source_target_pairs={{0,1},{1,0},{2,3},{3,2},{4,5},{5,4},{6,7},{7,6}} | collective-permute-start | bytes 5505032 | tf_op jit(solution)/shard_map/ppermute | solution.py:191
  22.4 11.2 %copy-start.6 = (bf16[1024,4,128]{2,1,0:T(4,128)(2,1)S(1)}, bf16[1024,4,128]{2,1,0:T(4,128)(2,1)}, u32[]{:S(2)}) copy-start(bf16[1024,4,128]{2,1,0:T(4,128)(2,1)} %param.10) | copy-start | bytes 3145732
  31.6 2.1 copy-start.7
  32.4 7.3 %collective-permute-start.10 = (f32[2,2,7,512]{3,2,1,0:T(8,128)}, f32[2,2,7,512]{3,2,1,0:T(8,128)}, u32[]{:S(2)}, u32[]{:S(2)}) collective-permute-start(f32[2,2,7,512]{3,2,1,0:T(8,128)} %bitcast.90), channel_id=1, source_target_pairs={{0,1},{1,0},{2,3},{3,2},{4,5},{5,4},{6,7},{7,6}} | collective-permute-start | bytes 172040 | tf_op jit(solution)/shard_map/ppermute | solution.py:191
  33.6 7.0 %collective-permute-start.2 = (f32[2,2,7,512]{3,2,1,0:T(8,128)}, f32[2,2,7,512]{3,2,1,0:T(8,128)}, u32[]{:S(2)}, u32[]{:S(2)}) collective-permute-start(f32[2,2,7,512]{3,2,1,0:T(8,128)} %bitcast.91), channel_id=1, source_target_pairs={{0,1},{1,0},{2,3},{3,2},{4,5},{5,4},{6,7},{7,6}} | collective-permute-start | bytes 172040 | tf_op jit(solution)/shard_map/ppermute | solution.py:191
  34.0 1.7 copy-start
  35.7 5.7 %collective-permute-start.3 = (bf16[2,2,512,128]{3,2,1,0:T(8,128)(2,1)}, bf16[2,2,512,128]{3,2,1,0:T(8,128)(2,1)S(1)}, u32[]{:S(2)}, u32[]{:S(2)}) collective-permute-start(bf16[2,2,512,128]{3,2,1,0:T(8,128)(2,1)} %get-tuple-element.48), channel_id=1, source_target_pairs={{0,1},{1,0},{2,3},{3,2},{4,5},{5,4},{6,7},{7,6}} | collective-permute-start | bytes 1572872 | tf_op jit(solution)/shard_map/ppermute | solution.py:191
  39.7 6.3 %copy-start.10 = (s32[128]{0:T(128)S(1)}, s32[128]{0:T(128)}, u32[]{:S(2)}) copy-start(s32[128]{0:T(128)} %get-tuple-element.66) | copy-start | bytes 1540
  39.7 6.3 %copy-start.11 = (s32[128]{0:T(128)S(1)}, s32[128]{0:T(128)}, u32[]{:S(2)}) copy-start(s32[128]{0:T(128)} %get-tuple-element.67) | copy-start | bytes 1540
  39.7 6.3 %copy-start.12 = (pred[128]{0:T(512)(128)(4,1)S(1)}, pred[128]{0:T(512)(128)(4,1)}, u32[]{:S(2)}) copy-start(pred[128]{0:T(512)(128)(4,1)} %get-tuple-element.64) | copy-start | bytes 388
  39.7 6.3 %copy-start.13 = (pred[128]{0:T(512)(128)(4,1)S(1)}, pred[128]{0:T(512)(128)(4,1)}, u32[]{:S(2)}) copy-start(pred[128]{0:T(512)(128)(4,1)} %get-tuple-element.65) | copy-start | bytes 388
  39.8 249.8 %collective-permute-start.9 = (bf16[2,7,512,128]{3,2,1,0:T(8,128)(2,1)}, bf16[2,7,512,128]{3,2,1,0:T(8,128)(2,1)}, u32[]{:S(2)}, u32[]{:S(2)}) collective-permute-start(bf16[2,7,512,128]{3,2,1,0:T(8,128)(2,1)} %get-tuple-element.36), channel_id=1, source_target_pairs={{0,1},{1,0},{2,3},{3,2},{4,5},{5,4},{6,7},{7,6}} | collective-permute-start | bytes 5505032 | tf_op jit(solution)/shard_map/ppermute | solution.py:191
  41.5 26.4 %collective-permute-start.5 = (bf16[2,4,512,128]{3,2,1,0:T(8,128)(2,1)S(1)}, bf16[2,4,512,128]{3,2,1,0:T(8,128)(2,1)S(1)}, u32[]{:S(2)}, u32[]{:S(2)}) collective-permute-start(bf16[2,4,512,128]{3,2,1,0:T(8,128)(2,1)S(1)} %pad_maximum_fusion.6.k_ref.v_ref), channel_id=1, source_target_pairs={{0,4},{1,5},{2,6},{3,7},{4,0},{5,1},{6,2},{7,3}} | collective-permute-start | bytes 3145736 | tf_op jit(solution)/shard_map/ppermute | solution.py:191
  44.5 24.8 %collective-permute-start.4 = (bf16[2,4,512,128]{3,2,1,0:T(8,128)(2,1)S(1)}, bf16[2,4,512,128]{3,2,1,0:T(8,128)(2,1)S(1)}, u32[]{:S(2)}, u32[]{:S(2)}) collective-permute-start(bf16[2,4,512,128]{3,2,1,0:T(8,128)(2,1)S(1)} %pad_maximum_fusion.6.k_ref.v_ref), channel_id=1, source_target_pairs={{0,2},{1,3},{2,0},{3,1},{4,6},{5,7},{6,4},{7,5}} | collective-permute-start | bytes 3145736 | tf_op jit(solution)/shard_map/ppermute | solution.py:191
  46.0 21.8 %copy-start.8 = (bf16[2,2,512,128]{3,2,1,0:T(8,128)(2,1)S(1)}, bf16[2,2,512,128]{3,2,1,0:T(8,128)(2,1)}, u32[]{:S(2)}) copy-start(bf16[2,2,512,128]{3,2,1,0:T(8,128)(2,1)} %get-tuple-element.47) | copy-start | bytes 1572868
  67.9 4.4 copy-start.2
  67.9 190.5 %collective-permute-start.11 = (bf16[2,2,512,128]{3,2,1,0:T(8,128)(2,1)S(1)}, bf16[2,2,512,128]{3,2,1,0:T(8,128)(2,1)S(1)}, u32[]{:S(2)}, u32[]{:S(2)}) collective-permute-start(bf16[2,2,512,128]{3,2,1,0:T(8,128)(2,1)S(1)} %copy-done.8), channel_id=1, source_target_pairs={{0,1},{1,0},{2,3},{3,2},{4,5},{5,4},{6,7},{7,6}} | collective-permute-start | bytes 1572872 | tf_op jit(solution)/shard_map/ppermute | solution.py:191
  69.3 54.8 %collective-permute-start.6 = (bf16[2,4,512,128]{3,2,1,0:T(8,128)(2,1)S(1)}, bf16[2,4,512,128]{3,2,1,0:T(8,128)(2,1)S(1)}, u32[]{:S(2)}, u32[]{:S(2)}) collective-permute-start(bf16[2,4,512,128]{3,2,1,0:T(8,128)(2,1)S(1)} %pad_maximum_fusion.6.k_ref.v_ref), channel_id=1, source_target_pairs={{0,6},{1,7},{2,4},{3,5},{4,2},{5,3},{6,0},{7,1}} | collective-permute-start | bytes 3145736 | tf_op jit(solution)/shard_map/ppermute | solution.py:191
  72.3 3.8 copy-start.3
  258.4 34.8 %collective-permute-start.8 = (bf16[2,7,512,128]{3,2,1,0:T(8,128)(2,1)S(1)}, bf16[2,7,512,128]{3,2,1,0:T(8,128)(2,1)S(1)}, u32[]{:S(2)}, u32[]{:S(2)}) collective-permute-start(bf16[2,7,512,128]{3,2,1,0:T(8,128)(2,1)S(1)} %get-tuple-element.40), channel_id=1, source_target_pairs={{0,1},{1,0},{2,3},{3,2},{4,5},{5,4},{6,7},{7,6}} | collective-permute-start | bytes 5505032 | tf_op jit(solution)/shard_map/ppermute | solution.py:191
  258.5 27.6 %copy-start.5 = (bf16[4,7,512,128]{3,2,1,0:T(8,128)(2,1)S(1)}, bf16[4,7,512,128]{3,2,1,0:T(8,128)(2,1)}, u32[]{:S(2)}) copy-start(bf16[4,7,512,128]{3,2,1,0:T(8,128)(2,1)} %get-tuple-element.23) | copy-start | bytes 11010052
  258.5 25.6 %collective-permute-start.13 = (bf16[2,4,512,128]{3,2,1,0:T(8,128)(2,1)S(1)}, bf16[2,4,512,128]{3,2,1,0:T(8,128)(2,1)S(1)}, u32[]{:S(2)}, u32[]{:S(2)}) collective-permute-start(bf16[2,4,512,128]{3,2,1,0:T(8,128)(2,1)S(1)} %pad_maximum_fusion.7.k_ref.v_ref), channel_id=1, source_target_pairs={{0,4},{1,5},{2,6},{3,7},{4,0},{5,1},{6,2},{7,3}} | collective-permute-start | bytes 3145736 | tf_op jit(solution)/shard_map/ppermute | solution.py:191
  258.6 26.1 %collective-permute-start.12 = (bf16[2,4,512,128]{3,2,1,0:T(8,128)(2,1)S(1)}, bf16[2,4,512,128]{3,2,1,0:T(8,128)(2,1)S(1)}, u32[]{:S(2)}, u32[]{:S(2)}) collective-permute-start(bf16[2,4,512,128]{3,2,1,0:T(8,128)(2,1)S(1)} %pad_maximum_fusion.7.k_ref.v_ref), channel_id=1, source_target_pairs={{0,2},{1,3},{2,0},{3,1},{4,6},{5,7},{6,4},{7,5}} | collective-permute-start | bytes 3145736 | tf_op jit(solution)/shard_map/ppermute | solution.py:191
  258.6 50.0 %collective-permute-start.14 = (bf16[2,4,512,128]{3,2,1,0:T(8,128)(2,1)S(1)}, bf16[2,4,512,128]{3,2,1,0:T(8,128)(2,1)S(1)}, u32[]{:S(2)}, u32[]{:S(2)}) collective-permute-start(bf16[2,4,512,128]{3,2,1,0:T(8,128)(2,1)S(1)} %pad_maximum_fusion.7.k_ref.v_ref), channel_id=1, source_target_pairs={{0,6},{1,7},{2,4},{3,5},{4,2},{5,3},{6,0},{7,1}} | collective-permute-start | bytes 3145736 | tf_op jit(solution)/shard_map/ppermute | solution.py:191
  287.5 148.1 %collective-permute-start.7 = (bf16[2,7,512,128]{3,2,1,0:T(8,128)(2,1)}, bf16[2,7,512,128]{3,2,1,0:T(8,128)(2,1)}, u32[]{:S(2)}, u32[]{:S(2)}) collective-permute-start(bf16[2,7,512,128]{3,2,1,0:T(8,128)(2,1)} %slice.47), channel_id=1, source_target_pairs={{0,1},{1,0},{2,3},{3,2},{4,5},{5,4},{6,7},{7,6}} | collective-permute-start | bytes 5505032 | tf_op jit(solution)/shard_map/ppermute | solution.py:191
  287.5 148.2 %collective-permute-start.18 = (f32[2,4,512,128]{3,2,1,0:T(8,128)}, f32[2,4,512,128]{3,2,1,0:T(8,128)}, u32[]{:S(2)}, u32[]{:S(2)}) collective-permute-start(f32[2,4,512,128]{3,2,1,0:T(8,128)} %get-tuple-element.30), channel_id=1, source_target_pairs={{0,4},{1,5},{2,6},{3,7},{4,0},{5,1},{6,2},{7,3}} | collective-permute-start | bytes 6291464 | tf_op jit(solution)/shard_map/ppermute | solution.py:191
  289.5 198.4 %collective-permute-start.17 = (f32[2,4,512,128]{3,2,1,0:T(8,128)S(1)}, f32[2,4,512,128]{3,2,1,0:T(8,128)}, u32[]{:S(2)}, u32[]{:S(2)}) collective-permute-start(f32[2,4,512,128]{3,2,1,0:T(8,128)S(1)} %get-tuple-element.29), channel_id=1, source_target_pairs={{0,2},{1,3},{2,0},{3,1},{4,6},{5,7},{6,4},{7,5}} | collective-permute-start | bytes 6291464 | tf_op jit(solution)/shard_map/ppermute | solution.py:191
  293.2 197.7 %collective-permute-start.16 = (f32[2,4,512,128]{3,2,1,0:T(8,128)S(1)}, f32[2,4,512,128]{3,2,1,0:T(8,128)}, u32[]{:S(2)}, u32[]{:S(2)}) collective-permute-start(f32[2,4,512,128]{3,2,1,0:T(8,128)S(1)} %get-tuple-element.28), channel_id=1, source_target_pairs={{0,6},{1,7},{2,4},{3,5},{4,2},{5,3},{6,0},{7,1}} | collective-permute-start | bytes 6291464 | tf_op jit(solution)/shard_map/ppermute | solution.py:191
  435.6 61.0 %collective-permute-start.22 = (f32[2,4,512,128]{3,2,1,0:T(8,128)}, f32[2,4,512,128]{3,2,1,0:T(8,128)}, u32[]{:S(2)}, u32[]{:S(2)}) collective-permute-start(f32[2,4,512,128]{3,2,1,0:T(8,128)} %get-tuple-element.34), channel_id=1, source_target_pairs={{0,4},{1,5},{2,6},{3,7},{4,0},{5,1},{6,2},{7,3}} | collective-permute-start | bytes 6291464 | tf_op jit(solution)/shard_map/ppermute | solution.py:191
  435.7 60.9 %collective-permute-start.21 = (f32[2,4,512,128]{3,2,1,0:T(8,128)}, f32[2,4,512,128]{3,2,1,0:T(8,128)}, u32[]{:S(2)}, u32[]{:S(2)}) collective-permute-start(f32[2,4,512,128]{3,2,1,0:T(8,128)} %get-tuple-element.33), channel_id=1, source_target_pairs={{0,2},{1,3},{2,0},{3,1},{4,6},{5,7},{6,4},{7,5}} | collective-permute-start | bytes 6291464 | tf_op jit(solution)/shard_map/ppermute | solution.py:191
  435.7 92.5 %collective-permute-start.20 = (f32[2,4,512,128]{3,2,1,0:T(8,128)S(1)}, f32[2,4,512,128]{3,2,1,0:T(8,128)}, u32[]{:S(2)}, u32[]{:S(2)}) collective-permute-start(f32[2,4,512,128]{3,2,1,0:T(8,128)S(1)} %get-tuple-element.32), channel_id=1, source_target_pairs={{0,6},{1,7},{2,4},{3,5},{4,2},{5,3},{6,0},{7,1}} | collective-permute-start | bytes 6291464 | tf_op jit(solution)/shard_map/ppermute | solution.py:191
  488.0 43.6 %collective-permute-start.15 = (bf16[2,7,512,128]{3,2,1,0:T(8,128)(2,1)S(1)}, bf16[2,7,512,128]{3,2,1,0:T(8,128)(2,1)S(1)}, u32[]{:S(2)}, u32[]{:S(2)}) collective-permute-start(bf16[2,7,512,128]{3,2,1,0:T(8,128)(2,1)S(1)} %slice.51), channel_id=1, source_target_pairs={{0,1},{1,0},{2,3},{3,2},{4,5},{5,4},{6,7},{7,6}} | collective-permute-start | bytes 5505032 | tf_op jit(solution)/shard_map/ppermute | solution.py:191
  490.9 4.1 copy-start.4
  494.4 2.0 copy-start.1
  494.4 2.1 collective-permute-start.19
  531.6 8.5 %collective-permute-start.23 = (bf16[2,2,512,128]{3,2,1,0:T(8,128)(2,1)S(1)}, bf16[2,2,512,128]{3,2,1,0:T(8,128)(2,1)S(1)}, u32[]{:S(2)}, u32[]{:S(2)}) collective-permute-start(bf16[2,2,512,128]{3,2,1,0:T(8,128)(2,1)S(1)} %slice.65), channel_id=1, source_target_pairs={{0,1},{1,0},{2,3},{3,2},{4,5},{5,4},{6,7},{7,6}} | collective-permute-start | bytes 1572872 | tf_op jit(solution)/shard_map/ppermute | solution.py:191

commit v5 on v4

--- a/solution.py
+++ b/solution.py
@@ -12,7 +12,7 @@
 F32 = jnp.float32
 BF16 = jnp.bfloat16
 Q_TILE = 256
-FULL_TILE = 512
+FULL_TILE = 256
 N_PART = 3
 
 
@@ -40,7 +40,8 @@
     return np.array(tables, np.int32)
 
 
-def block_kernel(has_in, is_end, has_diag, n_peer, tab_ref, q_ref, do_ref, aug_ref, k_ref, v_ref, *refs):
+def block_kernel(has_in, is_end, has_diag, n_peer, tab_ref, q_ref, do_ref, aug_ref, *refs):
+    kv_refs, refs = refs[:2 * n_peer], refs[2 * n_peer:]
     if has_in:
         dqi_ref, *refs = refs
     dq_ref, *refs = refs
@@ -61,15 +62,14 @@
         kt_scr[head_dim:, :] = jnp.where(row_id < N_PART, -1.0, 0.0).astype(BF16)
         vt_scr[head_dim:, :] = jnp.where((row_id >= N_PART) & (row_id < 2 * N_PART), -1.0, 0.0).astype(BF16)
 
-    if has_in:
-        @pl.when(is_first == 1)
-        def _():
-            dq_acc[...] = dqi_ref[...]
-
     def run_task(masked):
         tile = Q_TILE if masked else FULL_TILE
-        kt_scr[:head_dim, :] = k_ref[...].T
-        vt_scr[:head_dim, :] = v_ref[...].T
+        k_blk, v_blk = kv_refs[0][...], kv_refs[1][...]
+        if n_peer == 2:
+            k_blk = jnp.where(k_slot < 4, k_blk, kv_refs[2][...])
+            v_blk = jnp.where(k_slot < 4, v_blk, kv_refs[3][...])
+        kt_scr[:head_dim, :] = k_blk.T
+        vt_scr[:head_dim, :] = v_blk.T
         fresh = is_first == 1
 
         def scores(h, sub, slot):
@@ -93,7 +93,7 @@
             ds = ds_scr[slot, :tile, :n_key]
             dkv_acc[k_slot, 1, :, :n_key] += lax.dot_general(do_ref[h, rows, :], prob, (((0,), (0,)), ((), ())), preferred_element_type=F32)
             dkv_acc[k_slot, 0, :, :n_key] += lax.dot_general(q_ref[h, rows, :], ds, (((0,), (0,)), ((), ())), preferred_element_type=F32)
-            base = dq_acc[h, :, rows] if has_in else jnp.where(fresh, 0.0, dq_acc[h, :, rows])
+            base = jnp.where(fresh, dqi_ref[h, :, rows] if has_in else 0.0, dq_acc[h, :, rows])
             dq_acc[h, :, rows] = base + lax.dot_general(kt_scr[:head_dim, :n_key], ds, (((1,), (1,)), ((), ())), preferred_element_type=F32)
 
         tiles = [(h, sub) for h in range(n_head) for sub in range(n_row // tile)]
@@ -111,10 +111,10 @@
         @pl.when(kind == 2)
         def _():
             run_task(True)
-    elif not has_in:
+    else:
         @pl.when(kind == 0)
         def _():
-            dq_acc[...] = jnp.zeros_like(dq_acc)
+            dq_acc[...] = dqi_ref[...] if has_in else jnp.zeros_like(dq_acc)
 
     if is_end:
         @pl.when(is_last == 1)
@@ -137,12 +137,12 @@
 
 def block_call(table, q, do, aug, kv, dq_in, is_end, has_diag):
     n_q, n_head, n_row, head_dim = q.shape
-    n_key = kv.shape[1]
-    n_peer = n_key // 4
+    n_peer = len(kv)
+    n_key = 4 * n_peer
     n_step = table.shape[0]
     has_in = dq_in is not None
     q_spec = pl.BlockSpec((None, n_head, n_row, head_dim), lambda t, tab: (tab[t, 0], 0, 0, 0))
-    kv_specs = [pl.BlockSpec((None, None, n_row, head_dim), lambda t, tab, i=i: (i, tab[t, 1], 0, 0)) for i in range(2)]
+    kv_specs = [pl.BlockSpec((None, None, n_row, head_dim), lambda t, tab, i=i, p=p: (i, jnp.clip(tab[t, 1] - 4 * p, 0, 3), 0, 0)) for p in range(n_peer) for i in range(2)]
     qt_spec = pl.BlockSpec((None, n_head, head_dim, n_row), lambda t, tab: (tab[t, 0], 0, 0, 0))
     n_task = 8 * n_peer
     return pl.pallas_call(
@@ -165,7 +165,7 @@
         out_shape=[jax.ShapeDtypeStruct(q.shape, BF16) if is_end else jax.ShapeDtypeStruct((n_q, n_head, head_dim, n_row), F32)] + [jax.ShapeDtypeStruct((2, 4, n_row, head_dim), F32)] * n_peer,
         compiler_params=pltpu.CompilerParams(dimension_semantics=('arbitrary',), vmem_limit_bytes=50 * 1024 * 1024),
         cost_estimate=pl.CostEstimate(flops=n_task * n_head * 10 * n_row * n_row * head_dim, bytes_accessed=32 * 1024 * 1024, transcendentals=n_task * n_head * n_row * n_row),
-    )(table, q, do, aug, kv, kv, *([dq_in] if has_in else []))
+    )(table, q, do, aug, *[x for x in kv for _ in range(2)], *([dq_in] if has_in else []))
 
 
 def lane_parts(lse, delta):
@@ -212,7 +212,7 @@
         kv_rows = jnp.stack([key_rows, value_rows]).reshape(2, 2, half_tok, kv_heads, head_dim).transpose(3, 0, 1, 2, 4)
         kv_chip = [chip_rows(kv_rows, g, axis=1) for g in range(n_grp)]
         kv_far = [swap(kv_chip[g], 6) for g in range(n_grp)]
-        kv_near = [jnp.concatenate([swap(kv_chip[g], 2), swap(kv_chip[g], 4)], axis=1) for g in range(n_grp)]
+        kv_near = [(swap(kv_chip[g], 2), swap(kv_chip[g], 4)) for g in range(n_grp)]
 
         q_pf, do_pf = pieces_first(query_rows), pieces_first(grad_out)
         q_pf, do_pf = lax.optimization_barrier((q_pf, do_pf))
@@ -237,11 +237,11 @@
             last = g == n_grp - 1
             dq = None
             if not last:
-                dq, dkv_own = run('own', kv_chip[g], None, False)
-            dq, dkv_far = run('far', kv_far[g], dq, False)
+                dq, dkv_own = run('own', (kv_chip[g],), None, False)
+            dq, dkv_far = run('far', (kv_far[g],), dq, False)
             dq, dkv_x, dkv_y = run('near', kv_near[g], dq, not last)
             if last:
-                dq, dkv_own = run('own', kv_chip[g], dq, True)
+                dq, dkv_own = run('own', (kv_chip[g],), dq, True)
             dkv = dkv_own + swap(dkv_far, 6) + swap(dkv_x, 2) + swap(dkv_y, 4)
             dkv = dkv.astype(BF16)
             dq_all = lax.dynamic_update_index_in_dim(dq_all, dq[:2], core * n_grp + g, 0)

time: 551 us -> 509 us (0.924)
  waiting for transfers between devices: 79.2 us -> 53.2 us
  Pallas kernels: 348 us -> 339 us
    ppermute x24, waiting for transfers between devices: 79.2 us -> 53.2 us  [swap(): return lax.ppermute(x, ctx_axes, [(dev, dev ^ bit) for dev in range(n_ctx)])]
    pallas_call x6, Pallas kernels: 348 us -> 339 us  [block_call(): pl.pallas_call(functools.partial(block_kernel, has_in, is_end, has_diag,...]
  transfers between devices with their start and end apart: 24 -> 24, of which waited for: 7 -> 3; matrix products, arithmetic and copies ran while one was open for 14% -> 15% of each run, Pallas kernels for 64% -> 68%
where the time goes in v5:
time: 509 us; the launch traced here: 502 us
  Pallas kernels  339 us (67%)
  waiting for transfers between devices  53.2 us (10%)
  local copies, waits for them, and re-layouts  51.2 us (10%)
  other arithmetic  42.5 us (8%)
  starting transfers between devices  14.5 us (3%)
    pallas_call x6, Pallas kernels, block_call(): pl.pallas_call(functools.partial(block_kernel, has_in, is_end, has_diag,...  339 us
    ppermute x24, waiting for transfers between devices, swap(): return lax.ppermute(x, ctx_axes, [(dev, dev ^ bit) for dev in range(n_ctx)])  53.2 us
    squeeze x5, local copies, waits for them, and re-layouts, pick(): return lax.dynamic_index_in_dim(x, sel * n_grp + g, axis=0, keepdims=False)  16 us
    ppermute x24, starting transfers between devices, swap(): return lax.ppermute(x, ctx_axes, [(dev, dev ^ bit) for dev in range(n_ctx)])  14.5 us
    concatenate x6, other arithmetic, chip_rows(): jnp.concatenate([pick(x, g, True), swap(pick(x, g, False), 1)], axis=axis)  13.6 us
    convert_element_type x1, other arithmetic, lane_parts(): return jnp.where(lane < 2 * N_PART, out, 0.0).astype(BF16)  10.9 us
    transpose x1, local copies, waits for them, and re-layouts, pieces_first(): rows.reshape(2, half_tok, kv_heads, group_size, head_dim)  10.7 us
  transfers between devices with their start and end apart: 24, of which 3 were waited for; matrix products, arithmetic and copies ran while one was open for 15% of the time, Pallas kernels for 68%

profile of v5, /device:TPU:0, one launch (start us, length us, event | category | flops | bytes accessed | tf_op | source)
XLA Modules:
  0.0 502.1 jit_solution(16054517294723363078)
XLA Ops:
  0.7 10.7 %copy_bitcast_fusion = (bf16[4,2,7,512,128]{4,3,2,1,0:T(8,128)(2,1)}, bf16[4,2,7,512,128]{4,3,2,1,0:T(8,128)(2,1)}) fusion(bf16[2,512,4,7,128]{4,1,0,3,2:T(8,128)(2,1)} %bitcast.92, bf16[2,512,4,7,128]{4,1,0,3,2:T(8,128)(2,1)} %bitcast.95), kind=kLoop, calls=%fused_computation.18 | loop fusion | bytes 29360128 | tf_op jit(solution)/shard_map/transpose | solution.py:207
  11.3 4.3 dynamic-slice_bitcast_fusion.7
  15.6 0.8 collective-permute-start
  16.5 5.8 %dynamic-slice_bitcast_fusion.1 = (bf16[2,7,512,128]{3,2,1,0:T(8,128)(2,1)S(1)}, bf16[2,7,512,128]{3,2,1,0:T(8,128)(2,1)}, bf16[2,7,512,128]{3,2,1,0:T(8,128)(2,1)}, bf16[2,7,512,128]{3,2,1,0:T(8,128)(2,1)}) fusion(bf16[4,2,7,512,128]{4,3,2,1,0:T(8,128)(2,1)} %get-tuple-element.20, s32[]{:T(128)S(6)} %select_n.103, s32[]{:T(128)S(6)} %select_n.104, ...), kind=kLoop, calls=%fused_computation.31 | loop fusion | bytes 14680080 | tf_op jit(solution)/shard_map/jit(dynamic_index_in_dim)/squeeze | solution.py:204
  22.3 0.1 reshape.45
  22.4 9.1 %fusion = f32[1024,28]{0,1:T(8,128)S(1)} fusion(bf16[1024,28,128]{2,0,1:T(8,128)(2,1)} %param.13, bf16[1024,28,128]{2,0,1:T(8,128)(2,1)} %param.12), kind=kLoop, calls=%fused_computation.1 | loop fusion | flops 14651392 | bytes 14794752 | tf_op jit(solution)/shard_map/thd,thd->th/dot_general | solution.py:219
  31.5 0.1 reshape.46
  31.6 0.1 fusion.20
  31.8 0.6 copy.42
  32.4 0.5 collective-permute-start.10
  32.9 0.6 copy.43
  33.6 0.1 copy_dynamic-update-slice_fusion.1
  33.7 0.3 copy_dynamic-update-slice_fusion
  34.0 1.3 dynamic-slice_bitcast_fusion.9
  35.3 0.4 copy-done
  35.7 0.5 collective-permute-start.3
  36.2 0.6 iota_remainder_fusion
  36.8 0.6 compare_and_fusion
  37.4 0.7 fusion.21
  38.1 0.1 copy.20.tab_ref
  38.2 0.7 fusion.22
  38.9 0.1 copy.19.tab_ref
  39.0 0.7 fusion.23
  39.6 0.1 copy.18.tab_ref
  39.8 0.8 fusion.12
  40.6 0.8 fusion.14
  41.4 10.9 %fusion.8 = (bf16[4,7,512,128]{3,2,1,0:T(8,128)(2,1)}, bf16[4,7,512,128]{3,2,1,0:T(8,128)(2,1)}) fusion(f32[4,7,512]{2,1,0:T(8,128)S(1)} %get-tuple-element.55, f32[4,7,512]{2,1,0:T(8,128)S(1)} %get-tuple-element.54, s32[128]{0:T(128)} %get-tuple-element.66, s32[128]{0:T(128)} %get-tuple-element.67, pred[128]{0:T(512)(128)(4,1)} %get-tuple-element.65, ...), kind=kLoop, calls=%fused_computation.17 | loop fusion | flops 42205184 | bytes 7570816 | tf_op jit(solution)/shard_map/convert_element_type | solution.py:180
  52.3 0.1 pad_maximum_fusion.4.refs_0_.refs_1_
  52.4 3.0 collective-permute-start.4
  55.4 1.5 collective-permute-start.5
  56.9 3.8 pad_maximum_fusion.q_ref
  60.7 3.7 pad_maximum_fusion.1.do_ref
  64.5 43.7 %shard_map.112 = (f32[4,7,128,512]{3,2,1,0:T(8,128)}, f32[2,4,512,128]{3,2,1,0:T(8,128)S(1)}) custom-call(s32[10,5]{1,0:T(8,128)S(1)} %copy.18.tab_ref, bf16[4,7,512,128]{3,2,1,0:T(8,128)(2,1)} %pad_maximum_fusion.q_ref, bf16[4,7,512,128]{3,2,1,0:T(8,128)(2,1)} %pad_maximum_fusion.1.do_ref, bf16[4,7,512,128]{3,2,1,0:T(8,128)(2,1)} %get-tuple-element.59.aug_ref, ...), custom_call_target="tpu_custom_call" | custom-call | flops 18790481920 | bytes 33554432 | tf_op jit(solution)/shard_map/pallas_call | solution.py:148
  108.2 44.4 %shard_map.113 = (f32[4,7,128,512]{3,2,1,0:T(8,128)}, f32[2,4,512,128]{3,2,1,0:T(8,128)S(1)}) custom-call(s32[10,5]{1,0:T(8,128)S(1)} %copy.19.tab_ref, bf16[4,7,512,128]{3,2,1,0:T(8,128)(2,1)} %pad_maximum_fusion.q_ref, bf16[4,7,512,128]{3,2,1,0:T(8,128)(2,1)} %pad_maximum_fusion.1.do_ref, bf16[4,7,512,128]{3,2,1,0:T(8,128)(2,1)} %get-tuple-element.59.aug_ref, ...), custom_call_target="tpu_custom_call" | custom-call | flops 18790481920 | bytes 33554432 | tf_op jit(solution)/shard_map/pallas_call | solution.py:148
  152.6 81.2 %shard_map.114 = (bf16[4,7,512,128]{3,2,1,0:T(8,128)(2,1)}, f32[2,4,512,128]{3,2,1,0:T(8,128)}, f32[2,4,512,128]{3,2,1,0:T(8,128)}) custom-call(s32[18,5]{1,0:T(8,128)S(1)} %copy.20.tab_ref, bf16[4,7,512,128]{3,2,1,0:T(8,128)(2,1)} %pad_maximum_fusion.q_ref, bf16[4,7,512,128]{3,2,1,0:T(8,128)(2,1)} %pad_maximum_fusion.1.do_ref, ...), custom_call_target="tpu_custom_call" | custom-call | flops 37580963840 | bytes 33554432 | tf_op jit(solution)/shard_map/pallas_call | solution.py:148
  233.8 4.6 dynamic-slice_bitcast_fusion.3
  238.5 0.5 collective-permute-start.11
  239.0 4.0 collective-permute-done.11
  243.0 0.1 pad_maximum_fusion.5.refs_0_.refs_1_
  243.2 3.4 collective-permute-start.13
  246.6 1.4 slice.47
  248.1 3.7 pad_maximum_fusion.3.do_ref
  251.7 2.2 pad_maximum_fusion.2.q_ref
  253.9 16.2 %collective-permute-done.14.refs_0_.refs_1_ = bf16[2,4,512,128]{3,2,1,0:T(8,128)(2,1)S(1)} collective-permute-done((bf16[2,4,512,128]{3,2,1,0:T(8,128)(2,1)S(1)}, bf16[2,4,512,128]{3,2,1,0:T(8,128)(2,1)S(1)}, u32[]{:S(2)}, u32[]{:S(2)}) %collective-permute-start.14) | collective-permute-done | bytes 1048608 | tf_op jit(solution)/shard_map/ppermute | solution.py:191
  270.1 42.4 %shard_map.115 = (f32[4,7,128,512]{3,2,1,0:T(8,128)}, f32[2,4,512,128]{3,2,1,0:T(8,128)S(1)}) custom-call(s32[10,5]{1,0:T(8,128)S(1)} %copy.19.tab_ref, bf16[4,7,512,128]{3,2,1,0:T(8,128)(2,1)} %pad_maximum_fusion.2.q_ref, bf16[4,7,512,128]{3,2,1,0:T(8,128)(2,1)} %pad_maximum_fusion.3.do_ref, bf16[4,7,512,128]{3,2,1,0:T(8,128)(2,1)} %get-tuple-element.58.aug_ref, ...), custom_call_target="tpu_custom_call" | custom-call | flops 18790481920 | bytes 33554432 | tf_op jit(solution)/shard_map/pallas_call | solution.py:148
  312.6 81.2 %shard_map.116 = (f32[4,7,128,512]{3,2,1,0:T(8,128)}, f32[2,4,512,128]{3,2,1,0:T(8,128)}, f32[2,4,512,128]{3,2,1,0:T(8,128)}) custom-call(s32[18,5]{1,0:T(8,128)S(1)} %copy.20.tab_ref, bf16[4,7,512,128]{3,2,1,0:T(8,128)(2,1)} %pad_maximum_fusion.2.q_ref, bf16[4,7,512,128]{3,2,1,0:T(8,128)(2,1)} %pad_maximum_fusion.3.do_ref, ...), custom_call_target="tpu_custom_call" | custom-call | flops 37580963840 | bytes 33554432 | tf_op jit(solution)/shard_map/pallas_call | solution.py:148
  393.9 3.4 collective-permute-start.20
  397.3 46.4 %shard_map.117 = (bf16[4,7,512,128]{3,2,1,0:T(8,128)(2,1)}, f32[2,4,512,128]{3,2,1,0:T(8,128)S(1)}) custom-call(s32[10,5]{1,0:T(8,128)S(1)} %copy.18.tab_ref, bf16[4,7,512,128]{3,2,1,0:T(8,128)(2,1)} %pad_maximum_fusion.2.q_ref, bf16[4,7,512,128]{3,2,1,0:T(8,128)(2,1)} %pad_maximum_fusion.3.do_ref, bf16[4,7,512,128]{3,2,1,0:T(8,128)(2,1)} %get-tuple-element.58.aug_ref, ...), custom_call_target="tpu_custom_call" | custom-call | flops 18790481920 | bytes 33554432 | tf_op jit(solution)/shard_map/pallas_call | solution.py:148
  443.7 1.6 slice.51
  445.4 2.9 bitcast_dynamic-update-slice_fusion.2
  448.3 2.8 add_convert_fusion.1
  451.2 0.5 collective-permute-start.19
  451.7 1.4 bitcast_dynamic-update-slice_fusion.1
  453.1 0.1 fusion.10
  453.3 0.1 bitcast_dynamic-update-slice_fusion.5
  453.4 32.9 %collective-permute-done.20 = f32[2,4,512,128]{3,2,1,0:T(8,128)} collective-permute-done((f32[2,4,512,128]{3,2,1,0:T(8,128)S(1)}, f32[2,4,512,128]{3,2,1,0:T(8,128)}, u32[]{:S(2)}, u32[]{:S(2)}) %collective-permute-start.20) | collective-permute-done | bytes 2097184 | tf_op jit(solution)/shard_map/ppermute | solution.py:191
  486.2 3.3 add_convert_fusion
  489.6 1.4 bitcast_dynamic-update-slice_fusion
  491.0 7.0 %copy.26 = bf16[2,512,4,7,128]{4,1,0,3,2:T(8,128)(2,1)} copy(bf16[2,512,4,7,128]{4,1,3,0,2:T(8,128)(2,1)} %bitcast.37) | data formatting | bytes 14680064 | tf_op jit(solution)/shard_map/transpose | solution.py:252
  498.0 0.1 fusion.9
  498.1 0.1 bitcast_dynamic-update-slice_fusion.4
  498.2 0.1 fusion.24
  498.3 1.8 copy.27
  500.1 1.8 copy.28
  (60 shorter events, 0.5 us)
Async XLA Ops:
  15.6 41.3 %collective-permute-start = (bf16[2,7,512,128]{3,2,1,0:T(8,128)(2,1)}, bf16[2,7,512,128]{3,2,1,0:T(8,128)(2,1)}, u32[]{:S(2)}, u32[]{:S(2)}) collective-permute-start(bf16[2,7,512,128]{3,2,1,0:T(8,128)(2,1)} %get-tuple-element.43), channel_id=1, source_target_pairs={{0,1},{1,0},{2,3},{3,2},{4,5},{5,4},{6,7},{7,6}} | collective-permute-start | bytes 5505032 | tf_op jit(solution)/shard_map/ppermute | solution.py:191
  16.5 5.8 %copy-start.9 = (f32[1024,28]{0,1:T(8,128)S(1)}, f32[1024,28]{0,1:T(8,128)}, u32[]{:S(2)}) copy-start(f32[1024,28]{0,1:T(8,128)} %param.14) | copy-start | bytes 344068
  22.3 38.5 %collective-permute-start.1 = (bf16[2,7,512,128]{3,2,1,0:T(8,128)(2,1)}, bf16[2,7,512,128]{3,2,1,0:T(8,128)(2,1)}, u32[]{:S(2)}, u32[]{:S(2)}) collective-permute-start(bf16[2,7,512,128]{3,2,1,0:T(8,128)(2,1)} %get-tuple-element.37), channel_id=1, source_target_pairs={{0,1},{1,0},{2,3},{3,2},{4,5},{5,4},{6,7},{7,6}} | collective-permute-start | bytes 5505032 | tf_op jit(solution)/shard_map/ppermute | solution.py:191
  22.4 11.2 %copy-start.6 = (bf16[1024,4,128]{2,1,0:T(4,128)(2,1)S(1)}, bf16[1024,4,128]{2,1,0:T(4,128)(2,1)}, u32[]{:S(2)}) copy-start(bf16[1024,4,128]{2,1,0:T(4,128)(2,1)} %param.10) | copy-start | bytes 3145732
  31.6 2.1 copy-start.7
  32.4 7.4 %collective-permute-start.10 = (f32[2,2,7,512]{3,2,1,0:T(8,128)}, f32[2,2,7,512]{3,2,1,0:T(8,128)}, u32[]{:S(2)}, u32[]{:S(2)}) collective-permute-start(f32[2,2,7,512]{3,2,1,0:T(8,128)} %bitcast.90), channel_id=1, source_target_pairs={{0,1},{1,0},{2,3},{3,2},{4,5},{5,4},{6,7},{7,6}} | collective-permute-start | bytes 172040 | tf_op jit(solution)/shard_map/ppermute | solution.py:191
  33.6 7.1 %collective-permute-start.2 = (f32[2,2,7,512]{3,2,1,0:T(8,128)}, f32[2,2,7,512]{3,2,1,0:T(8,128)}, u32[]{:S(2)}, u32[]{:S(2)}) collective-permute-start(f32[2,2,7,512]{3,2,1,0:T(8,128)} %bitcast.91), channel_id=1, source_target_pairs={{0,1},{1,0},{2,3},{3,2},{4,5},{5,4},{6,7},{7,6}} | collective-permute-start | bytes 172040 | tf_op jit(solution)/shard_map/ppermute | solution.py:191
  34.0 1.7 copy-start
  35.7 16.6 %collective-permute-start.3 = (bf16[2,2,512,128]{3,2,1,0:T(8,128)(2,1)}, bf16[2,2,512,128]{3,2,1,0:T(8,128)(2,1)S(1)}, u32[]{:S(2)}, u32[]{:S(2)}) collective-permute-start(bf16[2,2,512,128]{3,2,1,0:T(8,128)(2,1)} %get-tuple-element.48), channel_id=1, source_target_pairs={{0,1},{1,0},{2,3},{3,2},{4,5},{5,4},{6,7},{7,6}} | collective-permute-start | bytes 1572872 | tf_op jit(solution)/shard_map/ppermute | solution.py:191
  39.8 208.3 %collective-permute-start.9 = (bf16[2,7,512,128]{3,2,1,0:T(8,128)(2,1)}, bf16[2,7,512,128]{3,2,1,0:T(8,128)(2,1)}, u32[]{:S(2)}, u32[]{:S(2)}) collective-permute-start(bf16[2,7,512,128]{3,2,1,0:T(8,128)(2,1)} %get-tuple-element.36), channel_id=1, source_target_pairs={{0,1},{1,0},{2,3},{3,2},{4,5},{5,4},{6,7},{7,6}} | collective-permute-start | bytes 5505032 | tf_op jit(solution)/shard_map/ppermute | solution.py:191
  52.3 4.6 copy-start.2
  52.4 100.2 %collective-permute-start.4 = (bf16[2,4,512,128]{3,2,1,0:T(8,128)(2,1)S(1)}, bf16[2,4,512,128]{3,2,1,0:T(8,128)(2,1)S(1)}, u32[]{:S(2)}, u32[]{:S(2)}) collective-permute-start(bf16[2,4,512,128]{3,2,1,0:T(8,128)(2,1)S(1)} %pad_maximum_fusion.4.refs_0_.refs_1_), channel_id=1, source_target_pairs={{0,2},{1,3},{2,0},{3,1},{4,6},{5,7},{6,4},{7,5}} | collective-permute-start | bytes 3145736 | tf_op jit(solution)/shard_map/ppermute | solution.py:191
  55.4 97.2 %collective-permute-start.5 = (bf16[2,4,512,128]{3,2,1,0:T(8,128)(2,1)S(1)}, bf16[2,4,512,128]{3,2,1,0:T(8,128)(2,1)S(1)}, u32[]{:S(2)}, u32[]{:S(2)}) collective-permute-start(bf16[2,4,512,128]{3,2,1,0:T(8,128)(2,1)S(1)} %pad_maximum_fusion.4.refs_0_.refs_1_), channel_id=1, source_target_pairs={{0,4},{1,5},{2,6},{3,7},{4,0},{5,1},{6,2},{7,3}} | collective-permute-start | bytes 3145736 | tf_op jit(solution)/shard_map/ppermute | solution.py:191
  56.9 51.3 %collective-permute-start.6 = (bf16[2,4,512,128]{3,2,1,0:T(8,128)(2,1)S(1)}, bf16[2,4,512,128]{3,2,1,0:T(8,128)(2,1)S(1)}, u32[]{:S(2)}, u32[]{:S(2)}) collective-permute-start(bf16[2,4,512,128]{3,2,1,0:T(8,128)(2,1)S(1)} %pad_maximum_fusion.4.refs_0_.refs_1_), channel_id=1, source_target_pairs={{0,6},{1,7},{2,4},{3,5},{4,2},{5,3},{6,0},{7,1}} | collective-permute-start | bytes 3145736 | tf_op jit(solution)/shard_map/ppermute | solution.py:191
  56.9 3.8 copy-start.3
  233.8 4.7 copy-start.8
  233.8 12.8 %copy-start.5 = (bf16[4,7,512,128]{3,2,1,0:T(8,128)(2,1)S(1)}, bf16[4,7,512,128]{3,2,1,0:T(8,128)(2,1)}, u32[]{:S(2)}) copy-start(bf16[4,7,512,128]{3,2,1,0:T(8,128)(2,1)} %get-tuple-element.23) | copy-start | bytes 11010052
  238.5 13.3 %collective-permute-start.8 = (bf16[2,7,512,128]{3,2,1,0:T(8,128)(2,1)S(1)}, bf16[2,7,512,128]{3,2,1,0:T(8,128)(2,1)S(1)}, u32[]{:S(2)}, u32[]{:S(2)}) collective-permute-start(bf16[2,7,512,128]{3,2,1,0:T(8,128)(2,1)S(1)} %get-tuple-element.40), channel_id=1, source_target_pairs={{0,1},{1,0},{2,3},{3,2},{4,5},{5,4},{6,7},{7,6}} | collective-permute-start | bytes 5505032 | tf_op jit(solution)/shard_map/ppermute | solution.py:191
  238.5 4.5 collective-permute-start.11
  243.1 27.0 %collective-permute-start.14 = (bf16[2,4,512,128]{3,2,1,0:T(8,128)(2,1)S(1)}, bf16[2,4,512,128]{3,2,1,0:T(8,128)(2,1)S(1)}, u32[]{:S(2)}, u32[]{:S(2)}) collective-permute-start(bf16[2,4,512,128]{3,2,1,0:T(8,128)(2,1)S(1)} %pad_maximum_fusion.5.refs_0_.refs_1_), channel_id=1, source_target_pairs={{0,6},{1,7},{2,4},{3,5},{4,2},{5,3},{6,0},{7,1}} | collective-permute-start | bytes 3145736 | tf_op jit(solution)/shard_map/ppermute | solution.py:191
  243.1 69.4 %collective-permute-start.12 = (bf16[2,4,512,128]{3,2,1,0:T(8,128)(2,1)S(1)}, bf16[2,4,512,128]{3,2,1,0:T(8,128)(2,1)S(1)}, u32[]{:S(2)}, u32[]{:S(2)}) collective-permute-start(bf16[2,4,512,128]{3,2,1,0:T(8,128)(2,1)S(1)} %pad_maximum_fusion.5.refs_0_.refs_1_), channel_id=1, source_target_pairs={{0,2},{1,3},{2,0},{3,1},{4,6},{5,7},{6,4},{7,5}} | collective-permute-start | bytes 3145736 | tf_op jit(solution)/shard_map/ppermute | solution.py:191
  243.2 69.4 %collective-permute-start.13 = (bf16[2,4,512,128]{3,2,1,0:T(8,128)(2,1)S(1)}, bf16[2,4,512,128]{3,2,1,0:T(8,128)(2,1)S(1)}, u32[]{:S(2)}, u32[]{:S(2)}) collective-permute-start(bf16[2,4,512,128]{3,2,1,0:T(8,128)(2,1)S(1)} %pad_maximum_fusion.5.refs_0_.refs_1_), channel_id=1, source_target_pairs={{0,4},{1,5},{2,6},{3,7},{4,0},{5,1},{6,2},{7,3}} | collective-permute-start | bytes 3145736 | tf_op jit(solution)/shard_map/ppermute | solution.py:191
  248.0 145.8 %collective-permute-start.7 = (bf16[2,7,512,128]{3,2,1,0:T(8,128)(2,1)}, bf16[2,7,512,128]{3,2,1,0:T(8,128)(2,1)}, u32[]{:S(2)}, u32[]{:S(2)}) collective-permute-start(bf16[2,7,512,128]{3,2,1,0:T(8,128)(2,1)} %slice.47), channel_id=1, source_target_pairs={{0,1},{1,0},{2,3},{3,2},{4,5},{5,4},{6,7},{7,6}} | collective-permute-start | bytes 5505032 | tf_op jit(solution)/shard_map/ppermute | solution.py:191
  251.7 142.1 %collective-permute-start.18 = (f32[2,4,512,128]{3,2,1,0:T(8,128)}, f32[2,4,512,128]{3,2,1,0:T(8,128)S(1)}, u32[]{:S(2)}, u32[]{:S(2)}) collective-permute-start(f32[2,4,512,128]{3,2,1,0:T(8,128)} %get-tuple-element.30), channel_id=1, source_target_pairs={{0,4},{1,5},{2,6},{3,7},{4,0},{5,1},{6,2},{7,3}} | collective-permute-start | bytes 6291464 | tf_op jit(solution)/shard_map/ppermute | solution.py:191
  270.1 175.3 %collective-permute-start.17 = (f32[2,4,512,128]{3,2,1,0:T(8,128)}, f32[2,4,512,128]{3,2,1,0:T(8,128)}, u32[]{:S(2)}, u32[]{:S(2)}) collective-permute-start(f32[2,4,512,128]{3,2,1,0:T(8,128)} %get-tuple-element.29), channel_id=1, source_target_pairs={{0,2},{1,3},{2,0},{3,1},{4,6},{5,7},{6,4},{7,5}} | collective-permute-start | bytes 6291464 | tf_op jit(solution)/shard_map/ppermute | solution.py:191
  312.6 135.8 %collective-permute-start.16 = (f32[2,4,512,128]{3,2,1,0:T(8,128)S(1)}, f32[2,4,512,128]{3,2,1,0:T(8,128)}, u32[]{:S(2)}, u32[]{:S(2)}) collective-permute-start(f32[2,4,512,128]{3,2,1,0:T(8,128)S(1)} %get-tuple-element.28), channel_id=1, source_target_pairs={{0,6},{1,7},{2,4},{3,5},{4,2},{5,3},{6,0},{7,1}} | collective-permute-start | bytes 6291464 | tf_op jit(solution)/shard_map/ppermute | solution.py:191
  393.8 59.6 %collective-permute-start.22 = (f32[2,4,512,128]{3,2,1,0:T(8,128)}, f32[2,4,512,128]{3,2,1,0:T(8,128)}, u32[]{:S(2)}, u32[]{:S(2)}) collective-permute-start(f32[2,4,512,128]{3,2,1,0:T(8,128)} %get-tuple-element.34), channel_id=1, source_target_pairs={{0,4},{1,5},{2,6},{3,7},{4,0},{5,1},{6,2},{7,3}} | collective-permute-start | bytes 6291464 | tf_op jit(solution)/shard_map/ppermute | solution.py:191
  393.8 59.5 %collective-permute-start.21 = (f32[2,4,512,128]{3,2,1,0:T(8,128)}, f32[2,4,512,128]{3,2,1,0:T(8,128)}, u32[]{:S(2)}, u32[]{:S(2)}) collective-permute-start(f32[2,4,512,128]{3,2,1,0:T(8,128)} %get-tuple-element.33), channel_id=1, source_target_pairs={{0,2},{1,3},{2,0},{3,1},{4,6},{5,7},{6,4},{7,5}} | collective-permute-start | bytes 6291464 | tf_op jit(solution)/shard_map/ppermute | solution.py:191
  393.9 92.4 %collective-permute-start.20 = (f32[2,4,512,128]{3,2,1,0:T(8,128)S(1)}, f32[2,4,512,128]{3,2,1,0:T(8,128)}, u32[]{:S(2)}, u32[]{:S(2)}) collective-permute-start(f32[2,4,512,128]{3,2,1,0:T(8,128)S(1)} %get-tuple-element.32), channel_id=1, source_target_pairs={{0,6},{1,7},{2,4},{3,5},{4,2},{5,3},{6,0},{7,1}} | collective-permute-start | bytes 6291464 | tf_op jit(solution)/shard_map/ppermute | solution.py:191
  445.4 44.2 %collective-permute-start.15 = (bf16[2,7,512,128]{3,2,1,0:T(8,128)(2,1)S(1)}, bf16[2,7,512,128]{3,2,1,0:T(8,128)(2,1)S(1)}, u32[]{:S(2)}, u32[]{:S(2)}) collective-permute-start(bf16[2,7,512,128]{3,2,1,0:T(8,128)(2,1)S(1)} %slice.51), channel_id=1, source_target_pairs={{0,1},{1,0},{2,3},{3,2},{4,5},{5,4},{6,7},{7,6}} | collective-permute-start | bytes 5505032 | tf_op jit(solution)/shard_map/ppermute | solution.py:191
  448.3 3.4 copy-start.4
  451.2 2.0 copy-start.1
  451.2 2.1 collective-permute-start.19
  489.6 8.5 %collective-permute-start.23 = (bf16[2,2,512,128]{3,2,1,0:T(8,128)(2,1)S(1)}, bf16[2,2,512,128]{3,2,1,0:T(8,128)(2,1)S(1)}, u32[]{:S(2)}, u32[]{:S(2)}) collective-permute-start(bf16[2,2,512,128]{3,2,1,0:T(8,128)(2,1)S(1)} %slice.65), channel_id=1, source_target_pairs={{0,1},{1,0},{2,3},{3,2},{4,5},{5,4},{6,7},{7,6}} | collective-permute-start | bytes 1572872 | tf_op jit(solution)/shard_map/ppermute | solution.py:191
